TPU v7x, 64 devices: a 2x2x8 block of a 4x4x8 slice. The times are simulated.
64 devices in a mesh: rep: 8 (over x, y, core), dp: 8 (over z).
Axes of the slice: x: 2, y: 2, z: 8, core: 2. Of those that a mesh axis runs over, the one named last changes fastest.
The devices are a block of a 4x4x8 slice.
Arguments:
- x: bfloat16 [64, 2048, 768], P(('rep', 'dp')), parts along dimension 0
- dy: bfloat16 [64, 2048, 768], P(('rep', 'dp')), parts along dimension 0
- w_gate: bfloat16 [2, 768, 1792], replicated
- w_up: bfloat16 [2, 768, 1792], replicated
- w_down: bfloat16 [2, 1792, 768], replicated
- m_w_gate: float32 [2, 768, 1792], replicated
- m_w_up: float32 [2, 768, 1792], replicated
- m_w_down: float32 [2, 1792, 768], replicated
- v_w_gate: float32 [2, 768, 1792], replicated
- v_w_up: float32 [2, 768, 1792], replicated
- v_w_down: float32 [2, 1792, 768], replicated
Outputs:
- output 1: bfloat16 [16, 768, 1792], P('rep'), parts along dimension 0
- output 2: bfloat16 [16, 768, 1792], P('rep'), parts along dimension 0
- output 3: bfloat16 [16, 1792, 768], P('rep'), parts along dimension 0
- output 4: float32 [16, 768, 1792], P('rep'), parts along dimension 0
- output 5: float32 [16, 768, 1792], P('rep'), parts along dimension 0
- output 6: float32 [16, 1792, 768], P('rep'), parts along dimension 0
- output 7: float32 [16, 768, 1792], P('rep'), parts along dimension 0
- output 8: float32 [16, 768, 1792], P('rep'), parts along dimension 0
- output 9: float32 [16, 1792, 768], P('rep'), parts along dimension 0
There are 8 independent parts. A program takes and returns all parts, laid end to end along the dimension named above; an argument that names none is the same for every part.
All inputs are finite; a program needn't handle non-finite values.
Results may differ from a plain program's by a relative error of at most 0.022.
Values are sent between devices in bfloat16 or wider.
A program may use at most 768 MiB of HBM per device.

v0:
```python
import jax
import jax.numpy as jnp
from jax import lax
from jax.sharding import PartitionSpec as P

NAMES = ("w_gate", "w_up", "w_down")


def matmul(a, w):
    return jnp.dot(a, w, preferred_element_type=jnp.float32).astype(jnp.bfloat16)


def normed(h):
    wide = h.astype(jnp.float32)
    scale = lax.rsqrt(jnp.mean(wide**2, -1, keepdims=True) + 1e-6)
    return (wide * scale).astype(jnp.bfloat16)


def layer(h, w):
    a = normed(h)
    gate = jnp.dot(a, w["w_gate"], preferred_element_type=jnp.float32)
    up = jnp.dot(a, w["w_up"], preferred_element_type=jnp.float32)
    return h + matmul((jax.nn.silu(gate) * up).astype(jnp.bfloat16), w["w_down"])


def adamw(w, m, v, g):
    m = 0.9 * m + 0.1 * g
    v = 0.95 * v + 0.05 * g * g
    step = m * lax.rsqrt(v + 1e-8) + 0.1 * w
    return (w - 0.02 * step).astype(jnp.bfloat16), m, v


def clipped(gradients, sum_of_squares, count):
    factor = jnp.minimum(1.0, 0.5 * lax.rsqrt(sum_of_squares / count + 1e-30))
    return [g * factor for g in gradients]


def solution(mesh):
    def step(x, dy, *arrays):
        weights, m, v = (arrays[i : i + 3] for i in (0, 3, 6))
        layers = weights[0].shape[0]
        h, kept = x[0], []
        for number in range(layers):
            kept.append(h)
            h = layer(h, {name: w[number] for name, w in zip(NAMES, weights, strict=True)})
        by_h, summed = dy[0], [None] * layers
        for number in reversed(range(layers)):
            _, back = jax.vjp(lambda w, h: layer(h, w), {name: w[number] for name, w in zip(NAMES, weights, strict=True)}, kept[number])
            by_w, by_h = back(by_h)
            summed[number] = [lax.psum(by_w[name], "dp") for name in NAMES]
        gradients = [jnp.stack([summed[number][i] for number in range(layers)]).astype(jnp.float32) for i in range(3)]
        gradients = clipped(gradients, sum(jnp.sum(g * g) for g in gradients), sum(g.size for g in gradients))
        new = [adamw(w.astype(jnp.float32), m, v, g) for w, m, v, g in zip(weights, m, v, gradients, strict=True)]
        return tuple(one[which] for which in range(3) for one in new)

    return jax.shard_map(
        step,
        mesh=mesh,
        in_specs=(P(("rep", "dp"), None, None),) * 2 + (P(None, None, None),) * 9,
        out_specs=(P("rep", None, None),) * 9,
        check_vma=False,
    )
```

profile of v0, /device:TPU:21, one launch (start us, length us, event | category | flops | bytes accessed | tf_op | source)
XLA Modules:
  0.0 633.3 jit_solution(17029320176697973697)
XLA Ops:
  7.3 3.2 copy.20
  11.2 5.0 copy.21
  16.2 10.3 %convolution_convert_fusion.1 = bf16[2048,1792]{1,0:T(8,128)(2,1)} fusion(bf16[1,2048,768]{2,1,0:T(8,128)(2,1)} %param.12, bf16[2,1792,768]{2,1,0:T(8,128)(2,1)} %param.15), kind=kOutput, calls=%fused_computation.66 | convolution fusion | flops 5640814592 | bytes 13238272 | tf_op jit(solution)/shard_map/transpose(jvp())/dot_general | solution.py:10
  26.5 11.1 %fusion.77 = f32[2048,1792]{1,0:T(8,128)} fusion(bf16[2,768,1792]{2,1,0:T(8,128)(2,1)} %param.13, bf16[1,2048,768]{2,1,0:T(8,128)(2,1)S(1)} %copy-done.5, f32[2048]{0:T(1024)S(1)} %add_rsqrt_fusion), kind=kOutput, calls=%fused_computation.111 | convolution fusion | flops 5641863168 | bytes 20586496 | tf_op jit(solution)/shard_map/dot_general | solution.py:21
  37.6 16.2 %multiply_convert_fusion.1 = (bf16[2048,1792]{1,0:T(8,128)(2,1)}, f32[2048,1792]{1,0:T(8,128)}) fusion(f32[2048,1792]{1,0:T(8,128)} %fusion.77, bf16[2,768,1792]{2,1,0:T(8,128)(2,1)S(1)} %bitcast.77, bf16[1,2048,768]{2,1,0:T(8,128)(2,1)} %param.11, f32[2048]{0:T(1024)S(1)} %add_rsqrt_fusion), kind=kOutput, calls=%fused_computation.20 | convolution fusion | flops 5663883264 | bytes 42606592 | tf_op jit(solution)/shard_map/dot_general | solution.py:22
  53.9 9.7 %fusion.40 = (f32[2048]{0:T(1024)S(1)}, bf16[2048,768]{0,1:T(8,128)(2,1)S(1)}) fusion(bf16[2048,1792]{1,0:T(8,128)(2,1)} %get-tuple-element.24, bf16[2,1792,768]{2,1,0:T(8,128)(2,1)} %param.15, bf16[1,2048,768]{1,2,0:T(8,128)(2,1)S(1)} %copy.20), kind=kOutput, calls=%fused_computation.73 | convolution fusion | flops 5645006848 | bytes 16392192 | tf_op jit(solution)/shard_map/dot_general | solution.py:10
  65.2 9.3 %fusion.66 = f32[2048,1792]{1,0:T(8,128)} fusion(bf16[2,768,1792]{2,1,0:T(8,128)(2,1)S(1)} %bitcast.77, bf16[2048,768]{0,1:T(8,128)(2,1)S(1)} %get-tuple-element.27, f32[2048]{0:T(1024)S(1)} %fusion.100), kind=kOutput, calls=%fused_computation.100 | convolution fusion | flops 5641863168 | bytes 20586496 | tf_op jit(solution)/shard_map/jvp()/dot_general | solution.py:22
  74.5 23.3 %fusion.2 = (bf16[2048,1792]{1,0:T(8,128)(2,1)}, f32[2048,1792]{1,0:T(8,128)}) fusion(f32[2048,1792]{1,0:T(8,128)} %fusion.66, bf16[2048,1792]{1,0:T(8,128)(2,1)} %convolution_convert_fusion.1, bf16[2,768,1792]{2,1,0:T(8,128)(2,1)} %param.13, bf16[2048,768]{0,1:T(8,128)(2,1)} %copy-done.7, f32[2048]{0:T(1024)S(1)} %fusion.100), kind=kOutput, calls=%fused_computation.11 | convolution fusion | flops 5685903360 | bytes 49946624 | tf_op jit(solution)/shard_map/jvp()/dot_general | solution.py:21
  97.8 10.8 %fusion.57 = bf16[1,768,1792]{2,1,0:T(8,128)(2,1)} fusion(bf16[2048,1792]{1,0:T(8,128)(2,1)} %get-tuple-element.28, bf16[2048,768]{0,1:T(8,128)(2,1)S(1)} %copy-done.8, f32[2048]{0:T(1024)S(1)} %fusion.100), kind=kOutput, calls=%fused_computation.95 | convolution fusion | flops 5641863168 | bytes 13246464 | tf_op jit(solution)/shard_map/transpose(jvp())/dot_general | solution.py:21
  108.6 9.2 %convolution_convert_fusion.4 = bf16[2048,768]{0,1:T(8,128)(2,1)} fusion(bf16[2048,1792]{1,0:T(8,128)(2,1)S(1)} %copy-done.14, bf16[2,768,1792]{2,1,0:T(8,128)(2,1)} %param.13), kind=kOutput, calls=%fused_computation.82 | convolution fusion | flops 5637144576 | bytes 13238272 | tf_op jit(solution)/shard_map/transpose(jvp())/dot_general | solution.py:21
  117.8 14.1 %fusion.61 = bf16[1,1792,768]{2,1,0:T(8,128)(2,1)} fusion(bf16[1,2048,768]{2,1,0:T(8,128)(2,1)S(1)} %copy-done.6, f32[2048,1792]{1,0:T(8,128)} %fusion.66, f32[2048,1792]{1,0:T(8,128)} %get-tuple-element.29), kind=kOutput, calls=%fused_computation.99 | convolution fusion | flops 5660540928 | bytes 35258368 | tf_op jit(solution)/shard_map/transpose(jvp())/dot_general | solution.py:10
  131.9 12.5 %fusion.60 = bf16[1,768,1792]{2,1,0:T(8,128)(2,1)} fusion(bf16[2048,1792]{1,0:T(8,128)(2,1)} %convolution_convert_fusion.1, bf16[2048,768]{0,1:T(8,128)(2,1)S(1)} %copy-done.9, f32[2048]{0:T(1024)S(1)} %fusion.100, f32[2048,1792]{1,0:T(8,128)} %get-tuple-element.29), kind=kOutput, calls=%fused_computation.98 | convolution fusion | flops 5665259520 | bytes 27926528 | tf_op jit(solution)/shard_map/transpose(jvp())/dot_general | solution.py:22
  144.4 14.0 %fusion.42 = (f32[2048]{0:T(1024)S(1)}, bf16[2048,768]{0,1:T(8,128)(2,1)}) fusion(bf16[2048,768]{0,1:T(8,128)(2,1)} %copy-done.7, bf16[2048,768]{0,1:T(8,128)(2,1)} %convolution_convert_fusion.4, bf16[2,768,1792]{2,1,0:T(8,128)(2,1)S(1)} %bitcast.79, bf16[2048,1792]{1,0:T(8,128)(2,1)} %convolution_convert_fusion.1, f32[2048,1792]{1,0:T(8,128)} %get-tuple-element.29), kind=kOutput, calls=%fused_computation.75 | convolution fusion | flops 5668599808 | bytes 34217984 | tf_op jit(solution)/shard_map/transpose(jvp())/dot_general | solution.py:22
  158.5 5.2 fusion.51
  163.6 9.4 %fusion.58 = bf16[1,1792,768]{2,1,0:T(8,128)(2,1)} fusion(bf16[2048,1792]{1,0:T(8,128)(2,1)} %get-tuple-element.24, bf16[2048,768]{0,1:T(8,128)(2,1)S(1)} %fusion.51), kind=kOutput, calls=%fused_computation.96 | convolution fusion | flops 5638520832 | bytes 13238272 | tf_op jit(solution)/shard_map/transpose(jvp())/dot_general | solution.py:10
  173.1 6.4 %convolution_convert_fusion = bf16[2048,1792]{1,0:T(8,128)(2,1)S(1)} fusion(bf16[2048,768]{0,1:T(8,128)(2,1)S(1)} %fusion.51, bf16[2,1792,768]{2,1,0:T(8,128)(2,1)S(1)} %bitcast.81), kind=kOutput, calls=%fused_computation.65 | convolution fusion | flops 5640814592 | bytes 13238272 | tf_op jit(solution)/shard_map/transpose(jvp())/dot_general | solution.py:10
  179.5 14.2 %fusion.59 = bf16[1,768,1792]{2,1,0:T(8,128)(2,1)} fusion(bf16[2048,1792]{1,0:T(8,128)(2,1)S(1)} %convolution_convert_fusion, bf16[1,2048,768]{1,2,0:T(8,128)(2,1)S(1)} %copy-done.1, f32[2048]{0:T(1024)S(1)} %copy-done.13, f32[2048,1792]{1,0:T(8,128)} %fusion.77), kind=kOutput, calls=%fused_computation.97 | convolution fusion | flops 5665259520 | bytes 27926528 | tf_op jit(solution)/shard_map/transpose(jvp())/dot_general | solution.py:22
  193.7 17.0 %fusion.54 = bf16[1,768,1792]{2,1,0:T(8,128)(2,1)} fusion(f32[2048,1792]{1,0:T(8,128)} %fusion.77, f32[2048,1792]{1,0:T(8,128)} %get-tuple-element.25, bf16[2048,1792]{1,0:T(8,128)(2,1)} %copy-done.15, bf16[1,2048,768]{1,2,0:T(8,128)(2,1)S(1)} %copy-done.1, f32[2048]{0:T(1024)S(1)} %copy-done.13), kind=kOutput, calls=%fused_computation.94 | convolution fusion | flops 5683609600 | bytes 42606592 | tf_op jit(solution)/shard_map/transpose(jvp())/dot_general | solution.py:21
  210.8 338.2 %all-reduce.3.cloned.1.call-done = (bf16[1,768,1792]{2,1,0:T(8,128)(2,1)}, bf16[1,768,1792]{2,1,0:T(8,128)(2,1)}, bf16[1,768,1792]{2,1,0:T(8,128)(2,1)}, bf16[1,...) async-done(((bf16[1,768,1792]{2,1,0:T(8,128)(2,1)}, bf16[1,768,1792]{2,1,0:T(8,128)(2,1)}, bf16[1,768,1792]{2,1,0:T(8,128)(2,1)}, ...) | async-done | bytes 16515088 | tf_op jit(solution)/shard_map/psum | solution.py:50
  549.0 6.2 fusion.22
  555.2 6.0 fusion.21
  561.3 3.4 fusion.20
  566.7 21.9 %fusion.28 = (bf16[2,1792,768]{2,1,0:T(8,128)(2,1)}, f32[2,1792,768]{2,1,0:T(8,128)}, f32[2,1792,768]{2,1,0:T(8,128)}) fusion(bf16[2,1792,768]{2,1,0:T(8,128)(2,1)} %param.15, f32[]{:T(128)S(6)} %min_shard_map.3, bf16[1,1792,768]{2,1,0:T(8,128)(2,1)} %get-tuple-element.13, bf16[1,1792,768]{2,1,0:T(8,128)(2,1)} %get-tuple-element.14, ...), kind=kLoop, calls=%fused_computation.52 | loop fusion | flops 55050240 | bytes 60555268 | tf_op jit(solution)/shard_map/convert_element_type | solution.py:30
  588.6 37.3 %fusion.19 = (bf16[2,768,1792]{2,1,0:T(8,128)(2,1)}, f32[2,768,1792]{2,1,0:T(8,128)}, f32[2,768,1792]{2,1,0:T(8,128)}, bf16[2,768,1792]{2,1,0:T(8,128)(2,1)}, f3...) fusion(bf16[2,768,1792]{2,1,0:T(8,128)(2,1)} %param.13, f32[]{:T(128)S(6)} %min_shard_map.3, ...), kind=kLoop, calls=%fused_computation.43 | loop fusion | flops 110100480 | bytes 121110528 | tf_op jit(solution)/shard_map/convert_element_type | solution.py:30
  (53 shorter events, 2.5 us)
Async XLA Ops:
  7.2 541.8 %all-reduce.3.cloned.1.call-start = ((), (), s32[]{:S(2)}) async-start(), calls=%async_computation | async-start | bytes 33030144 | tf_op jit(solution)/shard_map/psum | solution.py:50
  10.5 43.4 %copy-start = (bf16[1,2048,768]{1,2,0:T(8,128)(2,1)}, bf16[1,2048,768]{1,2,0:T(8,128)(2,1)S(1)}, u32[]{:S(2)}) copy-start(bf16[1,2048,768]{1,2,0:T(8,128)(2,1)S(1)} %copy.20) | copy-start | bytes 9437188
  11.1 26.5 %copy-start.12 = (f32[2048]{0:T(1024)}, f32[2048]{0:T(1024)S(1)}, u32[]{:S(2)}) copy-start(f32[2048]{0:T(1024)S(1)} %add_rsqrt_fusion) | copy-start | bytes 24580
  16.2 10.4 %copy-start.5 = (bf16[1,2048,768]{2,1,0:T(8,128)(2,1)S(1)}, bf16[1,2048,768]{2,1,0:T(8,128)(2,1)}, u32[]{:S(2)}) copy-start(bf16[1,2048,768]{2,1,0:T(8,128)(2,1)} %param.11) | copy-start | bytes 9437188
  16.2 21.4 %slice-start = ((s8[5505024]{0:T(1024)(128)(4,1)}), s8[4194304]{0:T(1024)(128)(4,1)S(1)}, s32[]{:S(2)}) async-start(s8[5505024]{0:T(1024)(128)(4,1)} %bitcast.76), calls=%async_computation.1 | async-start | bytes 8388608
  26.5 11.1 %slice-start.1 = ((s8[5505024]{0:T(1024)(128)(4,1)}), s8[1310720]{0:T(1024)(128)(4,1)S(1)}, s32[]{:S(2)}) async-start(s8[5505024]{0:T(1024)(128)(4,1)} %bitcast.76), calls=%async_computation.2 | async-start | bytes 2621440
  63.5 1.7 copy-start.7
  63.6 1.7 copy-start.10
  74.5 23.3 %copy-start.8 = (bf16[2048,768]{0,1:T(8,128)(2,1)S(1)}, bf16[2048,768]{0,1:T(8,128)(2,1)}, u32[]{:S(2)}) copy-start(bf16[2048,768]{0,1:T(8,128)(2,1)} %copy-done.7) | copy-start | bytes 9437188
  97.8 10.8 %copy-start.14 = (bf16[2048,1792]{1,0:T(8,128)(2,1)S(1)}, bf16[2048,1792]{1,0:T(8,128)(2,1)}, u32[]{:S(2)}) copy-start(bf16[2048,1792]{1,0:T(8,128)(2,1)} %get-tuple-element.28) | copy-start | bytes 22020100
  108.6 9.2 %copy-start.6 = (bf16[1,2048,768]{2,1,0:T(8,128)(2,1)S(1)}, bf16[1,2048,768]{2,1,0:T(8,128)(2,1)}, u32[]{:S(2)}) copy-start(bf16[1,2048,768]{2,1,0:T(8,128)(2,1)} %param.12) | copy-start | bytes 9437188
  117.8 14.1 %copy-start.9 = (bf16[2048,768]{0,1:T(8,128)(2,1)S(1)}, bf16[2048,768]{0,1:T(8,128)(2,1)}, u32[]{:S(2)}) copy-start(bf16[2048,768]{0,1:T(8,128)(2,1)} %copy-done.7) | copy-start | bytes 9437188
  117.8 26.6 %slice-start.2 = ((s8[5505024]{0:T(1024)(128)(4,1)}), s8[4194304]{0:T(1024)(128)(4,1)S(1)}, s32[]{:S(2)}) async-start(s8[5505024]{0:T(1024)(128)(4,1)} %bitcast.78), calls=%async_computation.3 | async-start | bytes 8388608
  131.9 12.5 %slice-start.3 = ((s8[5505024]{0:T(1024)(128)(4,1)}), s8[1310720]{0:T(1024)(128)(4,1)S(1)}, s32[]{:S(2)}) async-start(s8[5505024]{0:T(1024)(128)(4,1)} %bitcast.78), calls=%async_computation.4 | async-start | bytes 2621440
  144.4 14.0 %copy-start.11 = (f32[2048]{0:T(1024)S(1)}, f32[2048]{0:T(1024)}, u32[]{:S(2)}) copy-start(f32[2048]{0:T(1024)} %copy-done.10) | copy-start | bytes 24580
  144.4 14.0 %copy-start.2 = (bf16[1,2048,768]{1,2,0:T(8,128)(2,1)S(1)}, bf16[1,2048,768]{1,2,0:T(8,128)(2,1)}, u32[]{:S(2)}) copy-start(bf16[1,2048,768]{1,2,0:T(8,128)(2,1)} %copy.21) | copy-start | bytes 9437188
  158.5 14.6 %slice-start.4 = ((s8[5505024]{0:T(1024)(128)(4,1)}), s8[1310720]{0:T(1024)(128)(4,1)S(1)}, s32[]{:S(2)}) async-start(s8[5505024]{0:T(1024)(128)(4,1)} %bitcast.80), calls=%async_computation.5 | async-start | bytes 2621440
  163.6 9.4 %slice-start.5 = ((s8[5505024]{0:T(1024)(128)(4,1)}), s8[4194304]{0:T(1024)(128)(4,1)S(1)}, s32[]{:S(2)}) async-start(s8[5505024]{0:T(1024)(128)(4,1)} %bitcast.80), calls=%async_computation.6 | async-start | bytes 8388608
  173.1 6.4 %copy-start.1 = (bf16[1,2048,768]{1,2,0:T(8,128)(2,1)S(1)}, bf16[1,2048,768]{1,2,0:T(8,128)(2,1)}, u32[]{:S(2)}) copy-start(bf16[1,2048,768]{1,2,0:T(8,128)(2,1)} %copy-done) | copy-start | bytes 9437188
  173.1 6.4 %copy-start.13 = (f32[2048]{0:T(1024)S(1)}, f32[2048]{0:T(1024)}, u32[]{:S(2)}) copy-start(f32[2048]{0:T(1024)} %copy-done.12) | copy-start | bytes 24580
  179.5 14.2 %copy-start.15 = (bf16[2048,1792]{1,0:T(8,128)(2,1)}, bf16[2048,1792]{1,0:T(8,128)(2,1)S(1)}, u32[]{:S(2)}) copy-start(bf16[2048,1792]{1,0:T(8,128)(2,1)S(1)} %convolution_convert_fusion) | copy-start | bytes 22020100
  549.0 12.2 %copy-start.3 = (bf16[1,768,1792]{2,1,0:T(8,128)(2,1)S(1)}, bf16[1,768,1792]{2,1,0:T(8,128)(2,1)}, u32[]{:S(2)}) copy-start(bf16[1,768,1792]{2,1,0:T(8,128)(2,1)} %get-tuple-element.9) | copy-start | bytes 8257540
  549.0 12.2 %copy-start.4 = (bf16[1,768,1792]{2,1,0:T(8,128)(2,1)S(1)}, bf16[1,768,1792]{2,1,0:T(8,128)(2,1)}, u32[]{:S(2)}) copy-start(bf16[1,768,1792]{2,1,0:T(8,128)(2,1)} %get-tuple-element.10) | copy-start | bytes 8257540
Sparse Core Ops, SparseCore 0:
  210.9 338.0 all-reduce.2
where the time goes:
time: 641 us; the launch traced here: 633 us
  waiting for transfers between devices  338 us (53%)
  matrix products  187 us (29%)
  other arithmetic  80.7 us (13%)
  between operations  16.8 us (3%)
  local copies, waits for them, and re-layouts  9.95 us (2%)
    psum x1, waiting for transfers between devices, step(): summed[number] = [lax.psum(by_w[name], 'dp') for name in NAMES]  338 us
    dot_general x5, matrix products, layer(): gate = jnp.dot(a, w['w_gate'], preferred_element_type=jnp.float32)  71.4 us
    dot_general x5, matrix products, layer(): up = jnp.dot(a, w['w_up'], preferred_element_type=jnp.float32)  66.1 us
    convert_element_type x2, other arithmetic, adamw(): return ((w - 0.02 * step).astype(jnp.bfloat16), m, v)  59.2 us
    dot_general x5, matrix products, matmul(): jnp.dot(a, w, preferred_element_type=jnp.float32).astype(jnp.bfloat16)  50 us
    reduce_sum x3, other arithmetic, step(): jnp.sum(g * g)  15.7 us
  transfers between devices with their start and end apart: 1, of which 1 were waited for; matrix products, arithmetic and copies ran while one was open for 0% of the time, Pallas kernels for 0%

commit v1 on v0

v1 whole, which is shorter than its diff:
```python
import functools

import jax
import jax.numpy as jnp
from jax import lax
from jax.experimental import pallas as pl
from jax.experimental.pallas import tpu as pltpu
from jax.sharding import PartitionSpec as P


BW = 256
RB = 3
f32, bf16 = jnp.float32, jnp.bfloat16
NT = (((1,), (1,)), ((), ()))
TN = (((0,), (0,)), ((), ()))

def mm(a, b, dims=(((1,), (0,)), ((), ()))):
    return lax.dot_general(a, b, dims, preferred_element_type=f32)

def rms_scale(wide):
    return lax.rsqrt(jnp.mean(wide * wide, -1, keepdims=True) + 1e-6)

def sigmoid(x):
    return 0.5 * jnp.tanh(0.5 * x) + 0.5

def kernel(cfg, x_in, dy_in, wg_in, wu_in, wd_in, own0, own1, ss, S, xh, a, aT, dh, hid, wg, wu, wd, recv,
           load_sem, x_sem, own_sem, send_sem, recv_sem, credit):
    n, T, D, F, tt, tb, comm = cfg["n"], cfg["T"], cfg["D"], cfg["F"], cfg["tt"], cfg["tb"], cfg["comm"]
    NB = F // BW
    NBLK = 2 * NB
    H = D // (2 * n)
    CH = 3 * H
    BR = 3 * D
    GB = NB * BR
    hr = BW // (2 * n)
    ncg = D // BW
    ramp = min(3, NBLK - 1)
    start = lambda b: jnp.where(b <= ramp, 2 * b, b + ramp)
    LAST = NBLK - 1 + ramp + n - 2
    me = lax.axis_index("dp")
    right, left = lax.rem(me + 1, n), lax.rem(me + n - 1, n)

    loads = [pltpu.make_async_copy(s, d, load_sem.at[i]) for i, (s, d) in enumerate((
        (x_in, xh), (wg_in.at[0], wg.at[0]), (wu_in.at[0], wu.at[0]), (wd_in.at[0], wd.at[0]), (dy_in, dh),
        (wg_in.at[1], wg.at[1]), (wu_in.at[1], wu.at[1]), (wd_in.at[1], wd.at[1])))]
    for c in loads[:4]:
        c.start()
    if comm:
        barrier = pltpu.get_barrier_semaphore()
        for nb in (left, right):
            pl.semaphore_signal(barrier, inc=1, device_id={"dp": nb}, device_id_type=pl.DeviceIdType.MESH)
    ss[...] = jnp.zeros_like(ss)

    def chunk_row(b, c, d):
        return pl.multiple_of(b * BR + (2 * c + d) * CH, 16)

    def chunk_of(s, d):
        return lax.rem(me + 2 * n - 1 - s, n) if d == 0 else lax.rem(me + 1 + s, n)

    def block_of(r, s):
        z = r - s
        b = jnp.where(z < 2 * ramp, lax.div(z, 2), z - ramp)
        return b, (z >= 0) & ((z >= 2 * ramp) | (lax.rem(z, 2) == 0)) & (b < NBLK)

    def hop(r, s, d):
        b, _ = block_of(r, s)
        slot = lax.rem(r, RB) * (n - 1) + s
        return pltpu.make_async_remote_copy(
            src_ref=S.at[pl.ds(chunk_row(b, chunk_of(s, d), d), CH), :], dst_ref=recv.at[d, slot],
            send_sem=send_sem.at[d, slot], recv_sem=recv_sem.at[d, slot],
            device_id={"dp": right if d == 0 else left}, device_id_type=pl.DeviceIdType.MESH)

    def arrival(d, slot):
        return pltpu.make_async_remote_copy(
            src_ref=recv.at[d, slot], dst_ref=recv.at[d, slot], send_sem=send_sem.at[d, slot], recv_sem=recv_sem.at[d, slot],
            device_id={"dp": right if d == 0 else left}, device_id_type=pl.DeviceIdType.MESH)

    def op(q, _):
        r, s = lax.div(q, n), lax.rem(q, n)
        b, live = block_of(r, s)
        @pl.when((s == 0) & (r >= RB) & (r <= LAST))
        def _():
            pl.semaphore_wait(credit.at[0], 1)
            pl.semaphore_wait(credit.at[1], 1)
        @pl.when(live & (s >= 1))
        def _():
            slot = lax.rem(r + RB - 1, RB) * (n - 1) + s - 1
            for d in range(2):
                arrival(d, slot).wait_recv()
                rows = pl.ds(chunk_row(b, chunk_of(s, d), d), CH)
                total = (S[rows, :].astype(f32) + recv[d, slot].astype(f32)).astype(bf16)
                S[rows, :] = total
                @pl.when(s == n - 1)
                def _():
                    t = total.astype(f32)
                    t = t * t
                    ss[...] += functools.reduce(jnp.add, [t[i * 8:(i + 1) * 8, h * 128:(h + 1) * 128] for i in range(CH // 8) for h in range(BW // 128)])
        @pl.when(live & (s == n - 1))
        def _():
            for d in range(2):
                pltpu.make_async_copy(S.at[pl.ds(chunk_row(b, me, d), CH), :], (own0, own1)[d].at[b], own_sem.at[d, b]).start()
        _, before = block_of(r - RB, s)
        @pl.when((s <= n - 2) & (r >= RB) & before)
        def _():
            for d in range(2):
                hop(r - RB, s, d).wait_send()
        @pl.when(live & (s <= n - 2))
        def _():
            for d in range(2):
                hop(r, s, d).start()
        @pl.when((s == n - 1) & (r >= 1) & (r <= LAST - RB + 1))
        def _():
            pl.semaphore_signal(credit.at[0], inc=1, device_id={"dp": left}, device_id_type=pl.DeviceIdType.MESH)
            pl.semaphore_signal(credit.at[1], inc=1, device_id={"dp": right}, device_id_type=pl.DeviceIdType.MESH)
        return 0

    def ops(q, count, ready):
        if not comm:
            return q
        limit = n * start(ready)
        end = jnp.where(q + count < limit, q + count, limit)
        lax.fori_loop(q, end, op, 0)
        return end

    for c in loads[:4]:
        c.wait()
    for c in loads[4:]:
        c.start()
    def fwd(t, _):
        rows = pl.ds(pl.multiple_of(t * tt, tt), tt)
        xw = xh[rows, :].astype(f32)
        at = (xw * rms_scale(xw)).astype(bf16)
        parts = []
        for j in range(NB):
            cols = slice(j * BW, (j + 1) * BW)
            g = mm(at, wg[0, :, cols])
            u = mm(at, wu[0, :, cols])
            parts.append((g * sigmoid(g) * u).astype(bf16))
        down = mm(jnp.concatenate(parts, axis=1), wd[0]).astype(bf16)
        h = (xw + down.astype(f32)).astype(bf16)
        xh[rows, :] = h
        hw = h.astype(f32)
        a1 = (hw * rms_scale(hw)).astype(bf16)
        a[rows, :] = a1
        aT[:, rows] = a1.T
        return 0
    lax.fori_loop(0, T // tt, fwd, 0)

    def block(l, j, dg0, du0, b, q, pace):
        cols = pl.ds(pl.multiple_of(j * BW, BW), BW)
        def tokens(t, q):
            q = ops(q, pace[0], b)
            rows = pl.ds(pl.multiple_of(t * tb, tb), tb)
            at = a[rows, :]
            g = mm(at, wg[l, :, cols])
            u = mm(at, wu[l, :, cols])
            dhid = mm(dh[rows, :], wd[l, cols, :], NT).astype(bf16).astype(f32)
            sg = sigmoid(g)
            s = g * sg
            hid[rows, :] = (s * u).astype(bf16)
            S[pl.ds(pl.multiple_of(du0 + t * tb, 16), tb), :] = (dhid * s).astype(bf16)
            S[pl.ds(pl.multiple_of(dg0 + t * tb, 16), tb), :] = (dhid * u * (sg + s * (1.0 - sg))).astype(bf16)
            return q
        q = lax.fori_loop(0, T // tb, tokens, q)
        base = b * BR
        def matmul_gate_up(k, row0):
            w = mm(aT[...], S[pl.ds(pl.multiple_of(row0, 16), T), :]).astype(bf16)
            for e in range(2 * n):
                S[pl.ds(pl.multiple_of(base + e * CH + k * H, 16), H), :] = w[e * H:(e + 1) * H]
        q = ops(q, pace[1], b)
        matmul_gate_up(0, dg0)
        q = ops(q, pace[1], b)
        matmul_gate_up(1, du0)
        q = ops(q, pace[1], b)
        w = mm(hid[...], dh[...], TN).astype(bf16)
        for e in range(2 * n):
            for cg in range(ncg):
                S[pl.ds(pl.multiple_of(base + e * CH + 2 * H + cg * hr, 16), hr), :] = w[e * hr:(e + 1) * hr, cg * BW:(cg + 1) * BW]
        return q

    for c in loads[4:]:
        c.wait()
    def last_layer(j, q):
        pace = jnp.where(j <= 2, n, 2)
        return block(1, j, GB + j * 2 * T, GB + j * 2 * T + T, j, q, (pace, pace))
    if comm:
        pl.semaphore_wait(barrier, 2)
    q = lax.fori_loop(0, NB, last_layer, 0)

    def d_input(t, q):
        q = ops(q, 3, NB)
        rows = pl.ds(pl.multiple_of(t * tt, tt), tt)
        dg = jnp.concatenate([S[pl.ds(pl.multiple_of(GB + j * 2 * T + t * tt, 16), tt), :] for j in range(NB)], axis=1)
        du = jnp.concatenate([S[pl.ds(pl.multiple_of(GB + j * 2 * T + T + t * tt, 16), tt), :] for j in range(NB)], axis=1)
        da = (mm(dg, wg[1], NT).astype(bf16).astype(f32) + mm(du, wu[1], NT).astype(bf16).astype(f32)).astype(bf16).astype(f32)
        wide = xh[rows, :].astype(f32)
        scale = rms_scale(wide)
        dot = jnp.sum(da * wide, -1, keepdims=True)
        dw = da * scale - wide * (scale * scale * scale * dot * (1.0 / D))
        dh[rows, :] = (dh[rows, :].astype(f32) + dw.astype(bf16).astype(f32)).astype(bf16)
        pltpu.make_async_copy(x_in.at[rows, :], xh.at[rows, :], x_sem).start()
        return q
    q = lax.fori_loop(0, T // tt, d_input, q)
    def renorm(t, q):
        rows = pl.ds(pl.multiple_of(t * tt, tt), tt)
        wide = xh[rows, :].astype(f32)
        a0 = (wide * rms_scale(wide)).astype(bf16)
        a[rows, :] = a0
        aT[:, rows] = a0.T
        return q
    pltpu.make_async_copy(x_in, xh, x_sem).wait()
    q = ops(q, 2, NB)
    lax.fori_loop(0, T // tt, renorm, 0)

    def first_layer(j, q):
        return block(0, j, 2 * GB, 2 * GB + T, NB + j, q, (1, 2))
    q = lax.fori_loop(0, NB, first_layer, q)
    if comm:
        lax.fori_loop(q, (LAST + 2) * n, op, 0)
        for r in range(LAST - RB + 2, LAST + 1):
            for s in range(n - 1):
                z = r - s
                b = z // 2 if z < 2 * ramp else z - ramp
                if z >= 0 and (z >= 2 * ramp or z % 2 == 0) and b < NBLK:
                    for d in range(2):
                        hop(r, s, d).wait_send()
        for d in range(2):
            for b in range(NBLK):
                pltpu.make_async_copy(S.at[pl.ds(0, CH), :], (own0, own1)[d].at[b], own_sem.at[d, b]).wait()
    else:
        cps = [pltpu.make_async_copy(S.at[pl.ds(b * BR + d * CH, CH), :], (own0, own1)[d].at[b], own_sem.at[d, b]) for d in range(2) for b in range(NBLK)]
        for c in cps: c.start()
        for c in cps: c.wait()

def k1(x, dy, wg, wu, wd, n, tt=256, tb=512, comm=True, cid=0):
    T, D = x.shape
    F = wg.shape[2]
    NB = F // BW
    NBLK = 2 * NB
    H = D // (2 * n); CH = 3 * H
    GB = NB * 3 * D
    cfg = dict(n=n, T=T, D=D, F=F, tt=min(tt, T), tb=min(tb, T), comm=comm)
    any_ = pl.BlockSpec(memory_space=pl.ANY)
    flops = 18 * 2 * T * D * F
    return pl.pallas_call(
        functools.partial(kernel, cfg),
        out_shape=(jax.ShapeDtypeStruct((NBLK, CH, BW), bf16),) * 2 + (jax.ShapeDtypeStruct((8, 128), f32),),
        in_specs=[any_] * 5,
        out_specs=(any_, any_, pl.BlockSpec(memory_space=pltpu.VMEM)),
        scratch_shapes=[
            pltpu.VMEM((max(GB + NB * 2 * T, 2 * GB + 2 * T), BW), bf16),
            pltpu.VMEM((T, D), bf16), pltpu.VMEM((T, D), bf16), pltpu.VMEM((D, T), bf16), pltpu.VMEM((T, D), bf16),
            pltpu.VMEM((T, BW), bf16),
            pltpu.VMEM((2, D, F), bf16), pltpu.VMEM((2, D, F), bf16), pltpu.VMEM((2, F, D), bf16),
            pltpu.VMEM((2, RB * (n - 1), CH, BW), bf16),
            pltpu.SemaphoreType.DMA((8,)), pltpu.SemaphoreType.DMA, pltpu.SemaphoreType.DMA((2, NBLK)),
            pltpu.SemaphoreType.DMA((2, RB * (n - 1))), pltpu.SemaphoreType.DMA((2, RB * (n - 1))), pltpu.SemaphoreType.REGULAR((2,)),
        ],
        compiler_params=pltpu.CompilerParams(vmem_limit_bytes=67043328, collective_id=cid if comm else None, has_side_effects=True),
        cost_estimate=pl.CostEstimate(flops=flops, bytes_accessed=40 * 10**6, transcendentals=0),
        name="grads")(x, dy, wg, wu, wd)


def adam_math(w, m, v, g):
    m = 0.9 * m + 0.1 * g
    v = 0.95 * v + 0.05 * g * g
    step = m * lax.rsqrt(v + 1e-8) + 0.1 * w
    return (w - 0.02 * step).astype(jnp.bfloat16), m, v

def opt_body(nb, idx_ref, fac_ref, p0, p1, wg, wu, wd, mg, mu, md, vg, vu, vd, *rest):
    outs = rest[-9:]
    factor = fac_ref[0]
    def one(p):
        for k,(w,m,v,o) in enumerate(((wg,mg,vg,0),(wu,mu,vu,1))):
            for j in range(nb):
                c = slice(j*BW,(j+1)*BW)
                g = p[0,j,k].astype(jnp.float32)*factor
                a,b,cc = adam_math(w[0,0,:,c].astype(jnp.float32), m[0,0,:,c], v[0,0,:,c], g)
                outs[o][0,0,:,c]=a; outs[3+o][0,0,:,c]=b; outs[6+o][0,0,:,c]=cc
        r = wd.shape[3]
        for j in range(nb):
            for q in range(wd.shape[4]//BW):
                c = slice(q*BW,(q+1)*BW)
                g = p[0,j,2,q*r:(q+1)*r].astype(jnp.float32)*factor
                a,b,cc = adam_math(wd[0,j,0,:,c].astype(jnp.float32), md[0,j,0,:,c], vd[0,j,0,:,c], g)
                outs[2][0,j,0,:,c]=a; outs[5][0,j,0,:,c]=b; outs[8][0,j,0,:,c]=cc
    d = pl.program_id(0)
    @pl.when(d==0)
    def _(): one(p0)
    @pl.when(d==1)
    def _(): one(p1)

def opt_call(idx, fac, p0, p1, ins, prev):
    L, nb = p0.shape[0], p0.shape[1]
    wg, wd = ins[0], ins[2]
    def gm(d,l,idx): return (l, jnp.where(d==0, idx[0], idx[1]), 0, 0)
    def dm(d,l,idx): return (l, 0, jnp.where(d==0, idx[0], idx[1]), 0, 0)
    gs = pl.BlockSpec((1,1)+wg.shape[2:], gm)
    ds = pl.BlockSpec((1,nb,1)+wd.shape[3:], dm)
    ps0 = pl.BlockSpec((1,)+p0.shape[1:], lambda d,l,idx:(L-1-jnp.where(d==0,l,L-1),0,0,0,0))
    ps1 = pl.BlockSpec((1,)+p0.shape[1:], lambda d,l,idx:(L-1-jnp.where(d==0,0,l),0,0,0,0))
    specs=[gs,gs,ds]*3
    any_=[pl.BlockSpec(memory_space=pl.ANY)]*9 if prev is not None else []
    fresh = prev is None
    grid_spec=pltpu.PrefetchScalarGridSpec(num_scalar_prefetch=1, grid=(2,L),
        in_specs=[pl.BlockSpec(memory_space=pltpu.SMEM),ps0,ps1]+specs+any_, out_specs=specs)
    odt=[jnp.bfloat16]*3+[jnp.float32]*6
    n=sum(x.size for x in ins[:3])
    return pl.pallas_call(functools.partial(opt_body,nb), grid_spec=grid_spec,
        out_shape=[jax.ShapeDtypeStruct(x.shape,t) for x,t in zip(ins,odt)],
        input_output_aliases={} if fresh else {13+i:i for i in range(9)},
        compiler_params=pltpu.CompilerParams(vmem_limit_bytes=62*2**20, dimension_semantics=("arbitrary","arbitrary")),
        cost_estimate=pl.CostEstimate(flops=int(5e9),bytes_accessed=22*10**6,transcendentals=0),
        name="adamw")(idx, fac, p0, p1, *ins, *(prev or []))
def views(arrs, n):
    out=[]
    for i,a in enumerate(arrs):
        L,r,c=a.shape
        if i%3<2: out.append(a.reshape(L,2*n,r//(2*n),c))
        else:
            nb=r//BW
            out.append(a.reshape(L,nb,2*n,BW//(2*n),c))
    return out


def solution(mesh):
    n = mesh.shape["dp"]
    right = [(i, (i + 1) % n) for i in range(n)]
    left = [(i, (i - 1) % n) for i in range(n)]

    def step(x, dy, *arrays):
        me = lax.axis_index("dp")
        own0, own1, squares = k1(x[0], dy[0], *arrays[:3], n)
        L, _, F = arrays[0].shape
        NB = F // BW
        ins = views(arrays, n)
        count = sum(w.size for w in arrays[:3])
        a, b = (o.reshape(L, NB, 3, o.shape[1] // 3, BW) for o in (own0, own1))
        factor, outs = None, None
        for s in range(n):
            na = nb = None
            if s < n - 1:
                na = lax.ppermute(a, "dp", right)
                nb = lax.ppermute(b, "dp", left)
            if factor is None:
                total = lax.psum(jnp.sum(squares), "dp")
                factor = jnp.minimum(1.0, 0.5 * lax.rsqrt(total / count + 1e-30)).reshape(1)
            c0, c1 = lax.rem(me - s + n, n), lax.rem(me + s, n)
            idx = jnp.stack([2 * c0, 2 * c1 + 1]).astype(jnp.int32)
            outs = opt_call(idx, factor, a, b, ins, outs)
            a, b = na, nb
        return tuple(o.reshape(w.shape) for o, w in zip(outs, arrays))

    step = jax.shard_map(
        step,
        mesh=mesh,
        in_specs=(P(("rep", "dp"), None, None),) * 2 + (P(None, None, None),) * 9,
        out_specs=(P("rep", None, None),) * 9,
        check_vma=False,
    )
    return step
```

time: 641 us -> 440 us (0.69)
  the two profiles are of different devices: /device:TPU:21 before, /device:TPU:22 now
where the time goes in v1:
time: 440 us; the launch traced here: 439 us
  Pallas kernels  320 us (73%)
  waiting for transfers between devices  70.1 us (16%)
  blocking collectives  26.6 us (6%)
  starting transfers between devices  14.6 us (3%)
  other arithmetic  6.37 us (1%)
    pallas_call x1, Pallas kernels, k1(): pl.pallas_call(functools.partial(kernel, cfg), out_shape=(jax.ShapeDtypeS...  240 us
    pallas_call x8, Pallas kernels, opt_call(): pl.pallas_call(functools.partial(opt_body, nb), grid_spec=grid_spec, out_...  79.9 us
    ppermute x7, waiting for transfers between devices, step(): nb = lax.ppermute(b, 'dp', left)  69.8 us
    psum x1, blocking collectives, step(): total = lax.psum(jnp.sum(squares), 'dp')  26.6 us
    ppermute x7, starting transfers between devices, step(): nb = lax.ppermute(b, 'dp', left)  10.8 us
  transfers between devices with their start and end apart: 14, of which 5 were waited for; matrix products, arithmetic and copies ran while one was open for 1% of the time, Pallas kernels for 16%

profile of v1, /device:TPU:22, one launch (start us, length us, event | category | flops | bytes accessed | tf_op | source)
XLA Modules:
  0.0 439.2 jit_solution(10784373955740254072)
XLA Ops:
  0.6 240.1 %grads.1 = (bf16[14,144,256]{2,1,0:T(8,128)(2,1)}, bf16[14,144,256]{2,1,0:T(8,128)(2,1)}, f32[8,128]{1,0:T(8,128)}) custom-call(bf16[2048,768]{1,0:T(8,128)(2,1)} %bitcast.124, bf16[2048,768]{1,0:T(8,128)(2,1)} %bitcast.125, bf16[2,768,1792]{2,1,0:T(8,128)(2,1)} %wg_in.1, bf16[2,768,1792]{2,1,0:T(8,128)(2,1)} %wu_in.1, bf16[2,1792,768]{2,1,0:T(8,128)(2,1)} %wd_in.1), custom_call_target="tpu_custom_call" | custom-call | flops 101468602368 | bytes 40000000 | tf_op jit(solution)/shard_map/grads/pallas_call | solution.py:245
  240.7 1.4 collective-permute-start.7
  242.1 0.7 collective-permute-start
  242.8 21.2 %collective-permute-done.7.p1 = bf16[2,7,3,48,256]{4,3,2,1,0:T(8,128)(2,1)S(1)} collective-permute-done((bf16[2,7,3,48,256]{4,3,2,1,0:T(8,128)(2,1)}, bf16[2,7,3,48,256]{4,3,2,1,0:T(8,128)(2,1)S(1)}, u32[]{:S(2)}, u32[]{:S(2)}) %collective-permute-start.7) | collective-permute-done | bytes 1032224 | tf_op jit(solution)/shard_map/ppermute | solution.py:344
  264.0 1.3 collective-permute-start.8
  266.0 20.9 %collective-permute-done.8.p1 = bf16[2,7,3,48,256]{4,3,2,1,0:T(8,128)(2,1)S(1)} collective-permute-done((bf16[2,7,3,48,256]{4,3,2,1,0:T(8,128)(2,1)S(1)}, bf16[2,7,3,48,256]{4,3,2,1,0:T(8,128)(2,1)S(1)}, u32[]{:S(2)}, u32[]{:S(2)}) %collective-permute-start.8) | collective-permute-done | bytes 1032224 | tf_op jit(solution)/shard_map/ppermute | solution.py:344
  287.0 1.3 collective-permute-start.9
  289.0 20.8 %collective-permute-done.9.p1 = bf16[2,7,3,48,256]{4,3,2,1,0:T(8,128)(2,1)S(1)} collective-permute-done((bf16[2,7,3,48,256]{4,3,2,1,0:T(8,128)(2,1)S(1)}, bf16[2,7,3,48,256]{4,3,2,1,0:T(8,128)(2,1)S(1)}, u32[]{:S(2)}, u32[]{:S(2)}) %collective-permute-start.9) | collective-permute-done | bytes 1032224 | tf_op jit(solution)/shard_map/ppermute | solution.py:344
  309.8 1.4 collective-permute-start.10
  312.0 1.3 reduce_sum.9
  313.3 26.6 %psum.7 = f32[]{:T(128)} all-reduce(f32[]{:T(128)} %reduce_sum.9), channel_id=1, replica_groups=mesh['rep'=8,'dp'=8] {'dp'}, use_global_device_ids=true, to_apply=%region_1.0 | all-reduce | flops 1 | bytes 8 | tf_op jit(solution)/shard_map/psum | solution.py:346
  341.8 2.0 collective-permute-start.11
  347.8 9.9 %adamw.8 = (bf16[2,16,48,1792]{3,2,1,0:T(8,128)(2,1)}, bf16[2,16,48,1792]{3,2,1,0:T(8,128)(2,1)}, bf16[2,7,16,16,768]{4,3,2,1,0:T(8,128)(2,1)}, f32[2,16,48,1792...) custom-call(s32[2]{0:T(128)} %pad_add_fusion.7.idx_ref, ...), custom_call_target="tpu_custom_call" | custom-call | flops 5000000000 | bytes 22000000 | tf_op jit(solution)/shard_map/adamw/pallas_call | solution.py:309
  357.7 6.9 %collective-permute-done.11.p1 = bf16[2,7,3,48,256]{4,3,2,1,0:T(8,128)(2,1)} collective-permute-done((bf16[2,7,3,48,256]{4,3,2,1,0:T(8,128)(2,1)S(1)}, bf16[2,7,3,48,256]{4,3,2,1,0:T(8,128)(2,1)}, u32[]{:S(2)}, u32[]{:S(2)}) %collective-permute-start.11) | collective-permute-done | bytes 1032224 | tf_op jit(solution)/shard_map/ppermute | solution.py:344
  364.6 0.9 collective-permute-start.12
  365.7 0.9 collective-permute-start.5
  366.6 9.9 %adamw.9 = (bf16[2,16,48,1792]{3,2,1,0:T(8,128)(2,1)}, bf16[2,16,48,1792]{3,2,1,0:T(8,128)(2,1)}, bf16[2,7,16,16,768]{4,3,2,1,0:T(8,128)(2,1)}, f32[2,16,48,1792...) custom-call(s32[2]{0:T(128)} %pad_add_fusion.6.idx_ref, ...), custom_call_target="tpu_custom_call", output_to_operand_aliasing={{0}: (13, {}), {1}: (14, {}), {2}: (15, {}), {3}: (16, {}),... | custom-call | flops 5000000000 | bytes 22000000 | tf_op jit(solution)/shard_map/adamw/pallas_call | solution.py:309
  376.6 10.0 %adamw.10 = (bf16[2,16,48,1792]{3,2,1,0:T(8,128)(2,1)}, bf16[2,16,48,1792]{3,2,1,0:T(8,128)(2,1)}, bf16[2,7,16,16,768]{4,3,2,1,0:T(8,128)(2,1)}, f32[2,16,48,179...) custom-call(s32[2]{0:T(128)} %pad_add_fusion.5.idx_ref, ...), custom_call_target="tpu_custom_call", output_to_operand_aliasing={{0}: (13, {}), {1}: (14, {}), {2}: (15, {}), {3}: (16, {}),... | custom-call | flops 5000000000 | bytes 22000000 | tf_op jit(solution)/shard_map/adamw/pallas_call | solution.py:309
  386.6 10.0 %adamw.11 = (bf16[2,16,48,1792]{3,2,1,0:T(8,128)(2,1)}, bf16[2,16,48,1792]{3,2,1,0:T(8,128)(2,1)}, bf16[2,7,16,16,768]{4,3,2,1,0:T(8,128)(2,1)}, f32[2,16,48,179...) custom-call(s32[2]{0:T(128)} %pad_add_fusion.4.idx_ref, ...), custom_call_target="tpu_custom_call", output_to_operand_aliasing={{0}: (13, {}), {1}: (14, {}), {2}: (15, {}), {3}: (16, {}),... | custom-call | flops 5000000000 | bytes 22000000 | tf_op jit(solution)/shard_map/adamw/pallas_call | solution.py:309
  396.6 2.4 collective-permute-start.13
  399.0 9.9 %adamw.12 = (bf16[2,16,48,1792]{3,2,1,0:T(8,128)(2,1)}, bf16[2,16,48,1792]{3,2,1,0:T(8,128)(2,1)}, bf16[2,7,16,16,768]{4,3,2,1,0:T(8,128)(2,1)}, f32[2,16,48,179...) custom-call(s32[2]{0:T(128)} %pad_add_fusion.3.idx_ref, ...), custom_call_target="tpu_custom_call", output_to_operand_aliasing={{0}: (13, {}), {1}: (14, {}), {2}: (15, {}), {3}: (16, {}),... | custom-call | flops 5000000000 | bytes 22000000 | tf_op jit(solution)/shard_map/adamw/pallas_call | solution.py:309
  409.0 10.0 %adamw.13 = (bf16[2,16,48,1792]{3,2,1,0:T(8,128)(2,1)}, bf16[2,16,48,1792]{3,2,1,0:T(8,128)(2,1)}, bf16[2,7,16,16,768]{4,3,2,1,0:T(8,128)(2,1)}, f32[2,16,48,179...) custom-call(s32[2]{0:T(128)} %pad_add_fusion.2.idx_ref, ...), custom_call_target="tpu_custom_call", output_to_operand_aliasing={{0}: (13, {}), {1}: (14, {}), {2}: (15, {}), {3}: (16, {}),... | custom-call | flops 5000000000 | bytes 22000000 | tf_op jit(solution)/shard_map/adamw/pallas_call | solution.py:309
  419.0 10.0 %adamw.14 = (bf16[2,16,48,1792]{3,2,1,0:T(8,128)(2,1)}, bf16[2,16,48,1792]{3,2,1,0:T(8,128)(2,1)}, bf16[2,7,16,16,768]{4,3,2,1,0:T(8,128)(2,1)}, f32[2,16,48,179...) custom-call(s32[2]{0:T(128)} %pad_add_fusion.1.idx_ref, ...), custom_call_target="tpu_custom_call", output_to_operand_aliasing={{0}: (13, {}), {1}: (14, {}), {2}: (15, {}), {3}: (16, {}),... | custom-call | flops 5000000000 | bytes 22000000 | tf_op jit(solution)/shard_map/adamw/pallas_call | solution.py:309
  429.0 10.0 %adamw.15 = (bf16[2,16,48,1792]{3,2,1,0:T(8,128)(2,1)}, bf16[2,16,48,1792]{3,2,1,0:T(8,128)(2,1)}, bf16[2,7,16,16,768]{4,3,2,1,0:T(8,128)(2,1)}, f32[2,16,48,179...) custom-call(s32[2]{0:T(128)} %pad_add_fusion.idx_ref, ...), custom_call_target="tpu_custom_call", output_to_operand_aliasing={{0}: (13, {}), {1}: (14, {}), {2}: (15, {}), {3}: (16, {}),... | custom-call | flops 5000000000 | bytes 22000000 | tf_op jit(solution)/shard_map/adamw/pallas_call | solution.py:309
  (37 shorter events, 7.5 us)
Async XLA Ops:
  240.7 23.3 %collective-permute-start.7 = (bf16[2,7,3,48,256]{4,3,2,1,0:T(8,128)(2,1)}, bf16[2,7,3,48,256]{4,3,2,1,0:T(8,128)(2,1)S(1)}, u32[]{:S(2)}, u32[]{:S(2)}) collective-permute-start(bf16[2,7,3,48,256]{4,3,2,1,0:T(8,128)(2,1)} %bitcast.122), channel_id=1, source_target_pairs={{0,7},{1,0},{2,1},{3,2},{4,3},{5,4},{6,5},{7,6},{8,15},{9,8},{10,9... | collective-permute-start | bytes 3096584 | tf_op jit(solution)/shard_map/ppermute | solution.py:344
  242.1 23.2 %collective-permute-start = (bf16[2,7,3,48,256]{4,3,2,1,0:T(8,128)(2,1)}, bf16[2,7,3,48,256]{4,3,2,1,0:T(8,128)(2,1)S(1)}, u32[]{:S(2)}, u32[]{:S(2)}) collective-permute-start(bf16[2,7,3,48,256]{4,3,2,1,0:T(8,128)(2,1)} %bitcast.120), channel_id=1, source_target_pairs={{0,1},{1,2},{2,3},{3,4},{4,5},{5,6},{6,7},{7,0},{8,9},{9,10},{10,1... | collective-permute-start | bytes 3096584 | tf_op jit(solution)/shard_map/ppermute | solution.py:343
  264.0 47.3 %copy-start.4 = (bf16[2,7,3,48,256]{4,3,2,1,0:T(8,128)(2,1)}, bf16[2,7,3,48,256]{4,3,2,1,0:T(8,128)(2,1)S(1)}, u32[]{:S(2)}) copy-start(bf16[2,7,3,48,256]{4,3,2,1,0:T(8,128)(2,1)S(1)} %collective-permute-done.7.p1) | copy-start | bytes 3096580
  264.0 23.0 %collective-permute-start.8 = (bf16[2,7,3,48,256]{4,3,2,1,0:T(8,128)(2,1)S(1)}, bf16[2,7,3,48,256]{4,3,2,1,0:T(8,128)(2,1)S(1)}, u32[]{:S(2)}, u32[]{:S(2)}) collective-permute-start(bf16[2,7,3,48,256]{4,3,2,1,0:T(8,128)(2,1)S(1)} %collective-permute-done.7.p1), channel_id=1, source_target_pairs={{0,7},{1,0},{2,1},{3,2},{4,3},{5,4},{6,5},{7,6},{8,15},{9,8},{10,9... | collective-permute-start | bytes 3096584 | tf_op jit(solution)/shard_map/ppermute | solution.py:344
  265.3 46.6 %copy-start.5 = (bf16[2,7,3,48,256]{4,3,2,1,0:T(8,128)(2,1)}, bf16[2,7,3,48,256]{4,3,2,1,0:T(8,128)(2,1)S(1)}, u32[]{:S(2)}) copy-start(bf16[2,7,3,48,256]{4,3,2,1,0:T(8,128)(2,1)S(1)} %collective-permute-done.p0) | copy-start | bytes 3096580
  265.3 23.0 %collective-permute-start.1 = (bf16[2,7,3,48,256]{4,3,2,1,0:T(8,128)(2,1)S(1)}, bf16[2,7,3,48,256]{4,3,2,1,0:T(8,128)(2,1)S(1)}, u32[]{:S(2)}, u32[]{:S(2)}) collective-permute-start(bf16[2,7,3,48,256]{4,3,2,1,0:T(8,128)(2,1)S(1)} %collective-permute-done.p0), channel_id=1, source_target_pairs={{0,1},{1,2},{2,3},{3,4},{4,5},{5,6},{6,7},{7,0},{8,9},{9,10},{10,1... | collective-permute-start | bytes 3096584 | tf_op jit(solution)/shard_map/ppermute | solution.py:343
  287.0 22.9 %copy-start.2 = (bf16[2,7,3,48,256]{4,3,2,1,0:T(8,128)(2,1)}, bf16[2,7,3,48,256]{4,3,2,1,0:T(8,128)(2,1)S(1)}, u32[]{:S(2)}) copy-start(bf16[2,7,3,48,256]{4,3,2,1,0:T(8,128)(2,1)S(1)} %collective-permute-done.8.p1) | copy-start | bytes 3096580
  287.0 22.9 %collective-permute-start.9 = (bf16[2,7,3,48,256]{4,3,2,1,0:T(8,128)(2,1)S(1)}, bf16[2,7,3,48,256]{4,3,2,1,0:T(8,128)(2,1)S(1)}, u32[]{:S(2)}, u32[]{:S(2)}) collective-permute-start(bf16[2,7,3,48,256]{4,3,2,1,0:T(8,128)(2,1)S(1)} %collective-permute-done.8.p1), channel_id=1, source_target_pairs={{0,7},{1,0},{2,1},{3,2},{4,3},{5,4},{6,5},{7,6},{8,15},{9,8},{10,9... | collective-permute-start | bytes 3096584 | tf_op jit(solution)/shard_map/ppermute | solution.py:344
  288.3 23.0 %copy-start.3 = (bf16[2,7,3,48,256]{4,3,2,1,0:T(8,128)(2,1)}, bf16[2,7,3,48,256]{4,3,2,1,0:T(8,128)(2,1)S(1)}, u32[]{:S(2)}) copy-start(bf16[2,7,3,48,256]{4,3,2,1,0:T(8,128)(2,1)S(1)} %collective-permute-done.1.p0) | copy-start | bytes 3096580
  288.3 23.0 %collective-permute-start.2 = (bf16[2,7,3,48,256]{4,3,2,1,0:T(8,128)(2,1)S(1)}, bf16[2,7,3,48,256]{4,3,2,1,0:T(8,128)(2,1)}, u32[]{:S(2)}, u32[]{:S(2)}) collective-permute-start(bf16[2,7,3,48,256]{4,3,2,1,0:T(8,128)(2,1)S(1)} %collective-permute-done.1.p0), channel_id=1, source_target_pairs={{0,1},{1,2},{2,3},{3,4},{4,5},{5,6},{6,7},{7,0},{8,9},{9,10},{10,1... | collective-permute-start | bytes 3096584 | tf_op jit(solution)/shard_map/ppermute | solution.py:343
  309.8 31.9 %copy-start.1 = (bf16[2,7,3,48,256]{4,3,2,1,0:T(8,128)(2,1)}, bf16[2,7,3,48,256]{4,3,2,1,0:T(8,128)(2,1)S(1)}, u32[]{:S(2)}) copy-start(bf16[2,7,3,48,256]{4,3,2,1,0:T(8,128)(2,1)S(1)} %collective-permute-done.9.p1) | copy-start | bytes 3096580
  309.8 31.9 %collective-permute-start.10 = (bf16[2,7,3,48,256]{4,3,2,1,0:T(8,128)(2,1)S(1)}, bf16[2,7,3,48,256]{4,3,2,1,0:T(8,128)(2,1)S(1)}, u32[]{:S(2)}, u32[]{:S(2)}) collective-permute-start(bf16[2,7,3,48,256]{4,3,2,1,0:T(8,128)(2,1)S(1)} %collective-permute-done.9.p1), channel_id=1, source_target_pairs={{0,7},{1,0},{2,1},{3,2},{4,3},{5,4},{6,5},{7,6},{8,15},{9,8},{10,9... | collective-permute-start | bytes 3096584 | tf_op jit(solution)/shard_map/ppermute | solution.py:344
  311.3 32.5 %collective-permute-start.3 = (bf16[2,7,3,48,256]{4,3,2,1,0:T(8,128)(2,1)}, bf16[2,7,3,48,256]{4,3,2,1,0:T(8,128)(2,1)}, u32[]{:S(2)}, u32[]{:S(2)}) collective-permute-start(bf16[2,7,3,48,256]{4,3,2,1,0:T(8,128)(2,1)} %collective-permute-done.2.p0), channel_id=1, source_target_pairs={{0,1},{1,2},{2,3},{3,4},{4,5},{5,6},{6,7},{7,0},{8,9},{9,10},{10,1... | collective-permute-start | bytes 3096584 | tf_op jit(solution)/shard_map/ppermute | solution.py:343
  341.8 16.0 %copy-start = (bf16[2,7,3,48,256]{4,3,2,1,0:T(8,128)(2,1)}, bf16[2,7,3,48,256]{4,3,2,1,0:T(8,128)(2,1)S(1)}, u32[]{:S(2)}) copy-start(bf16[2,7,3,48,256]{4,3,2,1,0:T(8,128)(2,1)S(1)} %collective-permute-done.10.p1) | copy-start | bytes 3096580
  341.8 22.9 %collective-permute-start.11 = (bf16[2,7,3,48,256]{4,3,2,1,0:T(8,128)(2,1)S(1)}, bf16[2,7,3,48,256]{4,3,2,1,0:T(8,128)(2,1)}, u32[]{:S(2)}, u32[]{:S(2)}) collective-permute-start(bf16[2,7,3,48,256]{4,3,2,1,0:T(8,128)(2,1)S(1)} %collective-permute-done.10.p1), channel_id=1, source_target_pairs={{0,7},{1,0},{2,1},{3,2},{4,3},{5,4},{6,5},{7,6},{8,15},{9,8},{10,9... | collective-permute-start | bytes 3096584 | tf_op jit(solution)/shard_map/ppermute | solution.py:344
  343.7 22.0 %collective-permute-start.4 = (bf16[2,7,3,48,256]{4,3,2,1,0:T(8,128)(2,1)}, bf16[2,7,3,48,256]{4,3,2,1,0:T(8,128)(2,1)}, u32[]{:S(2)}, u32[]{:S(2)}) collective-permute-start(bf16[2,7,3,48,256]{4,3,2,1,0:T(8,128)(2,1)} %collective-permute-done.3.p0), channel_id=1, source_target_pairs={{0,1},{1,2},{2,3},{3,4},{4,5},{5,6},{6,7},{7,0},{8,9},{9,10},{10,1... | collective-permute-start | bytes 3096584 | tf_op jit(solution)/shard_map/ppermute | solution.py:343
  364.6 32.0 %collective-permute-start.12 = (bf16[2,7,3,48,256]{4,3,2,1,0:T(8,128)(2,1)}, bf16[2,7,3,48,256]{4,3,2,1,0:T(8,128)(2,1)S(1)}, u32[]{:S(2)}, u32[]{:S(2)}) collective-permute-start(bf16[2,7,3,48,256]{4,3,2,1,0:T(8,128)(2,1)} %collective-permute-done.11.p1), channel_id=1, source_target_pairs={{0,7},{1,0},{2,1},{3,2},{4,3},{5,4},{6,5},{7,6},{8,15},{9,8},{10,9... | collective-permute-start | bytes 3096584 | tf_op jit(solution)/shard_map/ppermute | solution.py:344
  365.7 33.3 %collective-permute-start.5 = (bf16[2,7,3,48,256]{4,3,2,1,0:T(8,128)(2,1)}, bf16[2,7,3,48,256]{4,3,2,1,0:T(8,128)(2,1)}, u32[]{:S(2)}, u32[]{:S(2)}) collective-permute-start(bf16[2,7,3,48,256]{4,3,2,1,0:T(8,128)(2,1)} %collective-permute-done.4.p0), channel_id=1, source_target_pairs={{0,1},{1,2},{2,3},{3,4},{4,5},{5,6},{6,7},{7,0},{8,9},{9,10},{10,1... | collective-permute-start | bytes 3096584 | tf_op jit(solution)/shard_map/ppermute | solution.py:343
  396.6 12.4 %copy-start.6 = (bf16[2,7,3,48,256]{4,3,2,1,0:T(8,128)(2,1)}, bf16[2,7,3,48,256]{4,3,2,1,0:T(8,128)(2,1)S(1)}, u32[]{:S(2)}) copy-start(bf16[2,7,3,48,256]{4,3,2,1,0:T(8,128)(2,1)S(1)} %collective-permute-done.12.p1) | copy-start | bytes 3096580
  396.6 32.4 %collective-permute-start.13 = (bf16[2,7,3,48,256]{4,3,2,1,0:T(8,128)(2,1)S(1)}, bf16[2,7,3,48,256]{4,3,2,1,0:T(8,128)(2,1)}, u32[]{:S(2)}, u32[]{:S(2)}) collective-permute-start(bf16[2,7,3,48,256]{4,3,2,1,0:T(8,128)(2,1)S(1)} %collective-permute-done.12.p1), channel_id=1, source_target_pairs={{0,7},{1,0},{2,1},{3,2},{4,3},{5,4},{6,5},{7,6},{8,15},{9,8},{10,9... | collective-permute-start | bytes 3096584 | tf_op jit(solution)/shard_map/ppermute | solution.py:344
  399.0 30.0 %collective-permute-start.6 = (bf16[2,7,3,48,256]{4,3,2,1,0:T(8,128)(2,1)}, bf16[2,7,3,48,256]{4,3,2,1,0:T(8,128)(2,1)}, u32[]{:S(2)}, u32[]{:S(2)}) collective-permute-start(bf16[2,7,3,48,256]{4,3,2,1,0:T(8,128)(2,1)} %collective-permute-done.5.p0), channel_id=1, source_target_pairs={{0,1},{1,2},{2,3},{3,4},{4,5},{5,6},{6,7},{7,0},{8,9},{9,10},{10,1... | collective-permute-start | bytes 3096584 | tf_op jit(solution)/shard_map/ppermute | solution.py:343

commit v2 on v1

v2 whole, which is shorter than its diff:
```python
import functools

import jax
import jax.numpy as jnp
from jax import lax
from jax.experimental import pallas as pl
from jax.experimental.pallas import tpu as pltpu
from jax.sharding import PartitionSpec as P


BW = 256
RB = 3
f32, bf16 = jnp.float32, jnp.bfloat16
NT = (((1,), (1,)), ((), ()))
TN = (((0,), (0,)), ((), ()))


def mm(a, b, dims=(((1,), (0,)), ((), ()))):
    return lax.dot_general(a, b, dims, preferred_element_type=f32)


def rms_scale(wide):
    return lax.rsqrt(jnp.mean(wide * wide, -1, keepdims=True) + 1e-6)


def sigmoid(x):
    return 0.5 * jnp.tanh(0.5 * x) + 0.5


def kernel(cfg, x_in, dy_in, wg_in, wu_in, wd_in, own00, own01, own10, own11, ss, S, xh, a, aT, dh, hid, wg, wu, wd, recv,
           load_sem, x_sem, own_sem, send_sem, recv_sem, credit):
    n, T, D, F, tt, tb, comm = cfg["n"], cfg["T"], cfg["D"], cfg["F"], cfg["tt"], cfg["tb"], cfg["comm"]
    NB = F // BW
    NBLK = 2 * NB
    H = D // (2 * n)
    CH = 3 * H
    BR = 3 * D
    GB = NB * BR
    hr = BW // (2 * n)
    ncg = D // BW
    ramp = max(NBLK - 4, 1)
    start = lambda b: jnp.where(b <= ramp, 2 * b, b + ramp)
    LAST = NBLK - 1 + ramp + n - 2
    me = lax.axis_index("dp")
    right, left = lax.rem(me + 1, n), lax.rem(me + n - 1, n)

    loads = [pltpu.make_async_copy(s, d, load_sem.at[i]) for i, (s, d) in enumerate((
        (x_in, xh), (wg_in.at[0], wg.at[0]), (wu_in.at[0], wu.at[0]), (wd_in.at[0], wd.at[0]), (dy_in, dh),
        (wg_in.at[1], wg.at[1]), (wu_in.at[1], wu.at[1]), (wd_in.at[1], wd.at[1])))]
    for c in loads[:3]:
        c.start()
    if comm:
        barrier = pltpu.get_barrier_semaphore()
        for nb in (left, right):
            pl.semaphore_signal(barrier, inc=1, device_id={"dp": nb}, device_id_type=pl.DeviceIdType.MESH)
    ss[...] = jnp.zeros_like(ss)

    def chunk_row(b, c, d):
        return pl.multiple_of(b * BR + (2 * c + d) * CH, 16)

    def chunk_of(s, d):
        return lax.rem(me + 2 * n - 1 - s, n) if d == 0 else lax.rem(me + 1 + s, n)

    def block_of(r, s):
        z = r - s
        b = jnp.where(z < 2 * ramp, lax.div(z, 2), z - ramp)
        return b, (z >= 0) & ((z >= 2 * ramp) | (lax.rem(z, 2) == 0)) & (b < NBLK)

    def hop(r, s, d):
        b, _ = block_of(r, s)
        slot = lax.rem(r, RB) * (n - 1) + s
        return pltpu.make_async_remote_copy(
            src_ref=S.at[pl.ds(chunk_row(b, chunk_of(s, d), d), CH), :], dst_ref=recv.at[d, slot],
            send_sem=send_sem.at[d, slot], recv_sem=recv_sem.at[d, slot],
            device_id={"dp": right if d == 0 else left}, device_id_type=pl.DeviceIdType.MESH)

    def arrival(d, slot):
        return pltpu.make_async_remote_copy(
            src_ref=recv.at[d, slot], dst_ref=recv.at[d, slot], send_sem=send_sem.at[d, slot], recv_sem=recv_sem.at[d, slot],
            device_id={"dp": right if d == 0 else left}, device_id_type=pl.DeviceIdType.MESH)

    def op(q, _):
        r, s = lax.div(q, n), lax.rem(q, n)
        b, live = block_of(r, s)
        @pl.when((s == 0) & (r >= RB) & (r <= LAST))
        def _():
            pl.semaphore_wait(credit.at[0], 1)
            pl.semaphore_wait(credit.at[1], 1)
        @pl.when(live & (s >= 1))
        def _():
            slot = lax.rem(r + RB - 1, RB) * (n - 1) + s - 1
            for d in range(2):
                arrival(d, slot).wait_recv()
                rows = pl.ds(chunk_row(b, chunk_of(s, d), d), CH)
                total = (S[rows, :].astype(f32) + recv[d, slot].astype(f32)).astype(bf16)
                S[rows, :] = total
                @pl.when(s == n - 1)
                def _():
                    t = total.astype(f32)
                    t = t * t
                    ss[...] += functools.reduce(jnp.add, [t[i * 8:(i + 1) * 8, h * 128:(h + 1) * 128] for i in range(CH // 8) for h in range(BW // 128)])
        @pl.when(live & (s == n - 1))
        def _():
            for d in range(2):
                rows = pl.ds(chunk_row(b, me, d), CH)
                @pl.when(b < NB)
                def _():
                    pltpu.make_async_copy(S.at[rows, :], (own00, own01)[d].at[b], own_sem.at[d, b]).start()
                @pl.when(b >= NB)
                def _():
                    pltpu.make_async_copy(S.at[rows, :], (own10, own11)[d].at[b - NB], own_sem.at[d, b]).start()
        _, before = block_of(r - RB, s)
        @pl.when((s <= n - 2) & (r >= RB) & before)
        def _():
            for d in range(2):
                hop(r - RB, s, d).wait_send()
        @pl.when(live & (s <= n - 2))
        def _():
            for d in range(2):
                hop(r, s, d).start()
        @pl.when((s == n - 1) & (r >= 1) & (r <= LAST - RB + 1))
        def _():
            pl.semaphore_signal(credit.at[0], inc=1, device_id={"dp": left}, device_id_type=pl.DeviceIdType.MESH)
            pl.semaphore_signal(credit.at[1], inc=1, device_id={"dp": right}, device_id_type=pl.DeviceIdType.MESH)
        return 0

    def ops(q, count, ready):
        if not comm:
            return q
        limit = n * start(ready)
        end = jnp.where(q + count < limit, q + count, limit)
        lax.fori_loop(q, end, op, 0)
        return end

    loads[0].wait()
    loads[3].start()
    loads[1].wait()
    loads[2].wait()
    def fwd(t, _):
        rows = pl.ds(pl.multiple_of(t * tt, tt), tt)
        xw = xh[rows, :].astype(f32)
        at = (xw * rms_scale(xw)).astype(bf16)
        for j in range(NB):
            cols = slice(j * BW, (j + 1) * BW)
            g = mm(at, wg[0, :, cols])
            u = mm(at, wu[0, :, cols])
            S[pl.ds(pl.multiple_of(GB + j * T + t * tt, 16), tt), :] = (g * sigmoid(g) * u).astype(bf16)
        return 0
    lax.fori_loop(0, T // tt, fwd, 0)
    loads[3].wait()
    for c in loads[4:]:
        c.start()
    def fwd_down(t, _):
        rows = pl.ds(pl.multiple_of(t * tt, tt), tt)
        hidden = jnp.concatenate([S[pl.ds(pl.multiple_of(GB + j * T + t * tt, 16), tt), :] for j in range(NB)], axis=1)
        h = (xh[rows, :].astype(f32) + mm(hidden, wd[0]).astype(bf16).astype(f32)).astype(bf16)
        xh[rows, :] = h
        hw = h.astype(f32)
        a1 = (hw * rms_scale(hw)).astype(bf16)
        a[rows, :] = a1
        aT[:, rows] = a1.T
        return 0
    lax.fori_loop(0, T // tt, fwd_down, 0)

    def block(l, j, dg0, du0, b, q, pace):
        cols = pl.ds(pl.multiple_of(j * BW, BW), BW)
        q = ops(q, pace, b)
        def tokens(t, q):
            rows = pl.ds(pl.multiple_of(t * tb, tb), tb)
            at = a[rows, :]
            g = mm(at, wg[l, :, cols])
            u = mm(at, wu[l, :, cols])
            dhid = mm(dh[rows, :], wd[l, cols, :], NT).astype(bf16).astype(f32)
            sg = sigmoid(g)
            s = g * sg
            hid[rows, :] = (s * u).astype(bf16)
            S[pl.ds(pl.multiple_of(du0 + t * tb, 16), tb), :] = (dhid * s).astype(bf16)
            S[pl.ds(pl.multiple_of(dg0 + t * tb, 16), tb), :] = (dhid * u * (sg + s * (1.0 - sg))).astype(bf16)
            return q
        q = lax.fori_loop(0, T // tb, tokens, q, unroll=True)
        base = b * BR
        def gate_up(w, k):
            for e in range(2 * n):
                S[pl.ds(pl.multiple_of(base + e * CH + k * H, 16), H), :] = w[e * H:(e + 1) * H]
        def down(w):
            for e in range(2 * n):
                for cg in range(ncg):
                    S[pl.ds(pl.multiple_of(base + e * CH + 2 * H + cg * hr, 16), hr), :] = w[e * hr:(e + 1) * hr, cg * BW:(cg + 1) * BW]
        dgv = lambda: S[pl.ds(pl.multiple_of(dg0, 16), T), :]
        duv = lambda: S[pl.ds(pl.multiple_of(du0, 16), T), :]
        q = ops(q, pace, b)
        w = mm(aT[...], jnp.concatenate([dgv(), duv()], axis=1)).astype(bf16)
        gate_up(w[:, :BW], 0)
        gate_up(w[:, BW:], 1)
        down(mm(hid[...], dh[...], TN).astype(bf16))
        return q

    for c in loads[4:]:
        c.wait()
    def last_layer(j, q):
        return block(1, j, GB + j * 2 * T, GB + j * 2 * T + T, j, q, jnp.where(j <= 2, n, cfg["pace"][0]))
    if comm:
        pl.semaphore_wait(barrier, 2)
    q = lax.fori_loop(0, NB, last_layer, 0)

    def d_input(t, q):
        q = ops(q, cfg["pace"][1], NB)
        rows = pl.ds(pl.multiple_of(t * tt, tt), tt)
        dg = jnp.concatenate([S[pl.ds(pl.multiple_of(GB + j * 2 * T + t * tt, 16), tt), :] for j in range(NB)], axis=1)
        du = jnp.concatenate([S[pl.ds(pl.multiple_of(GB + j * 2 * T + T + t * tt, 16), tt), :] for j in range(NB)], axis=1)
        da = (mm(dg, wg[1], NT).astype(bf16).astype(f32) + mm(du, wu[1], NT).astype(bf16).astype(f32)).astype(bf16).astype(f32)
        wide = xh[rows, :].astype(f32)
        scale = rms_scale(wide)
        dot = jnp.sum(da * wide, -1, keepdims=True)
        dw = da * scale - wide * (scale * scale * scale * dot * (1.0 / D))
        dh[rows, :] = (dh[rows, :].astype(f32) + dw.astype(bf16).astype(f32)).astype(bf16)
        pltpu.make_async_copy(x_in.at[rows, :], xh.at[rows, :], x_sem).start()
        return q
    q = lax.fori_loop(0, T // tt, d_input, q)
    def renorm(t, q):
        rows = pl.ds(pl.multiple_of(t * tt, tt), tt)
        wide = xh[rows, :].astype(f32)
        a0 = (wide * rms_scale(wide)).astype(bf16)
        a[rows, :] = a0
        aT[:, rows] = a0.T
        return q
    pltpu.make_async_copy(x_in, xh, x_sem).wait()
    q = ops(q, 2, NB)
    lax.fori_loop(0, T // tt, renorm, 0)

    def first_layer(j, q):
        return block(0, j, 2 * GB, 2 * GB + T, NB + j, q, cfg["pace"][2])
    q = lax.fori_loop(0, NB, first_layer, q)
    if comm:
        lax.fori_loop(q, (LAST + 2) * n, op, 0)
        for r in range(LAST - RB + 2, LAST + 1):
            for s in range(n - 1):
                z = r - s
                b = z // 2 if z < 2 * ramp else z - ramp
                if z >= 0 and (z >= 2 * ramp or z % 2 == 0) and b < NBLK:
                    for d in range(2):
                        hop(r, s, d).wait_send()
        for d in range(2):
            for b in range(NBLK):
                pltpu.make_async_copy(S.at[pl.ds(0, CH), :], (own00, own01, own10, own11)[2 * (b // NB) + d].at[b % NB], own_sem.at[d, b]).wait()
    else:
        cps = [pltpu.make_async_copy(S.at[pl.ds(b * BR + d * CH, CH), :], (own00, own01, own10, own11)[2 * (b // NB) + d].at[b % NB], own_sem.at[d, b]) for d in range(2) for b in range(NBLK)]
        for c in cps: c.start()
        for c in cps: c.wait()


def k1(x, dy, wg, wu, wd, n, tt=512, tb=512, comm=True, cid=0, pace=(6, 7, 6)):
    T, D = x.shape
    F = wg.shape[2]
    NB = F // BW
    NBLK = 2 * NB
    H = D // (2 * n); CH = 3 * H
    GB = NB * 3 * D
    cfg = dict(n=n, T=T, D=D, F=F, tt=min(tt, T), tb=min(tb, T), comm=comm, pace=pace)
    any_ = pl.BlockSpec(memory_space=pl.ANY)
    flops = 18 * 2 * T * D * F
    return pl.pallas_call(
        functools.partial(kernel, cfg),
        out_shape=(jax.ShapeDtypeStruct((NB, CH, BW), bf16),) * 4 + (jax.ShapeDtypeStruct((8, 128), f32),),
        in_specs=[any_] * 5,
        out_specs=(any_,) * 4 + (pl.BlockSpec(memory_space=pltpu.VMEM),),
        scratch_shapes=[
            pltpu.VMEM((max(GB + NB * 2 * T, 2 * GB + 2 * T), BW), bf16),
            pltpu.VMEM((T, D), bf16), pltpu.VMEM((T, D), bf16), pltpu.VMEM((D, T), bf16), pltpu.VMEM((T, D), bf16),
            pltpu.VMEM((T, BW), bf16),
            pltpu.VMEM((2, D, F), bf16), pltpu.VMEM((2, D, F), bf16), pltpu.VMEM((2, F, D), bf16),
            pltpu.VMEM((2, RB * (n - 1), CH, BW), bf16),
            pltpu.SemaphoreType.DMA((8,)), pltpu.SemaphoreType.DMA, pltpu.SemaphoreType.DMA((2, NBLK)),
            pltpu.SemaphoreType.DMA((2, RB * (n - 1))), pltpu.SemaphoreType.DMA((2, RB * (n - 1))), pltpu.SemaphoreType.REGULAR((2,)),
        ],
        compiler_params=pltpu.CompilerParams(vmem_limit_bytes=67043328, collective_id=cid if comm else None, has_side_effects=True),
        cost_estimate=pl.CostEstimate(flops=flops, bytes_accessed=40 * 10**6, transcendentals=0),
        name="grads")(x, dy, wg, wu, wd)


def factor_kernel(n, count, sq, out, slots, send_sem, recv_sem):
    me = lax.axis_index("dp")
    barrier = pltpu.get_barrier_semaphore()
    peers = [lax.rem(me + p, n) for p in range(1, n)]
    for q in peers:
        pl.semaphore_signal(barrier, inc=1, device_id={"dp": q}, device_id_type=pl.DeviceIdType.MESH)
    slots[me] = sq[...]
    pl.semaphore_wait(barrier, n - 1)
    copies = [
        pltpu.make_async_remote_copy(
            src_ref=sq, dst_ref=slots.at[me], send_sem=send_sem.at[i], recv_sem=recv_sem.at[me],
            device_id={"dp": q}, device_id_type=pl.DeviceIdType.MESH)
        for i, q in enumerate(peers)]
    for c in copies:
        c.start()
    for i, q in enumerate(peers):
        pltpu.make_async_remote_copy(
            src_ref=sq, dst_ref=slots.at[q], send_sem=send_sem.at[i], recv_sem=recv_sem.at[q],
            device_id={"dp": q}, device_id_type=pl.DeviceIdType.MESH).wait_recv()
    total = slots[0]
    for i in range(1, n):
        total = total + slots[i]
    total = jnp.sum(jnp.sum(total, axis=0, keepdims=True), axis=1, keepdims=True)
    out[...] = jnp.broadcast_to(jnp.minimum(1.0, 0.5 * lax.rsqrt(total / count + 1e-30)), out.shape)
    for c in copies:
        c.wait_send()


def clip_factor(squares, count, n):
    vmem = pl.BlockSpec(memory_space=pltpu.VMEM)
    return pl.pallas_call(
        functools.partial(factor_kernel, n, float(count)),
        out_shape=jax.ShapeDtypeStruct(squares.shape, f32),
        in_specs=[vmem],
        out_specs=vmem,
        scratch_shapes=[pltpu.VMEM((n,) + squares.shape, f32), pltpu.SemaphoreType.DMA((n - 1,)), pltpu.SemaphoreType.DMA((n,))],
        compiler_params=pltpu.CompilerParams(collective_id=1, has_side_effects=True, vmem_limit_bytes=2**20),
        cost_estimate=pl.CostEstimate(flops=10**9, bytes_accessed=10**5, transcendentals=0),
        name="factor")(squares)


def adam_math(w, m, v, g):
    m = 0.9 * m + 0.1 * g
    v = 0.95 * v + 0.05 * g * g
    step = m * lax.rsqrt(v + 1e-8) + 0.1 * w
    return (w - 0.02 * step).astype(bf16), m, v


def adam_kernel(pieces, idx_ref, fac_ref, *refs):
    pays, ins, outs = refs[: len(pieces)], refs[len(pieces) : len(pieces) + 9], refs[-9:]
    factor = fac_ref[0:1, 0:1]
    def one(p):
        def step(k, at, g):
            new = adam_math(ins[k][at].astype(f32), ins[3 + k][at], ins[6 + k][at], g.astype(f32) * factor)
            for i in range(3):
                outs[3 * i + k][at] = new[i]
        hr = ins[2].shape[3]
        def block(j, _):
            cols = pl.ds(pl.multiple_of(j * BW, BW), BW)
            step(0, (0, 0, slice(None), cols), p[j, 0])
            step(1, (0, 0, slice(None), cols), p[j, 1])
            for cg in range(ins[2].shape[4] // BW):
                step(2, (0, j, 0, slice(None), slice(cg * BW, (cg + 1) * BW)), p[j, 2, cg * hr : (cg + 1) * hr])
            return 0
        lax.fori_loop(0, p.shape[0], block, 0)
    if len(pieces) == 1:
        one(pays[0])
    else:
        for i in range(len(pieces)):
            pl.when(pl.program_id(0) == i)(functools.partial(one, pays[i]))


def pick(values, i):
    out = values[0]
    for k in range(1, len(values)):
        out = jnp.where(i == k, values[k], out)
    return out


def adam_call(idx, factor, pieces, pays, ins, prev):
    nb = pays[0].shape[0]
    layer = lambda i: pick([l for l, _ in pieces], i)
    chunk = lambda i, idx: pick([idx[d] for _, d in pieces], i)
    rows = pl.BlockSpec((1, 1) + ins[0].shape[2:], lambda i, idx: (layer(i), chunk(i, idx), 0, 0))
    down = pl.BlockSpec((1, nb, 1) + ins[2].shape[3:], lambda i, idx: (layer(i), 0, chunk(i, idx), 0, 0))
    pay = pl.BlockSpec(pays[0].shape, lambda i, idx: (0, 0, 0, 0), pipeline_mode=pl.Buffered(1))
    specs = [rows, rows, down] * 3
    any_ = [] if prev is None else [pl.BlockSpec(memory_space=pl.ANY)] * 9
    k = len(pieces)
    size = k * pays[0].size
    return pl.pallas_call(
        functools.partial(adam_kernel, tuple(pieces)),
        grid_spec=pltpu.PrefetchScalarGridSpec(
            num_scalar_prefetch=1, grid=(k,), in_specs=[pl.BlockSpec((8, 128), lambda i, idx: (0, 0))] + [pay] * k + specs + any_, out_specs=specs),
        out_shape=[jax.ShapeDtypeStruct(x.shape, x.dtype) for x in ins],
        input_output_aliases={} if prev is None else {2 + k + 9 + i: i for i in range(9)},
        compiler_params=pltpu.CompilerParams(vmem_limit_bytes=62 * 2**20, dimension_semantics=("arbitrary",)),
        cost_estimate=pl.CostEstimate(flops=4 * 10**9 * k // 4, bytes_accessed=22 * size, transcendentals=size),
        name="adamw")(idx, factor, *pays, *ins, *([] if prev is None else prev))


def views(arrays, n):
    out = []
    for i, a in enumerate(arrays):
        L, r, c = a.shape
        out.append(a.reshape(L, 2 * n, r // (2 * n), c) if i % 3 < 2 else a.reshape(L, r // BW, 2 * n, BW // (2 * n), c))
    return out


def solution(mesh):
    n = mesh.shape["dp"]
    to = ([(i, (i + 1) % n) for i in range(n)], [(i, (i - 1) % n) for i in range(n)])

    def step(x, dy, *arrays):
        me = lax.axis_index("dp")
        own00, own01, own10, own11, squares = k1(x[0], dy[0], *arrays[:3], n)
        _, _, F = arrays[0].shape
        ins = views(arrays, n)
        count = sum(w.size for w in arrays[:3])
        pieces = [(1, 0), (1, 1), (0, 0), (0, 1)]
        pays = [o.reshape(F // BW, 3, o.shape[1] // 3, BW) for o in (own00, own01, own10, own11)]
        factor, outs = None, None
        for s in range(n):
            coming = []
            if s < n - 1:
                for i, (l, d) in enumerate(pieces):
                    coming.append(lax.ppermute(pays[i], "dp", to[d]))
            if factor is None:
                factor = clip_factor(squares, count, n)
            c0, c1 = lax.rem(me - s + n, n), lax.rem(me + s, n)
            idx = jnp.stack([2 * c0, 2 * c1 + 1]).astype(jnp.int32)
            if s < n - 1:
                outs = adam_call(idx, factor, pieces, pays, ins, outs)
            else:
                outs = adam_call(idx, factor, pieces[:2], pays[:2], ins, outs)
                outs = adam_call(idx, factor, pieces[2:], pays[2:], ins, outs)
            pays = coming
        return tuple(o.reshape(w.shape) for o, w in zip(outs, arrays))

    step = jax.shard_map(
        step,
        mesh=mesh,
        in_specs=(P(("rep", "dp"), None, None),) * 2 + (P(None, None, None),) * 9,
        out_specs=(P("rep", None, None),) * 9,
        check_vma=False,
    )
    return step
```

time: 440 us -> 396 us (0.900)
  waiting for transfers between devices: 70.1 us -> 30.2 us
  starting transfers between devices: 14.6 us -> 41.4 us
  blocking collectives: 26.6 us -> 0 us
    ppermute x14 -> x28, waiting for transfers between devices: 70.1 us -> 30.2 us  [step(): coming.append(lax.ppermute(pays[i], 'dp', to[d]))]
    pallas_call x1, Pallas kernels: 240 us -> 211 us  [k1(): pl.pallas_call(functools.partial(kernel, cfg), out_shape=(jax.ShapeDtypeS...]
    ppermute x14 -> x28, starting transfers between devices: 14.6 us -> 41.4 us  [step(): coming.append(lax.ppermute(pays[i], 'dp', to[d]))]
    psum x1 -> x0, blocking collectives: 26.6 us -> none  [step(): total = lax.psum(jnp.sum(squares), 'dp')]
    pallas_call x8 -> x10, Pallas kernels: 79.9 us -> 105 us  [the longest x9 91.8 us: adam_call(): pl.pallas_call(functools.partial(adam_kernel, tuple(pieces)), grid_spec=p...]
  transfers between devices with their start and end apart: 14 -> 28, of which waited for: 5 -> 4; matrix products, arithmetic and copies ran while one was open for 1% -> 1% of each run, Pallas kernels for 16% -> 25%
where the time goes in v2:
time: 396 us; the launch traced here: 395 us
  Pallas kernels  316 us (80%)
  starting transfers between devices  41.4 us (10%)
  waiting for transfers between devices  30.2 us (8%)
  other arithmetic  4.65 us (1%)
    pallas_call x1, Pallas kernels, k1(): pl.pallas_call(functools.partial(kernel, cfg), out_shape=(jax.ShapeDtypeS...  211 us
    pallas_call x9, Pallas kernels, adam_call(): pl.pallas_call(functools.partial(adam_kernel, tuple(pieces)), grid_spec=p...  91.8 us
    ppermute x28, starting transfers between devices, step(): coming.append(lax.ppermute(pays[i], 'dp', to[d]))  41.4 us
    ppermute x28, waiting for transfers between devices, step(): coming.append(lax.ppermute(pays[i], 'dp', to[d]))  30.2 us
    pallas_call x1, Pallas kernels, clip_factor(): pl.pallas_call(functools.partial(factor_kernel, n, float(count)), out_sha...  13.4 us
  transfers between devices with their start and end apart: 28, of which 4 were waited for; matrix products, arithmetic and copies ran while one was open for 1% of the time, Pallas kernels for 25%

profile of v2, /device:TPU:22, one launch (start us, length us, event | category | flops | bytes accessed | tf_op | source)
XLA Modules:
  0.0 395.5 jit_solution(10860236093345058974)
XLA Ops:
  0.6 210.7 %grads.1 = (bf16[7,144,256]{2,1,0:T(8,128)(2,1)}, bf16[7,144,256]{2,1,0:T(8,128)(2,1)}, bf16[7,144,256]{2,1,0:T(8,128)(2,1)}, bf16[7,144,256]{2,1,0:T(8,128)(2,1)}, f32[8,128]{1,0:T(8,128)}) custom-call(bf16[2048,768]{1,0:T(8,128)(2,1)} %bitcast.138, bf16[2048,768]{1,0:T(8,128)(2,1)} %bitcast.139, bf16[2,768,1792]{2,1,0:T(8,128)(2,1)} %wg_in.1, ...), custom_call_target="tpu_custom_call" | custom-call | flops 101468602368 | bytes 40000000 | tf_op jit(solution)/shard_map/grads/pallas_call | solution.py:262
  211.9 2.8 collective-permute-start.21
  214.7 3.2 collective-permute-start.7
  217.9 9.6 %collective-permute-done.14.refs_0_ = bf16[7,3,48,256]{3,2,1,0:T(8,128)(2,1)S(1)} collective-permute-done((bf16[7,3,48,256]{3,2,1,0:T(8,128)(2,1)}, bf16[7,3,48,256]{3,2,1,0:T(8,128)(2,1)S(1)}, u32[]{:S(2)}, u32[]{:S(2)}) %collective-permute-start.14) | collective-permute-done | bytes 516128 | tf_op jit(solution)/shard_map/ppermute | solution.py:407
  227.5 3.2 collective-permute-start.22
  230.7 7.8 %collective-permute-done.refs_2_ = bf16[7,3,48,256]{3,2,1,0:T(8,128)(2,1)S(1)} collective-permute-done((bf16[7,3,48,256]{3,2,1,0:T(8,128)(2,1)}, bf16[7,3,48,256]{3,2,1,0:T(8,128)(2,1)S(1)}, u32[]{:S(2)}, u32[]{:S(2)}) %collective-permute-start) | collective-permute-done | bytes 516128 | tf_op jit(solution)/shard_map/ppermute | solution.py:407
  238.6 3.3 collective-permute-start.8
  243.1 6.6 %collective-permute-done.15.refs_0_ = bf16[7,3,48,256]{3,2,1,0:T(8,128)(2,1)S(1)} collective-permute-done((bf16[7,3,48,256]{3,2,1,0:T(8,128)(2,1)S(1)}, bf16[7,3,48,256]{3,2,1,0:T(8,128)(2,1)S(1)}, u32[]{:S(2)}, u32[]{:S(2)}) %collective-permute-start.15) | collective-permute-done | bytes 516128 | tf_op jit(solution)/shard_map/ppermute | solution.py:407
  249.6 3.2 collective-permute-start.23
  254.6 6.2 %collective-permute-done.1.refs_2_ = bf16[7,3,48,256]{3,2,1,0:T(8,128)(2,1)} collective-permute-done((bf16[7,3,48,256]{3,2,1,0:T(8,128)(2,1)S(1)}, bf16[7,3,48,256]{3,2,1,0:T(8,128)(2,1)}, u32[]{:S(2)}, u32[]{:S(2)}) %collective-permute-start.1) | collective-permute-done | bytes 516128 | tf_op jit(solution)/shard_map/ppermute | solution.py:407
  260.8 3.2 collective-permute-start.9
  264.7 13.4 %factor.1.fac_ref = f32[8,128]{1,0:T(8,128)S(1)} custom-call(f32[8,128]{1,0:T(8,128)S(1)} %copy-done.1), custom_call_target="tpu_custom_call" | custom-call | flops 1000000000 | bytes 100000 | tf_op jit(solution)/shard_map/factor/pallas_call | solution.py:311
  282.6 11.3 %adamw.9 = (bf16[2,16,48,1792]{3,2,1,0:T(8,128)(2,1)}, bf16[2,16,48,1792]{3,2,1,0:T(8,128)(2,1)}, bf16[2,7,16,16,768]{4,3,2,1,0:T(8,128)(2,1)}, f32[2,16,48,1792...) custom-call(s32[2]{0:T(128)} %pad_add_fusion.7.idx_ref, ...), custom_call_target="tpu_custom_call" | custom-call | flops 4000000000 | bytes 22708224 | tf_op jit(solution)/shard_map/adamw/pallas_call | solution.py:371
  297.5 3.1 collective-permute-start.25
  300.6 11.3 %adamw.10 = (bf16[2,16,48,1792]{3,2,1,0:T(8,128)(2,1)}, bf16[2,16,48,1792]{3,2,1,0:T(8,128)(2,1)}, bf16[2,7,16,16,768]{4,3,2,1,0:T(8,128)(2,1)}, f32[2,16,48,179...) custom-call(s32[2]{0:T(128)} %pad_add_fusion.6.idx_ref, ...), custom_call_target="tpu_custom_call", output_to_operand_aliasing={{0}: (15, {}), {1}: (16, {}), {2}: (17, {}), {3}: (18, {}),... | custom-call | flops 4000000000 | bytes 22708224 | tf_op jit(solution)/shard_map/adamw/pallas_call | solution.py:371
  314.0 11.3 %adamw.11 = (bf16[2,16,48,1792]{3,2,1,0:T(8,128)(2,1)}, bf16[2,16,48,1792]{3,2,1,0:T(8,128)(2,1)}, bf16[2,7,16,16,768]{4,3,2,1,0:T(8,128)(2,1)}, f32[2,16,48,179...) custom-call(s32[2]{0:T(128)} %pad_add_fusion.5.idx_ref, ...), custom_call_target="tpu_custom_call", output_to_operand_aliasing={{0}: (15, {}), {1}: (16, {}), {2}: (17, {}), {3}: (18, {}),... | custom-call | flops 4000000000 | bytes 22708224 | tf_op jit(solution)/shard_map/adamw/pallas_call | solution.py:371
  325.5 3.2 collective-permute-start.26
  328.7 11.3 %adamw.12 = (bf16[2,16,48,1792]{3,2,1,0:T(8,128)(2,1)}, bf16[2,16,48,1792]{3,2,1,0:T(8,128)(2,1)}, bf16[2,7,16,16,768]{4,3,2,1,0:T(8,128)(2,1)}, f32[2,16,48,179...) custom-call(s32[2]{0:T(128)} %pad_add_fusion.4.idx_ref, ...), custom_call_target="tpu_custom_call", output_to_operand_aliasing={{0}: (15, {}), {1}: (16, {}), {2}: (17, {}), {3}: (18, {}),... | custom-call | flops 4000000000 | bytes 22708224 | tf_op jit(solution)/shard_map/adamw/pallas_call | solution.py:371
  342.1 11.3 %adamw.13 = (bf16[2,16,48,1792]{3,2,1,0:T(8,128)(2,1)}, bf16[2,16,48,1792]{3,2,1,0:T(8,128)(2,1)}, bf16[2,7,16,16,768]{4,3,2,1,0:T(8,128)(2,1)}, f32[2,16,48,179...) custom-call(s32[2]{0:T(128)} %pad_add_fusion.3.idx_ref, ...), custom_call_target="tpu_custom_call", output_to_operand_aliasing={{0}: (15, {}), {1}: (16, {}), {2}: (17, {}), {3}: (18, {}),... | custom-call | flops 4000000000 | bytes 22708224 | tf_op jit(solution)/shard_map/adamw/pallas_call | solution.py:371
  353.5 3.2 collective-permute-start.27
  356.7 11.3 %adamw.14 = (bf16[2,16,48,1792]{3,2,1,0:T(8,128)(2,1)}, bf16[2,16,48,1792]{3,2,1,0:T(8,128)(2,1)}, bf16[2,7,16,16,768]{4,3,2,1,0:T(8,128)(2,1)}, f32[2,16,48,179...) custom-call(s32[2]{0:T(128)} %pad_add_fusion.2.idx_ref, ...), custom_call_target="tpu_custom_call", output_to_operand_aliasing={{0}: (15, {}), {1}: (16, {}), {2}: (17, {}), {3}: (18, {}),... | custom-call | flops 4000000000 | bytes 22708224 | tf_op jit(solution)/shard_map/adamw/pallas_call | solution.py:371
  370.1 11.3 %adamw.15 = (bf16[2,16,48,1792]{3,2,1,0:T(8,128)(2,1)}, bf16[2,16,48,1792]{3,2,1,0:T(8,128)(2,1)}, bf16[2,7,16,16,768]{4,3,2,1,0:T(8,128)(2,1)}, f32[2,16,48,179...) custom-call(s32[2]{0:T(128)} %pad_add_fusion.1.idx_ref, ...), custom_call_target="tpu_custom_call", output_to_operand_aliasing={{0}: (15, {}), {1}: (16, {}), {2}: (17, {}), {3}: (18, {}),... | custom-call | flops 4000000000 | bytes 22708224 | tf_op jit(solution)/shard_map/adamw/pallas_call | solution.py:371
  382.4 6.4 %adamw.16 = (bf16[2,16,48,1792]{3,2,1,0:T(8,128)(2,1)}, bf16[2,16,48,1792]{3,2,1,0:T(8,128)(2,1)}, bf16[2,7,16,16,768]{4,3,2,1,0:T(8,128)(2,1)}, f32[2,16,48,179...) custom-call(s32[2]{0:T(128)} %pad_add_fusion.idx_ref, ...), custom_call_target="tpu_custom_call", output_to_operand_aliasing={{0}: (13, {}), {1}: (14, {}), {2}: (15, {}), {3}: (16, {}),... | custom-call | flops 2000000000 | bytes 11354112 | tf_op jit(solution)/shard_map/adamw/pallas_call | solution.py:371
  388.8 6.5 %adamw.17 = (bf16[2,16,48,1792]{3,2,1,0:T(8,128)(2,1)}, bf16[2,16,48,1792]{3,2,1,0:T(8,128)(2,1)}, bf16[2,7,16,16,768]{4,3,2,1,0:T(8,128)(2,1)}, f32[2,16,48,179...) custom-call(s32[2]{0:T(128)} %pad_add_fusion.idx_ref, ...), custom_call_target="tpu_custom_call", output_to_operand_aliasing={{0}: (13, {}), {1}: (14, {}), {2}: (15, {}), {3}: (16, {}),... | custom-call | flops 2000000000 | bytes 11354112 | tf_op jit(solution)/shard_map/adamw/pallas_call | solution.py:371
  (77 shorter events, 19.8 us)
Async XLA Ops:
  214.7 23.9 %collective-permute-start = (bf16[7,3,48,256]{3,2,1,0:T(8,128)(2,1)}, bf16[7,3,48,256]{3,2,1,0:T(8,128)(2,1)S(1)}, u32[]{:S(2)}, u32[]{:S(2)}) collective-permute-start(bf16[7,3,48,256]{3,2,1,0:T(8,128)(2,1)} %bitcast.134), channel_id=1, source_target_pairs={{0,1},{1,2},{2,3},{3,4},{4,5},{5,6},{6,7},{7,0},{8,9},{9,10},{10,1... | collective-permute-start | bytes 1548296 | tf_op jit(solution)/shard_map/ppermute | solution.py:407
  214.7 23.9 %collective-permute-start.7 = (bf16[7,3,48,256]{3,2,1,0:T(8,128)(2,1)}, bf16[7,3,48,256]{3,2,1,0:T(8,128)(2,1)}, u32[]{:S(2)}, u32[]{:S(2)}) collective-permute-start(bf16[7,3,48,256]{3,2,1,0:T(8,128)(2,1)} %bitcast.136), channel_id=1, source_target_pairs={{0,7},{1,0},{2,1},{3,2},{4,3},{5,4},{6,5},{7,6},{8,15},{9,8},{10,9... | collective-permute-start | bytes 1548296 | tf_op jit(solution)/shard_map/ppermute | solution.py:407
  227.5 22.1 %collective-permute-start.15 = (bf16[7,3,48,256]{3,2,1,0:T(8,128)(2,1)S(1)}, bf16[7,3,48,256]{3,2,1,0:T(8,128)(2,1)S(1)}, u32[]{:S(2)}, u32[]{:S(2)}) collective-permute-start(bf16[7,3,48,256]{3,2,1,0:T(8,128)(2,1)S(1)} %collective-permute-done.14.refs_0_), channel_id=1, source_target_pairs={{0,1},{1,2},{2,3},{3,4},{4,5},{5,6},{6,7},{7,0},{8,9},{9,10},{10,1... | collective-permute-start | bytes 1548296 | tf_op jit(solution)/shard_map/ppermute | solution.py:407
  227.5 22.1 %collective-permute-start.22 = (bf16[7,3,48,256]{3,2,1,0:T(8,128)(2,1)S(1)}, bf16[7,3,48,256]{3,2,1,0:T(8,128)(2,1)S(1)}, u32[]{:S(2)}, u32[]{:S(2)}) collective-permute-start(bf16[7,3,48,256]{3,2,1,0:T(8,128)(2,1)S(1)} %collective-permute-done.21.refs_1_), channel_id=1, source_target_pairs={{0,7},{1,0},{2,1},{3,2},{4,3},{5,4},{6,5},{7,6},{8,15},{9,8},{10,9... | collective-permute-start | bytes 1548296 | tf_op jit(solution)/shard_map/ppermute | solution.py:407
  238.6 22.2 %collective-permute-start.1 = (bf16[7,3,48,256]{3,2,1,0:T(8,128)(2,1)S(1)}, bf16[7,3,48,256]{3,2,1,0:T(8,128)(2,1)}, u32[]{:S(2)}, u32[]{:S(2)}) collective-permute-start(bf16[7,3,48,256]{3,2,1,0:T(8,128)(2,1)S(1)} %collective-permute-done.refs_2_), channel_id=1, source_target_pairs={{0,1},{1,2},{2,3},{3,4},{4,5},{5,6},{6,7},{7,0},{8,9},{9,10},{10,1... | collective-permute-start | bytes 1548296 | tf_op jit(solution)/shard_map/ppermute | solution.py:407
  238.6 22.2 %collective-permute-start.8 = (bf16[7,3,48,256]{3,2,1,0:T(8,128)(2,1)}, bf16[7,3,48,256]{3,2,1,0:T(8,128)(2,1)}, u32[]{:S(2)}, u32[]{:S(2)}) collective-permute-start(bf16[7,3,48,256]{3,2,1,0:T(8,128)(2,1)} %collective-permute-done.7.refs_3_), channel_id=1, source_target_pairs={{0,7},{1,0},{2,1},{3,2},{4,3},{5,4},{6,5},{7,6},{8,15},{9,8},{10,9... | collective-permute-start | bytes 1548296 | tf_op jit(solution)/shard_map/ppermute | solution.py:407
  249.6 29.7 %collective-permute-start.16 = (bf16[7,3,48,256]{3,2,1,0:T(8,128)(2,1)S(1)}, bf16[7,3,48,256]{3,2,1,0:T(8,128)(2,1)}, u32[]{:S(2)}, u32[]{:S(2)}) collective-permute-start(bf16[7,3,48,256]{3,2,1,0:T(8,128)(2,1)S(1)} %collective-permute-done.15.refs_0_), channel_id=1, source_target_pairs={{0,1},{1,2},{2,3},{3,4},{4,5},{5,6},{6,7},{7,0},{8,9},{9,10},{10,1... | collective-permute-start | bytes 1548296 | tf_op jit(solution)/shard_map/ppermute | solution.py:407
  249.6 31.2 %collective-permute-start.23 = (bf16[7,3,48,256]{3,2,1,0:T(8,128)(2,1)S(1)}, bf16[7,3,48,256]{3,2,1,0:T(8,128)(2,1)}, u32[]{:S(2)}, u32[]{:S(2)}) collective-permute-start(bf16[7,3,48,256]{3,2,1,0:T(8,128)(2,1)S(1)} %collective-permute-done.22.refs_1_), channel_id=1, source_target_pairs={{0,7},{1,0},{2,1},{3,2},{4,3},{5,4},{6,5},{7,6},{8,15},{9,8},{10,9... | collective-permute-start | bytes 1548296 | tf_op jit(solution)/shard_map/ppermute | solution.py:407
  260.8 35.1 %collective-permute-start.2 = (bf16[7,3,48,256]{3,2,1,0:T(8,128)(2,1)}, bf16[7,3,48,256]{3,2,1,0:T(8,128)(2,1)}, u32[]{:S(2)}, u32[]{:S(2)}) collective-permute-start(bf16[7,3,48,256]{3,2,1,0:T(8,128)(2,1)} %collective-permute-done.1.refs_2_), channel_id=1, source_target_pairs={{0,1},{1,2},{2,3},{3,4},{4,5},{5,6},{6,7},{7,0},{8,9},{9,10},{10,1... | collective-permute-start | bytes 1548296 | tf_op jit(solution)/shard_map/ppermute | solution.py:407
  260.8 33.1 %collective-permute-start.9 = (bf16[7,3,48,256]{3,2,1,0:T(8,128)(2,1)}, bf16[7,3,48,256]{3,2,1,0:T(8,128)(2,1)}, u32[]{:S(2)}, u32[]{:S(2)}) collective-permute-start(bf16[7,3,48,256]{3,2,1,0:T(8,128)(2,1)} %collective-permute-done.8.refs_3_), channel_id=1, source_target_pairs={{0,7},{1,0},{2,1},{3,2},{4,3},{5,4},{6,5},{7,6},{8,15},{9,8},{10,9... | collective-permute-start | bytes 1548296 | tf_op jit(solution)/shard_map/ppermute | solution.py:407
  279.3 17.9 %collective-permute-start.17 = (bf16[7,3,48,256]{3,2,1,0:T(8,128)(2,1)}, bf16[7,3,48,256]{3,2,1,0:T(8,128)(2,1)}, u32[]{:S(2)}, u32[]{:S(2)}) collective-permute-start(bf16[7,3,48,256]{3,2,1,0:T(8,128)(2,1)} %collective-permute-done.16.refs_0_), channel_id=1, source_target_pairs={{0,1},{1,2},{2,3},{3,4},{4,5},{5,6},{6,7},{7,0},{8,9},{9,10},{10,1... | collective-permute-start | bytes 1548296 | tf_op jit(solution)/shard_map/ppermute | solution.py:407
  293.9 18.0 %collective-permute-start.10 = (bf16[7,3,48,256]{3,2,1,0:T(8,128)(2,1)}, bf16[7,3,48,256]{3,2,1,0:T(8,128)(2,1)S(1)}, u32[]{:S(2)}, u32[]{:S(2)}) collective-permute-start(bf16[7,3,48,256]{3,2,1,0:T(8,128)(2,1)} %collective-permute-done.9.refs_3_), channel_id=1, source_target_pairs={{0,7},{1,0},{2,1},{3,2},{4,3},{5,4},{6,5},{7,6},{8,15},{9,8},{10,9... | collective-permute-start | bytes 1548296 | tf_op jit(solution)/shard_map/ppermute | solution.py:407
  297.2 28.1 %collective-permute-start.18 = (bf16[7,3,48,256]{3,2,1,0:T(8,128)(2,1)}, bf16[7,3,48,256]{3,2,1,0:T(8,128)(2,1)S(1)}, u32[]{:S(2)}, u32[]{:S(2)}) collective-permute-start(bf16[7,3,48,256]{3,2,1,0:T(8,128)(2,1)} %collective-permute-done.17.refs_0_), channel_id=1, source_target_pairs={{0,1},{1,2},{2,3},{3,4},{4,5},{5,6},{6,7},{7,0},{8,9},{9,10},{10,1... | collective-permute-start | bytes 1548296 | tf_op jit(solution)/shard_map/ppermute | solution.py:407
  297.5 27.9 %collective-permute-start.25 = (bf16[7,3,48,256]{3,2,1,0:T(8,128)(2,1)}, bf16[7,3,48,256]{3,2,1,0:T(8,128)(2,1)S(1)}, u32[]{:S(2)}, u32[]{:S(2)}) collective-permute-start(bf16[7,3,48,256]{3,2,1,0:T(8,128)(2,1)} %collective-permute-done.24.refs_1_), channel_id=1, source_target_pairs={{0,7},{1,0},{2,1},{3,2},{4,3},{5,4},{6,5},{7,6},{8,15},{9,8},{10,9... | collective-permute-start | bytes 1548296 | tf_op jit(solution)/shard_map/ppermute | solution.py:407
  311.9 28.0 %collective-permute-start.11 = (bf16[7,3,48,256]{3,2,1,0:T(8,128)(2,1)S(1)}, bf16[7,3,48,256]{3,2,1,0:T(8,128)(2,1)}, u32[]{:S(2)}, u32[]{:S(2)}) collective-permute-start(bf16[7,3,48,256]{3,2,1,0:T(8,128)(2,1)S(1)} %collective-permute-done.10.refs_3_), channel_id=1, source_target_pairs={{0,7},{1,0},{2,1},{3,2},{4,3},{5,4},{6,5},{7,6},{8,15},{9,8},{10,9... | collective-permute-start | bytes 1548296 | tf_op jit(solution)/shard_map/ppermute | solution.py:407
  313.7 28.0 %collective-permute-start.4 = (bf16[7,3,48,256]{3,2,1,0:T(8,128)(2,1)}, bf16[7,3,48,256]{3,2,1,0:T(8,128)(2,1)}, u32[]{:S(2)}, u32[]{:S(2)}) collective-permute-start(bf16[7,3,48,256]{3,2,1,0:T(8,128)(2,1)} %collective-permute-done.3.refs_2_), channel_id=1, source_target_pairs={{0,1},{1,2},{2,3},{3,4},{4,5},{5,6},{6,7},{7,0},{8,9},{9,10},{10,1... | collective-permute-start | bytes 1548296 | tf_op jit(solution)/shard_map/ppermute | solution.py:407
  325.3 28.0 %collective-permute-start.19 = (bf16[7,3,48,256]{3,2,1,0:T(8,128)(2,1)S(1)}, bf16[7,3,48,256]{3,2,1,0:T(8,128)(2,1)}, u32[]{:S(2)}, u32[]{:S(2)}) collective-permute-start(bf16[7,3,48,256]{3,2,1,0:T(8,128)(2,1)S(1)} %collective-permute-done.18.refs_0_), channel_id=1, source_target_pairs={{0,1},{1,2},{2,3},{3,4},{4,5},{5,6},{6,7},{7,0},{8,9},{9,10},{10,1... | collective-permute-start | bytes 1548296 | tf_op jit(solution)/shard_map/ppermute | solution.py:407
  325.5 28.0 %collective-permute-start.26 = (bf16[7,3,48,256]{3,2,1,0:T(8,128)(2,1)S(1)}, bf16[7,3,48,256]{3,2,1,0:T(8,128)(2,1)}, u32[]{:S(2)}, u32[]{:S(2)}) collective-permute-start(bf16[7,3,48,256]{3,2,1,0:T(8,128)(2,1)S(1)} %collective-permute-done.25.refs_1_), channel_id=1, source_target_pairs={{0,7},{1,0},{2,1},{3,2},{4,3},{5,4},{6,5},{7,6},{8,15},{9,8},{10,9... | collective-permute-start | bytes 1548296 | tf_op jit(solution)/shard_map/ppermute | solution.py:407
  340.0 28.0 %collective-permute-start.12 = (bf16[7,3,48,256]{3,2,1,0:T(8,128)(2,1)}, bf16[7,3,48,256]{3,2,1,0:T(8,128)(2,1)S(1)}, u32[]{:S(2)}, u32[]{:S(2)}) collective-permute-start(bf16[7,3,48,256]{3,2,1,0:T(8,128)(2,1)} %collective-permute-done.11.refs_3_), channel_id=1, source_target_pairs={{0,7},{1,0},{2,1},{3,2},{4,3},{5,4},{6,5},{7,6},{8,15},{9,8},{10,9... | collective-permute-start | bytes 1548296 | tf_op jit(solution)/shard_map/ppermute | solution.py:407
  341.8 28.0 %collective-permute-start.5 = (bf16[7,3,48,256]{3,2,1,0:T(8,128)(2,1)}, bf16[7,3,48,256]{3,2,1,0:T(8,128)(2,1)}, u32[]{:S(2)}, u32[]{:S(2)}) collective-permute-start(bf16[7,3,48,256]{3,2,1,0:T(8,128)(2,1)} %collective-permute-done.4.refs_2_), channel_id=1, source_target_pairs={{0,1},{1,2},{2,3},{3,4},{4,5},{5,6},{6,7},{7,0},{8,9},{9,10},{10,1... | collective-permute-start | bytes 1548296 | tf_op jit(solution)/shard_map/ppermute | solution.py:407
  353.4 28.0 %collective-permute-start.20 = (bf16[7,3,48,256]{3,2,1,0:T(8,128)(2,1)}, bf16[7,3,48,256]{3,2,1,0:T(8,128)(2,1)S(1)}, u32[]{:S(2)}, u32[]{:S(2)}) collective-permute-start(bf16[7,3,48,256]{3,2,1,0:T(8,128)(2,1)} %collective-permute-done.19.refs_0_), channel_id=1, source_target_pairs={{0,1},{1,2},{2,3},{3,4},{4,5},{5,6},{6,7},{7,0},{8,9},{9,10},{10,1... | collective-permute-start | bytes 1548296 | tf_op jit(solution)/shard_map/ppermute | solution.py:407
  353.5 27.9 %collective-permute-start.27 = (bf16[7,3,48,256]{3,2,1,0:T(8,128)(2,1)}, bf16[7,3,48,256]{3,2,1,0:T(8,128)(2,1)S(1)}, u32[]{:S(2)}, u32[]{:S(2)}) collective-permute-start(bf16[7,3,48,256]{3,2,1,0:T(8,128)(2,1)} %collective-permute-done.26.refs_1_), channel_id=1, source_target_pairs={{0,7},{1,0},{2,1},{3,2},{4,3},{5,4},{6,5},{7,6},{8,15},{9,8},{10,9... | collective-permute-start | bytes 1548296 | tf_op jit(solution)/shard_map/ppermute | solution.py:407
  368.0 20.8 %collective-permute-start.13 = (bf16[7,3,48,256]{3,2,1,0:T(8,128)(2,1)S(1)}, bf16[7,3,48,256]{3,2,1,0:T(8,128)(2,1)}, u32[]{:S(2)}, u32[]{:S(2)}) collective-permute-start(bf16[7,3,48,256]{3,2,1,0:T(8,128)(2,1)S(1)} %collective-permute-done.12.refs_3_), channel_id=1, source_target_pairs={{0,7},{1,0},{2,1},{3,2},{4,3},{5,4},{6,5},{7,6},{8,15},{9,8},{10,9... | collective-permute-start | bytes 1548296 | tf_op jit(solution)/shard_map/ppermute | solution.py:407
  369.8 19.0 %collective-permute-start.6 = (bf16[7,3,48,256]{3,2,1,0:T(8,128)(2,1)}, bf16[7,3,48,256]{3,2,1,0:T(8,128)(2,1)}, u32[]{:S(2)}, u32[]{:S(2)}) collective-permute-start(bf16[7,3,48,256]{3,2,1,0:T(8,128)(2,1)} %collective-permute-done.5.refs_2_), channel_id=1, source_target_pairs={{0,1},{1,2},{2,3},{3,4},{4,5},{5,6},{6,7},{7,0},{8,9},{9,10},{10,1... | collective-permute-start | bytes 1548296 | tf_op jit(solution)/shard_map/ppermute | solution.py:407
  (17 other events, 366.2 us)

commit v3 on v2

--- a/solution.py
+++ b/solution.py
@@ -27,8 +27,8 @@
     return 0.5 * jnp.tanh(0.5 * x) + 0.5
 
 
-def kernel(cfg, x_in, dy_in, wg_in, wu_in, wd_in, own00, own01, own10, own11, ss, S, xh, a, aT, dh, hid, wg, wu, wd, recv,
-           load_sem, x_sem, own_sem, send_sem, recv_sem, credit):
+def kernel(cfg, x_in, dy_in, wg_in, wu_in, wd_in, own00, own01, own10, own11, got0, got1, ss, S, xh, a, aT, dh, hid, wg, wu, wd, recv,
+           load_sem, x_sem, own_sem, send_sem, recv_sem, credit, got_send, got_recv):
     n, T, D, F, tt, tb, comm = cfg["n"], cfg["T"], cfg["D"], cfg["F"], cfg["tt"], cfg["tb"], cfg["comm"]
     NB = F // BW
     NBLK = 2 * NB
@@ -79,6 +79,12 @@
             src_ref=recv.at[d, slot], dst_ref=recv.at[d, slot], send_sem=send_sem.at[d, slot], recv_sem=recv_sem.at[d, slot],
             device_id={"dp": right if d == 0 else left}, device_id_type=pl.DeviceIdType.MESH)
 
+    def onward(k, d):
+        return pltpu.make_async_remote_copy(
+            src_ref=S.at[pl.ds(chunk_row(k, me, d), CH), :], dst_ref=(got0, got1)[d].at[k],
+            send_sem=got_send.at[d, k], recv_sem=got_recv.at[d, k],
+            device_id={"dp": right if d == 0 else left}, device_id_type=pl.DeviceIdType.MESH)
+
     def op(q, _):
         r, s = lax.div(q, n), lax.rem(q, n)
         b, live = block_of(r, s)
@@ -118,6 +124,13 @@
         def _():
             for d in range(2):
                 hop(r, s, d).start()
+        for when, blocks in ((LAST - 1, range(0, 1)), (LAST, range(1, 3)), (LAST + 1, range(3, NB))):
+            @pl.when((s == n - 1) & (r == when))
+            def _():
+                for k in blocks:
+                    if k < NB:
+                        for d in range(2):
+                            onward(k, d).start()
         @pl.when((s == n - 1) & (r >= 1) & (r <= LAST - RB + 1))
         def _():
             pl.semaphore_signal(credit.at[0], inc=1, device_id={"dp": left}, device_id_type=pl.DeviceIdType.MESH)
@@ -241,6 +254,10 @@
                     for d in range(2):
                         hop(r, s, d).wait_send()
         for d in range(2):
+            for k in range(NB):
+                onward(k, d).wait_recv()
+                onward(k, d).wait_send()
+        for d in range(2):
             for b in range(NBLK):
                 pltpu.make_async_copy(S.at[pl.ds(0, CH), :], (own00, own01, own10, own11)[2 * (b // NB) + d].at[b % NB], own_sem.at[d, b]).wait()
     else:
@@ -261,9 +278,9 @@
     flops = 18 * 2 * T * D * F
     return pl.pallas_call(
         functools.partial(kernel, cfg),
-        out_shape=(jax.ShapeDtypeStruct((NB, CH, BW), bf16),) * 4 + (jax.ShapeDtypeStruct((8, 128), f32),),
+        out_shape=(jax.ShapeDtypeStruct((NB, CH, BW), bf16),) * 6 + (jax.ShapeDtypeStruct((8, 128), f32),),
         in_specs=[any_] * 5,
-        out_specs=(any_,) * 4 + (pl.BlockSpec(memory_space=pltpu.VMEM),),
+        out_specs=(any_,) * 6 + (pl.BlockSpec(memory_space=pltpu.VMEM),),
         scratch_shapes=[
             pltpu.VMEM((max(GB + NB * 2 * T, 2 * GB + 2 * T), BW), bf16),
             pltpu.VMEM((T, D), bf16), pltpu.VMEM((T, D), bf16), pltpu.VMEM((D, T), bf16), pltpu.VMEM((T, D), bf16),
@@ -272,6 +289,7 @@
             pltpu.VMEM((2, RB * (n - 1), CH, BW), bf16),
             pltpu.SemaphoreType.DMA((8,)), pltpu.SemaphoreType.DMA, pltpu.SemaphoreType.DMA((2, NBLK)),
             pltpu.SemaphoreType.DMA((2, RB * (n - 1))), pltpu.SemaphoreType.DMA((2, RB * (n - 1))), pltpu.SemaphoreType.REGULAR((2,)),
+            pltpu.SemaphoreType.DMA((2, NB)), pltpu.SemaphoreType.DMA((2, NB)),
         ],
         compiler_params=pltpu.CompilerParams(vmem_limit_bytes=67043328, collective_id=cid if comm else None, has_side_effects=True),
         cost_estimate=pl.CostEstimate(flops=flops, bytes_accessed=40 * 10**6, transcendentals=0),
@@ -326,57 +344,74 @@
     return (w - 0.02 * step).astype(bf16), m, v
 
 
-def adam_kernel(pieces, idx_ref, fac_ref, *refs):
-    pays, ins, outs = refs[: len(pieces)], refs[len(pieces) : len(pieces) + 9], refs[-9:]
+def adam_kernel(layers, idx_ref, fac_ref, *refs):
+    k = len(layers)
+    pays, ins, outs = refs[:k], refs[k : k + 9], refs[-17:-8]
+    gbuf, wbuf, wdown, fbuf, fdown, gsem, isem, osem = refs[-8:]
     factor = fac_ref[0:1, 0:1]
-    def one(p):
-        def step(k, at, g):
-            new = adam_math(ins[k][at].astype(f32), ins[3 + k][at], ins[6 + k][at], g.astype(f32) * factor)
-            for i in range(3):
-                outs[3 * i + k][at] = new[i]
-        hr = ins[2].shape[3]
+
+    def place(i, a):
+        which, kind = a // 3, a % 3
+        if which == 0:
+            return wdown.at[i] if kind == 2 else wbuf.at[i, kind]
+        return fdown.at[i, which - 1] if kind == 2 else fbuf.at[i, which - 1, kind]
+
+    def rows(arrays, i, a):
+        return arrays[a].at[layers[i], :, idx_ref[i]] if a % 3 == 2 else arrays[a].at[layers[i], idx_ref[i]]
+
+    loads = [[pltpu.make_async_copy(pays[i], gbuf.at[i], gsem.at[i])] + [pltpu.make_async_copy(rows(ins, i, a), place(i, a), isem.at[i, a]) for a in range(9)] for i in range(k)]
+    stores = [[pltpu.make_async_copy(place(i, a), rows(outs, i, a), osem.at[i, a]) for a in range(9)] for i in range(k)]
+    for piece in loads:
+        for c in piece:
+            c.start()
+    hr = wdown.shape[2]
+    for i in range(k):
+        for c in loads[i]:
+            c.wait()
+        def step(w, m, v, at, g):
+            new = adam_math(w[at].astype(f32), m[at], v[at], g.astype(f32) * factor)
+            for ref, value in zip((w, m, v), new, strict=True):
+                ref[at] = value
         def block(j, _):
             cols = pl.ds(pl.multiple_of(j * BW, BW), BW)
-            step(0, (0, 0, slice(None), cols), p[j, 0])
-            step(1, (0, 0, slice(None), cols), p[j, 1])
-            for cg in range(ins[2].shape[4] // BW):
-                step(2, (0, j, 0, slice(None), slice(cg * BW, (cg + 1) * BW)), p[j, 2, cg * hr : (cg + 1) * hr])
+            for kind in range(2):
+                step(wbuf.at[i, kind], fbuf.at[i, 0, kind], fbuf.at[i, 1, kind], (slice(None), cols), gbuf[i, j, kind])
+            for cg in range(wdown.shape[3] // BW):
+                at = (j, slice(None), slice(cg * BW, (cg + 1) * BW))
+                step(wdown.at[i], fdown.at[i, 0], fdown.at[i, 1], at, gbuf[i, j, 2, cg * hr : (cg + 1) * hr])
             return 0
-        lax.fori_loop(0, p.shape[0], block, 0)
-    if len(pieces) == 1:
-        one(pays[0])
-    else:
-        for i in range(len(pieces)):
-            pl.when(pl.program_id(0) == i)(functools.partial(one, pays[i]))
-
-
-def pick(values, i):
-    out = values[0]
-    for k in range(1, len(values)):
-        out = jnp.where(i == k, values[k], out)
-    return out
-
-
-def adam_call(idx, factor, pieces, pays, ins, prev):
-    nb = pays[0].shape[0]
-    layer = lambda i: pick([l for l, _ in pieces], i)
-    chunk = lambda i, idx: pick([idx[d] for _, d in pieces], i)
-    rows = pl.BlockSpec((1, 1) + ins[0].shape[2:], lambda i, idx: (layer(i), chunk(i, idx), 0, 0))
-    down = pl.BlockSpec((1, nb, 1) + ins[2].shape[3:], lambda i, idx: (layer(i), 0, chunk(i, idx), 0, 0))
-    pay = pl.BlockSpec(pays[0].shape, lambda i, idx: (0, 0, 0, 0), pipeline_mode=pl.Buffered(1))
-    specs = [rows, rows, down] * 3
-    any_ = [] if prev is None else [pl.BlockSpec(memory_space=pl.ANY)] * 9
+        lax.fori_loop(0, gbuf.shape[1], block, 0)
+        for c in stores[i]:
+            c.start()
+    for piece in stores:
+        for c in piece:
+            c.wait()
+
+
+def adam_call(factor, pieces, ins, prev):
     k = len(pieces)
+    layers = tuple(l for l, _, _ in pieces)
+    idx = jnp.stack([c for _, c, _ in pieces]).astype(jnp.int32)
+    pays = [g for _, _, g in pieces]
+    hbm = pl.BlockSpec(memory_space=pl.ANY)
+    kept = [] if prev is None else list(prev)
     size = k * pays[0].size
+    rows, down = ins[0].shape[2:], (ins[2].shape[1],) + ins[2].shape[3:]
     return pl.pallas_call(
-        functools.partial(adam_kernel, tuple(pieces)),
+        functools.partial(adam_kernel, layers),
         grid_spec=pltpu.PrefetchScalarGridSpec(
-            num_scalar_prefetch=1, grid=(k,), in_specs=[pl.BlockSpec((8, 128), lambda i, idx: (0, 0))] + [pay] * k + specs + any_, out_specs=specs),
+            num_scalar_prefetch=1, grid=(1,),
+            in_specs=[pl.BlockSpec((8, 128), lambda i, idx: (0, 0))] + [hbm] * (k + 9 + len(kept)),
+            out_specs=[hbm] * 9,
+            scratch_shapes=[
+                pltpu.VMEM((k,) + pays[0].shape, bf16), pltpu.VMEM((k, 2) + rows, bf16), pltpu.VMEM((k,) + down, bf16),
+                pltpu.VMEM((k, 2, 2) + rows, f32), pltpu.VMEM((k, 2) + down, f32),
+                pltpu.SemaphoreType.DMA((k,)), pltpu.SemaphoreType.DMA((k, 9)), pltpu.SemaphoreType.DMA((k, 9))]),
         out_shape=[jax.ShapeDtypeStruct(x.shape, x.dtype) for x in ins],
         input_output_aliases={} if prev is None else {2 + k + 9 + i: i for i in range(9)},
-        compiler_params=pltpu.CompilerParams(vmem_limit_bytes=62 * 2**20, dimension_semantics=("arbitrary",)),
-        cost_estimate=pl.CostEstimate(flops=4 * 10**9 * k // 4, bytes_accessed=22 * size, transcendentals=size),
-        name="adamw")(idx, factor, *pays, *ins, *([] if prev is None else prev))
+        compiler_params=pltpu.CompilerParams(vmem_limit_bytes=62 * 2**20),
+        cost_estimate=pl.CostEstimate(flops=10**9 * k, bytes_accessed=22 * size, transcendentals=size),
+        name="adamw")(idx, factor, *pays, *ins, *kept)
 
 
 def views(arrays, n):
@@ -393,28 +428,32 @@
 
     def step(x, dy, *arrays):
         me = lax.axis_index("dp")
-        own00, own01, own10, own11, squares = k1(x[0], dy[0], *arrays[:3], n)
+        *sums, squares = k1(x[0], dy[0], *arrays[:3], n)
         _, _, F = arrays[0].shape
         ins = views(arrays, n)
         count = sum(w.size for w in arrays[:3])
-        pieces = [(1, 0), (1, 1), (0, 0), (0, 1)]
-        pays = [o.reshape(F // BW, 3, o.shape[1] // 3, BW) for o in (own00, own01, own10, own11)]
-        factor, outs = None, None
-        for s in range(n):
-            coming = []
+        last, first, came = ([o.reshape(F // BW, 3, o.shape[1] // 3, BW) for o in sums[i : i + 2]] for i in (0, 2, 4))
+
+        def pieces(layer, pays, hops):
+            return [(layer, 2 * lax.rem(me - hops + n, n), pays[0]), (layer, 2 * lax.rem(me + hops, n) + 1, pays[1])]
+
+        waiting = pieces(1, last, 0) + pieces(0, first, 0) + pieces(1, came, 1)
+        outs, last = None, came
+        for s in range(1, n):
+            ahead = []
+            for d in range(2):
+                first[d] = lax.ppermute(first[d], "dp", to[d])
             if s < n - 1:
-                for i, (l, d) in enumerate(pieces):
-                    coming.append(lax.ppermute(pays[i], "dp", to[d]))
-            if factor is None:
+                for d in range(2):
+                    ahead.append(lax.ppermute(last[d], "dp", to[d]))
+            if s == 1:
                 factor = clip_factor(squares, count, n)
-            c0, c1 = lax.rem(me - s + n, n), lax.rem(me + s, n)
-            idx = jnp.stack([2 * c0, 2 * c1 + 1]).astype(jnp.int32)
-            if s < n - 1:
-                outs = adam_call(idx, factor, pieces, pays, ins, outs)
             else:
-                outs = adam_call(idx, factor, pieces[:2], pays[:2], ins, outs)
-                outs = adam_call(idx, factor, pieces[2:], pays[2:], ins, outs)
-            pays = coming
+                outs = adam_call(factor, waiting, ins, outs)
+                waiting = []
+            waiting = waiting + pieces(0, first, s) + (pieces(1, ahead, s + 1) if ahead else [])
+            first, last = list(first), ahead
+        outs = adam_call(factor, waiting, ins, outs)
         return tuple(o.reshape(w.shape) for o, w in zip(outs, arrays))
 
     step = jax.shard_map(

time: 396 us -> 399 us (level)
  the two profiles are of different devices: /device:TPU:22 before, /device:TPU:30 now
where the time goes in v3:
time: 399 us
  Pallas kernels  315 us (79%)
  waiting for transfers between devices  39.6 us (10%)
  starting transfers between devices  36.6 us (9%)
    pallas_call x1, Pallas kernels, k1(): pl.pallas_call(functools.partial(kernel, cfg), out_shape=(jax.ShapeDtypeS...  219 us
    pallas_call x7, Pallas kernels, adam_call(): pl.pallas_call(functools.partial(adam_kernel, layers), grid_spec=pltpu.Pr...  79.7 us
    ppermute x12, waiting for transfers between devices, step(): ahead.append(lax.ppermute(last[d], 'dp', to[d]))  20.2 us
    ppermute x12, starting transfers between devices, step(): ahead.append(lax.ppermute(last[d], 'dp', to[d]))  19.6 us
    ppermute x14, waiting for transfers between devices, step(): first[d] = lax.ppermute(first[d], 'dp', to[d])  19.5 us
    ppermute x14, starting transfers between devices, step(): first[d] = lax.ppermute(first[d], 'dp', to[d])  17 us
    pallas_call x1, Pallas kernels, clip_factor(): pl.pallas_call(functools.partial(factor_kernel, n, float(count)), out_sha...  16.2 us
  transfers between devices with their start and end apart: 26, of which 5 were waited for; matrix products, arithmetic and copies ran while one was open for 1% of the time, Pallas kernels for 22%

profile of v3, /device:TPU:30, one launch (start us, length us, event | category | flops | bytes accessed | tf_op | source)
XLA Modules:
  0.0 398.5 jit_solution(12154012391917496437)
XLA Ops:
  0.6 219.5 %grads.1 = (bf16[7,144,256]{2,1,0:T(8,128)(2,1)}, bf16[7,144,256]{2,1,0:T(8,128)(2,1)}, bf16[7,144,256]{2,1,0:T(8,128)(2,1)}, bf16[7,144,256]{2,1,0:T(8,128)(2,1...) custom-call(bf16[2048,768]{1,0:T(8,128)(2,1)} %bitcast.124, ...), custom_call_target="tpu_custom_call" | custom-call | flops 101468602368 | bytes 40000000 | tf_op jit(solution)/shard_map/grads/pallas_call | solution.py:279
  222.7 2.8 collective-permute-start.20
  225.5 9.6 %collective-permute-done.7.refs_7_ = bf16[7,3,48,256]{3,2,1,0:T(8,128)(2,1)S(1)} collective-permute-done((bf16[7,3,48,256]{3,2,1,0:T(8,128)(2,1)}, bf16[7,3,48,256]{3,2,1,0:T(8,128)(2,1)S(1)}, u32[]{:S(2)}, u32[]{:S(2)}) %collective-permute-start.7) | collective-permute-done | bytes 516128 | tf_op jit(solution)/shard_map/ppermute | solution.py:445
  235.1 2.8 collective-permute-start.8
  237.9 11.2 %collective-permute-done.14.refs_8_ = bf16[7,3,48,256]{3,2,1,0:T(8,128)(2,1)} collective-permute-done((bf16[7,3,48,256]{3,2,1,0:T(8,128)(2,1)}, bf16[7,3,48,256]{3,2,1,0:T(8,128)(2,1)}, u32[]{:S(2)}, u32[]{:S(2)}) %collective-permute-start.14) | collective-permute-done | bytes 516128 | tf_op jit(solution)/shard_map/ppermute | solution.py:448
  249.1 3.2 collective-permute-start.21
  252.3 4.9 %collective-permute-done.8.refs_1_ = bf16[7,3,48,256]{3,2,1,0:T(8,128)(2,1)S(1)} collective-permute-done((bf16[7,3,48,256]{3,2,1,0:T(8,128)(2,1)S(1)}, bf16[7,3,48,256]{3,2,1,0:T(8,128)(2,1)S(1)}, u32[]{:S(2)}, u32[]{:S(2)}) %collective-permute-start.8) | collective-permute-done | bytes 516128 | tf_op jit(solution)/shard_map/ppermute | solution.py:445
  257.2 2.8 collective-permute-start.9
  262.1 9.0 %collective-permute-done.15.refs_2_ = bf16[7,3,48,256]{3,2,1,0:T(8,128)(2,1)S(1)} collective-permute-done((bf16[7,3,48,256]{3,2,1,0:T(8,128)(2,1)}, bf16[7,3,48,256]{3,2,1,0:T(8,128)(2,1)S(1)}, u32[]{:S(2)}, u32[]{:S(2)}) %collective-permute-start.15) | collective-permute-done | bytes 516128 | tf_op jit(solution)/shard_map/ppermute | solution.py:448
  271.1 3.2 collective-permute-start.22
  274.3 5.0 %collective-permute-done.9.refs_1_ = bf16[7,3,48,256]{3,2,1,0:T(8,128)(2,1)S(1)} collective-permute-done((bf16[7,3,48,256]{3,2,1,0:T(8,128)(2,1)S(1)}, bf16[7,3,48,256]{3,2,1,0:T(8,128)(2,1)S(1)}, u32[]{:S(2)}, u32[]{:S(2)}) %collective-permute-start.9) | collective-permute-done | bytes 516128 | tf_op jit(solution)/shard_map/ppermute | solution.py:445
  279.3 2.8 collective-permute-start.10
  282.8 16.2 %factor.1.fac_ref = f32[8,128]{1,0:T(8,128)S(1)} custom-call(f32[8,128]{1,0:T(8,128)S(1)} %copy-done.1), custom_call_target="tpu_custom_call" | custom-call | flops 1000000000 | bytes 100000 | tf_op jit(solution)/shard_map/factor/pallas_call | solution.py:329
  305.6 1.8 collective-permute-start.4
  307.5 20.1 %adamw.7 = (bf16[2,16,48,1792]{3,2,1,0:T(8,128)(2,1)}, bf16[2,16,48,1792]{3,2,1,0:T(8,128)(2,1)}, bf16[2,7,16,16,768]{4,3,2,1,0:T(8,128)(2,1)}, f32[2,16,48,1792...) custom-call(s32[10]{0:T(128)} %stack.107.idx_ref, ...), custom_call_target="tpu_custom_call" | custom-call | flops 10000000000 | bytes 56770560 | tf_op jit(solution)/shard_map/adamw/pallas_call | solution.py:400
  328.2 2.7 collective-permute-start.24
  330.9 10.4 %adamw.8 = (bf16[2,16,48,1792]{3,2,1,0:T(8,128)(2,1)}, bf16[2,16,48,1792]{3,2,1,0:T(8,128)(2,1)}, bf16[2,7,16,16,768]{4,3,2,1,0:T(8,128)(2,1)}, f32[2,16,48,1792...) custom-call(s32[4]{0:T(128)} %pad_add_fusion.5.idx_ref, ...), custom_call_target="tpu_custom_call", output_to_operand_aliasing={{0}: (15, {}), {1}: (16, {}), {2}: (17, {}), {3}: (18, {}),... | custom-call | flops 4000000000 | bytes 22708224 | tf_op jit(solution)/shard_map/adamw/pallas_call | solution.py:400
  341.7 1.8 collective-permute-start.5
  343.5 10.4 %adamw.9 = (bf16[2,16,48,1792]{3,2,1,0:T(8,128)(2,1)}, bf16[2,16,48,1792]{3,2,1,0:T(8,128)(2,1)}, bf16[2,7,16,16,768]{4,3,2,1,0:T(8,128)(2,1)}, f32[2,16,48,1792...) custom-call(s32[4]{0:T(128)} %pad_add_fusion.4.idx_ref, ...), custom_call_target="tpu_custom_call", output_to_operand_aliasing={{0}: (15, {}), {1}: (16, {}), {2}: (17, {}), {3}: (18, {}),... | custom-call | flops 4000000000 | bytes 22708224 | tf_op jit(solution)/shard_map/adamw/pallas_call | solution.py:400
  354.1 3.2 collective-permute-start.25
  357.3 10.4 %adamw.10 = (bf16[2,16,48,1792]{3,2,1,0:T(8,128)(2,1)}, bf16[2,16,48,1792]{3,2,1,0:T(8,128)(2,1)}, bf16[2,7,16,16,768]{4,3,2,1,0:T(8,128)(2,1)}, f32[2,16,48,179...) custom-call(s32[4]{0:T(128)} %pad_add_fusion.3.idx_ref, ...), custom_call_target="tpu_custom_call", output_to_operand_aliasing={{0}: (15, {}), {1}: (16, {}), {2}: (17, {}), {3}: (18, {}),... | custom-call | flops 4000000000 | bytes 22708224 | tf_op jit(solution)/shard_map/adamw/pallas_call | solution.py:400
  369.9 10.4 %adamw.11 = (bf16[2,16,48,1792]{3,2,1,0:T(8,128)(2,1)}, bf16[2,16,48,1792]{3,2,1,0:T(8,128)(2,1)}, bf16[2,7,16,16,768]{4,3,2,1,0:T(8,128)(2,1)}, f32[2,16,48,179...) custom-call(s32[4]{0:T(128)} %pad_add_fusion.2.idx_ref, ...), custom_call_target="tpu_custom_call", output_to_operand_aliasing={{0}: (15, {}), {1}: (16, {}), {2}: (17, {}), {3}: (18, {}),... | custom-call | flops 4000000000 | bytes 22708224 | tf_op jit(solution)/shard_map/adamw/pallas_call | solution.py:400
  380.4 10.6 %adamw.12 = (bf16[2,16,48,1792]{3,2,1,0:T(8,128)(2,1)}, bf16[2,16,48,1792]{3,2,1,0:T(8,128)(2,1)}, bf16[2,7,16,16,768]{4,3,2,1,0:T(8,128)(2,1)}, f32[2,16,48,179...) custom-call(s32[4]{0:T(128)} %pad_add_fusion.1.idx_ref, ...), custom_call_target="tpu_custom_call", output_to_operand_aliasing={{0}: (15, {}), {1}: (16, {}), {2}: (17, {}), {3}: (18, {}),... | custom-call | flops 4000000000 | bytes 22708224 | tf_op jit(solution)/shard_map/adamw/pallas_call | solution.py:400
  391.0 7.3 %adamw.13 = (bf16[2,16,48,1792]{3,2,1,0:T(8,128)(2,1)}, bf16[2,16,48,1792]{3,2,1,0:T(8,128)(2,1)}, bf16[2,7,16,16,768]{4,3,2,1,0:T(8,128)(2,1)}, f32[2,16,48,179...) custom-call(s32[2]{0:T(128)} %pad_add_fusion.idx_ref, ...), custom_call_target="tpu_custom_call", output_to_operand_aliasing={{0}: (13, {}), {1}: (14, {}), {2}: (15, {}), {3}: (16, {}),... | custom-call | flops 2000000000 | bytes 11354112 | tf_op jit(solution)/shard_map/adamw/pallas_call | solution.py:400
  (68 shorter events, 15.1 us)
Async XLA Ops:
  222.3 26.8 %collective-permute-start.14 = (bf16[7,3,48,256]{3,2,1,0:T(8,128)(2,1)}, bf16[7,3,48,256]{3,2,1,0:T(8,128)(2,1)}, u32[]{:S(2)}, u32[]{:S(2)}) collective-permute-start(bf16[7,3,48,256]{3,2,1,0:T(8,128)(2,1)} %bitcast.120), channel_id=1, source_target_pairs={{0,1},{1,2},{2,3},{3,4},{4,5},{5,6},{6,7},{7,0},{8,9},{9,10},{10,1... | collective-permute-start | bytes 1548296 | tf_op jit(solution)/shard_map/ppermute | solution.py:448
  222.7 26.4 %collective-permute-start.20 = (bf16[7,3,48,256]{3,2,1,0:T(8,128)(2,1)}, bf16[7,3,48,256]{3,2,1,0:T(8,128)(2,1)}, u32[]{:S(2)}, u32[]{:S(2)}) collective-permute-start(bf16[7,3,48,256]{3,2,1,0:T(8,128)(2,1)} %bitcast.122), channel_id=1, source_target_pairs={{0,7},{1,0},{2,1},{3,2},{4,3},{5,4},{6,5},{7,6},{8,15},{9,8},{10,9... | collective-permute-start | bytes 1548296 | tf_op jit(solution)/shard_map/ppermute | solution.py:448
  235.1 22.1 %collective-permute-start.8 = (bf16[7,3,48,256]{3,2,1,0:T(8,128)(2,1)S(1)}, bf16[7,3,48,256]{3,2,1,0:T(8,128)(2,1)S(1)}, u32[]{:S(2)}, u32[]{:S(2)}) collective-permute-start(bf16[7,3,48,256]{3,2,1,0:T(8,128)(2,1)S(1)} %collective-permute-done.7.refs_7_), channel_id=1, source_target_pairs={{0,7},{1,0},{2,1},{3,2},{4,3},{5,4},{6,5},{7,6},{8,15},{9,8},{10,9... | collective-permute-start | bytes 1548296 | tf_op jit(solution)/shard_map/ppermute | solution.py:445
  237.9 22.1 %collective-permute-start.1 = (bf16[7,3,48,256]{3,2,1,0:T(8,128)(2,1)S(1)}, bf16[7,3,48,256]{3,2,1,0:T(8,128)(2,1)S(1)}, u32[]{:S(2)}, u32[]{:S(2)}) collective-permute-start(bf16[7,3,48,256]{3,2,1,0:T(8,128)(2,1)S(1)} %collective-permute-done.refs_6_), channel_id=1, source_target_pairs={{0,1},{1,2},{2,3},{3,4},{4,5},{5,6},{6,7},{7,0},{8,9},{9,10},{10,1... | collective-permute-start | bytes 1548296 | tf_op jit(solution)/shard_map/ppermute | solution.py:445
  249.1 22.0 %collective-permute-start.15 = (bf16[7,3,48,256]{3,2,1,0:T(8,128)(2,1)}, bf16[7,3,48,256]{3,2,1,0:T(8,128)(2,1)S(1)}, u32[]{:S(2)}, u32[]{:S(2)}) collective-permute-start(bf16[7,3,48,256]{3,2,1,0:T(8,128)(2,1)} %collective-permute-done.14.refs_8_), channel_id=1, source_target_pairs={{0,1},{1,2},{2,3},{3,4},{4,5},{5,6},{6,7},{7,0},{8,9},{9,10},{10,1... | collective-permute-start | bytes 1548296 | tf_op jit(solution)/shard_map/ppermute | solution.py:448
  249.1 22.0 %collective-permute-start.21 = (bf16[7,3,48,256]{3,2,1,0:T(8,128)(2,1)}, bf16[7,3,48,256]{3,2,1,0:T(8,128)(2,1)}, u32[]{:S(2)}, u32[]{:S(2)}) collective-permute-start(bf16[7,3,48,256]{3,2,1,0:T(8,128)(2,1)} %collective-permute-done.20.refs_9_), channel_id=1, source_target_pairs={{0,7},{1,0},{2,1},{3,2},{4,3},{5,4},{6,5},{7,6},{8,15},{9,8},{10,9... | collective-permute-start | bytes 1548296 | tf_op jit(solution)/shard_map/ppermute | solution.py:448
  257.2 22.1 %collective-permute-start.9 = (bf16[7,3,48,256]{3,2,1,0:T(8,128)(2,1)S(1)}, bf16[7,3,48,256]{3,2,1,0:T(8,128)(2,1)S(1)}, u32[]{:S(2)}, u32[]{:S(2)}) collective-permute-start(bf16[7,3,48,256]{3,2,1,0:T(8,128)(2,1)S(1)} %collective-permute-done.8.refs_1_), channel_id=1, source_target_pairs={{0,7},{1,0},{2,1},{3,2},{4,3},{5,4},{6,5},{7,6},{8,15},{9,8},{10,9... | collective-permute-start | bytes 1548296 | tf_op jit(solution)/shard_map/ppermute | solution.py:445
  260.0 22.1 %collective-permute-start.2 = (bf16[7,3,48,256]{3,2,1,0:T(8,128)(2,1)S(1)}, bf16[7,3,48,256]{3,2,1,0:T(8,128)(2,1)S(1)}, u32[]{:S(2)}, u32[]{:S(2)}) collective-permute-start(bf16[7,3,48,256]{3,2,1,0:T(8,128)(2,1)S(1)} %collective-permute-done.1.refs_0_), channel_id=1, source_target_pairs={{0,1},{1,2},{2,3},{3,4},{4,5},{5,6},{6,7},{7,0},{8,9},{9,10},{10,1... | collective-permute-start | bytes 1548296 | tf_op jit(solution)/shard_map/ppermute | solution.py:445
  271.1 31.1 %collective-permute-start.16 = (bf16[7,3,48,256]{3,2,1,0:T(8,128)(2,1)S(1)}, bf16[7,3,48,256]{3,2,1,0:T(8,128)(2,1)}, u32[]{:S(2)}, u32[]{:S(2)}) collective-permute-start(bf16[7,3,48,256]{3,2,1,0:T(8,128)(2,1)S(1)} %collective-permute-done.15.refs_2_), channel_id=1, source_target_pairs={{0,1},{1,2},{2,3},{3,4},{4,5},{5,6},{6,7},{7,0},{8,9},{9,10},{10,1... | collective-permute-start | bytes 1548296 | tf_op jit(solution)/shard_map/ppermute | solution.py:448
  271.1 32.6 %collective-permute-start.22 = (bf16[7,3,48,256]{3,2,1,0:T(8,128)(2,1)}, bf16[7,3,48,256]{3,2,1,0:T(8,128)(2,1)}, u32[]{:S(2)}, u32[]{:S(2)}) collective-permute-start(bf16[7,3,48,256]{3,2,1,0:T(8,128)(2,1)} %collective-permute-done.21.refs_3_), channel_id=1, source_target_pairs={{0,7},{1,0},{2,1},{3,2},{4,3},{5,4},{6,5},{7,6},{8,15},{9,8},{10,9... | collective-permute-start | bytes 1548296 | tf_op jit(solution)/shard_map/ppermute | solution.py:448
  279.3 26.1 %collective-permute-start.10 = (bf16[7,3,48,256]{3,2,1,0:T(8,128)(2,1)S(1)}, bf16[7,3,48,256]{3,2,1,0:T(8,128)(2,1)}, u32[]{:S(2)}, u32[]{:S(2)}) collective-permute-start(bf16[7,3,48,256]{3,2,1,0:T(8,128)(2,1)S(1)} %collective-permute-done.9.refs_1_), channel_id=1, source_target_pairs={{0,7},{1,0},{2,1},{3,2},{4,3},{5,4},{6,5},{7,6},{8,15},{9,8},{10,9... | collective-permute-start | bytes 1548296 | tf_op jit(solution)/shard_map/ppermute | solution.py:445
  282.1 23.5 %collective-permute-start.3 = (bf16[7,3,48,256]{3,2,1,0:T(8,128)(2,1)S(1)}, bf16[7,3,48,256]{3,2,1,0:T(8,128)(2,1)}, u32[]{:S(2)}, u32[]{:S(2)}) collective-permute-start(bf16[7,3,48,256]{3,2,1,0:T(8,128)(2,1)S(1)} %collective-permute-done.2.refs_0_), channel_id=1, source_target_pairs={{0,1},{1,2},{2,3},{3,4},{4,5},{5,6},{6,7},{7,0},{8,9},{9,10},{10,1... | collective-permute-start | bytes 1548296 | tf_op jit(solution)/shard_map/ppermute | solution.py:445
  302.2 25.4 %collective-permute-start.17 = (bf16[7,3,48,256]{3,2,1,0:T(8,128)(2,1)}, bf16[7,3,48,256]{3,2,1,0:T(8,128)(2,1)}, u32[]{:S(2)}, u32[]{:S(2)}) collective-permute-start(bf16[7,3,48,256]{3,2,1,0:T(8,128)(2,1)} %collective-permute-done.16.refs_2_), channel_id=1, source_target_pairs={{0,1},{1,2},{2,3},{3,4},{4,5},{5,6},{6,7},{7,0},{8,9},{9,10},{10,1... | collective-permute-start | bytes 1548296 | tf_op jit(solution)/shard_map/ppermute | solution.py:448
  303.7 24.4 %collective-permute-start.23 = (bf16[7,3,48,256]{3,2,1,0:T(8,128)(2,1)}, bf16[7,3,48,256]{3,2,1,0:T(8,128)(2,1)}, u32[]{:S(2)}, u32[]{:S(2)}) collective-permute-start(bf16[7,3,48,256]{3,2,1,0:T(8,128)(2,1)} %collective-permute-done.22.refs_3_), channel_id=1, source_target_pairs={{0,7},{1,0},{2,1},{3,2},{4,3},{5,4},{6,5},{7,6},{8,15},{9,8},{10,9... | collective-permute-start | bytes 1548296 | tf_op jit(solution)/shard_map/ppermute | solution.py:448
  305.4 35.9 %collective-permute-start.11 = (bf16[7,3,48,256]{3,2,1,0:T(8,128)(2,1)}, bf16[7,3,48,256]{3,2,1,0:T(8,128)(2,1)}, u32[]{:S(2)}, u32[]{:S(2)}) collective-permute-start(bf16[7,3,48,256]{3,2,1,0:T(8,128)(2,1)} %collective-permute-done.10.refs_1_), channel_id=1, source_target_pairs={{0,7},{1,0},{2,1},{3,2},{4,3},{5,4},{6,5},{7,6},{8,15},{9,8},{10,9... | collective-permute-start | bytes 1548296 | tf_op jit(solution)/shard_map/ppermute | solution.py:445
  305.6 36.1 %collective-permute-start.4 = (bf16[7,3,48,256]{3,2,1,0:T(8,128)(2,1)}, bf16[7,3,48,256]{3,2,1,0:T(8,128)(2,1)}, u32[]{:S(2)}, u32[]{:S(2)}) collective-permute-start(bf16[7,3,48,256]{3,2,1,0:T(8,128)(2,1)} %collective-permute-done.3.refs_0_), channel_id=1, source_target_pairs={{0,1},{1,2},{2,3},{3,4},{4,5},{5,6},{6,7},{7,0},{8,9},{9,10},{10,1... | collective-permute-start | bytes 1548296 | tf_op jit(solution)/shard_map/ppermute | solution.py:445
  327.6 26.4 %collective-permute-start.18 = (bf16[7,3,48,256]{3,2,1,0:T(8,128)(2,1)}, bf16[7,3,48,256]{3,2,1,0:T(8,128)(2,1)S(1)}, u32[]{:S(2)}, u32[]{:S(2)}) collective-permute-start(bf16[7,3,48,256]{3,2,1,0:T(8,128)(2,1)} %collective-permute-done.17.refs_2_), channel_id=1, source_target_pairs={{0,1},{1,2},{2,3},{3,4},{4,5},{5,6},{6,7},{7,0},{8,9},{9,10},{10,1... | collective-permute-start | bytes 1548296 | tf_op jit(solution)/shard_map/ppermute | solution.py:448
  328.2 25.9 %collective-permute-start.24 = (bf16[7,3,48,256]{3,2,1,0:T(8,128)(2,1)}, bf16[7,3,48,256]{3,2,1,0:T(8,128)(2,1)S(1)}, u32[]{:S(2)}, u32[]{:S(2)}) collective-permute-start(bf16[7,3,48,256]{3,2,1,0:T(8,128)(2,1)} %collective-permute-done.23.refs_3_), channel_id=1, source_target_pairs={{0,7},{1,0},{2,1},{3,2},{4,3},{5,4},{6,5},{7,6},{8,15},{9,8},{10,9... | collective-permute-start | bytes 1548296 | tf_op jit(solution)/shard_map/ppermute | solution.py:448
  341.4 26.4 %collective-permute-start.12 = (bf16[7,3,48,256]{3,2,1,0:T(8,128)(2,1)}, bf16[7,3,48,256]{3,2,1,0:T(8,128)(2,1)S(1)}, u32[]{:S(2)}, u32[]{:S(2)}) collective-permute-start(bf16[7,3,48,256]{3,2,1,0:T(8,128)(2,1)} %collective-permute-done.11.refs_1_), channel_id=1, source_target_pairs={{0,7},{1,0},{2,1},{3,2},{4,3},{5,4},{6,5},{7,6},{8,15},{9,8},{10,9... | collective-permute-start | bytes 1548296 | tf_op jit(solution)/shard_map/ppermute | solution.py:445
  341.7 26.4 %collective-permute-start.5 = (bf16[7,3,48,256]{3,2,1,0:T(8,128)(2,1)}, bf16[7,3,48,256]{3,2,1,0:T(8,128)(2,1)}, u32[]{:S(2)}, u32[]{:S(2)}) collective-permute-start(bf16[7,3,48,256]{3,2,1,0:T(8,128)(2,1)} %collective-permute-done.4.refs_0_), channel_id=1, source_target_pairs={{0,1},{1,2},{2,3},{3,4},{4,5},{5,6},{6,7},{7,0},{8,9},{9,10},{10,1... | collective-permute-start | bytes 1548296 | tf_op jit(solution)/shard_map/ppermute | solution.py:445
  353.9 26.4 %collective-permute-start.19 = (bf16[7,3,48,256]{3,2,1,0:T(8,128)(2,1)S(1)}, bf16[7,3,48,256]{3,2,1,0:T(8,128)(2,1)}, u32[]{:S(2)}, u32[]{:S(2)}) collective-permute-start(bf16[7,3,48,256]{3,2,1,0:T(8,128)(2,1)S(1)} %collective-permute-done.18.refs_2_), channel_id=1, source_target_pairs={{0,1},{1,2},{2,3},{3,4},{4,5},{5,6},{6,7},{7,0},{8,9},{9,10},{10,1... | collective-permute-start | bytes 1548296 | tf_op jit(solution)/shard_map/ppermute | solution.py:448
  354.1 26.3 %collective-permute-start.25 = (bf16[7,3,48,256]{3,2,1,0:T(8,128)(2,1)S(1)}, bf16[7,3,48,256]{3,2,1,0:T(8,128)(2,1)}, u32[]{:S(2)}, u32[]{:S(2)}) collective-permute-start(bf16[7,3,48,256]{3,2,1,0:T(8,128)(2,1)S(1)} %collective-permute-done.24.refs_3_), channel_id=1, source_target_pairs={{0,7},{1,0},{2,1},{3,2},{4,3},{5,4},{6,5},{7,6},{8,15},{9,8},{10,9... | collective-permute-start | bytes 1548296 | tf_op jit(solution)/shard_map/ppermute | solution.py:448
  367.8 23.2 %collective-permute-start.13 = (bf16[7,3,48,256]{3,2,1,0:T(8,128)(2,1)S(1)}, bf16[7,3,48,256]{3,2,1,0:T(8,128)(2,1)}, u32[]{:S(2)}, u32[]{:S(2)}) collective-permute-start(bf16[7,3,48,256]{3,2,1,0:T(8,128)(2,1)S(1)} %collective-permute-done.12.refs_1_), channel_id=1, source_target_pairs={{0,7},{1,0},{2,1},{3,2},{4,3},{5,4},{6,5},{7,6},{8,15},{9,8},{10,9... | collective-permute-start | bytes 1548296 | tf_op jit(solution)/shard_map/ppermute | solution.py:445
  368.1 22.9 %collective-permute-start.6 = (bf16[7,3,48,256]{3,2,1,0:T(8,128)(2,1)}, bf16[7,3,48,256]{3,2,1,0:T(8,128)(2,1)}, u32[]{:S(2)}, u32[]{:S(2)}) collective-permute-start(bf16[7,3,48,256]{3,2,1,0:T(8,128)(2,1)} %collective-permute-done.5.refs_0_), channel_id=1, source_target_pairs={{0,1},{1,2},{2,3},{3,4},{4,5},{5,6},{6,7},{7,0},{8,9},{9,10},{10,1... | collective-permute-start | bytes 1548296 | tf_op jit(solution)/shard_map/ppermute | solution.py:445
  (14 other events, 357.6 us)

commit v4 on v3

--- a/solution.py
+++ b/solution.py
@@ -27,8 +27,8 @@
     return 0.5 * jnp.tanh(0.5 * x) + 0.5
 
 
-def kernel(cfg, x_in, dy_in, wg_in, wu_in, wd_in, own00, own01, own10, own11, got0, got1, ss, S, xh, a, aT, dh, hid, wg, wu, wd, recv,
-           load_sem, x_sem, own_sem, send_sem, recv_sem, credit, got_send, got_recv):
+def kernel(cfg, x_in, dy_in, wg_in, wu_in, wd_in, own00, own01, own10, own11, got0, got1, factor, S, xh, a, aT, dh, hid, wg, wu, wd, recv,
+           load_sem, x_sem, own_sem, send_sem, recv_sem, credit, got_send, got_recv, ss, squares, sq_send, sq_recv):
     n, T, D, F, tt, tb, comm = cfg["n"], cfg["T"], cfg["D"], cfg["F"], cfg["tt"], cfg["tb"], cfg["comm"]
     NB = F // BW
     NBLK = 2 * NB
@@ -38,11 +38,15 @@
     GB = NB * BR
     hr = BW // (2 * n)
     ncg = D // BW
-    ramp = max(NBLK - 4, 1)
-    start = lambda b: jnp.where(b <= ramp, 2 * b, b + ramp)
-    LAST = NBLK - 1 + ramp + n - 2
+    gap = cfg["gap"]
+    ramp = max(NBLK - cfg["quick"], NB)
+    def start(b):
+        return jnp.where(b < NB, 2 * b, jnp.where(b <= ramp, 2 * b + gap, b + ramp + gap))
+    LAST = NBLK - 1 + ramp + gap + n - 2
+    ahead = ((LAST - 2, range(0, min(1, NB))), (LAST - 1, range(1, min(3, NB))), (LAST, range(3, min(6, NB))))
     me = lax.axis_index("dp")
     right, left = lax.rem(me + 1, n), lax.rem(me + n - 1, n)
+    peers = [lax.rem(me + i, n) for i in range(1, n)]
 
     loads = [pltpu.make_async_copy(s, d, load_sem.at[i]) for i, (s, d) in enumerate((
         (x_in, xh), (wg_in.at[0], wg.at[0]), (wu_in.at[0], wu.at[0]), (wd_in.at[0], wd.at[0]), (dy_in, dh),
@@ -51,8 +55,8 @@
         c.start()
     if comm:
         barrier = pltpu.get_barrier_semaphore()
-        for nb in (left, right):
-            pl.semaphore_signal(barrier, inc=1, device_id={"dp": nb}, device_id_type=pl.DeviceIdType.MESH)
+        for p in peers:
+            pl.semaphore_signal(barrier, inc=1, device_id={"dp": p}, device_id_type=pl.DeviceIdType.MESH)
     ss[...] = jnp.zeros_like(ss)
 
     def chunk_row(b, c, d):
@@ -63,8 +67,11 @@
 
     def block_of(r, s):
         z = r - s
-        b = jnp.where(z < 2 * ramp, lax.div(z, 2), z - ramp)
-        return b, (z >= 0) & ((z >= 2 * ramp) | (lax.rem(z, 2) == 0)) & (b < NBLK)
+        y = z - gap
+        b = jnp.where(z < 2 * NB, lax.div(z, 2), jnp.where(y < 2 * ramp, lax.div(y, 2), y - ramp))
+        early = (z >= 0) & (z < 2 * NB) & (lax.rem(z, 2) == 0)
+        late = (y >= 2 * NB) & ((y >= 2 * ramp) | (lax.rem(y, 2) == 0))
+        return b, (early | late) & (b < NBLK)
 
     def hop(r, s, d):
         b, _ = block_of(r, s)
@@ -124,13 +131,12 @@
         def _():
             for d in range(2):
                 hop(r, s, d).start()
-        for when, blocks in ((LAST - 1, range(0, 1)), (LAST, range(1, 3)), (LAST + 1, range(3, NB))):
+        for when, blocks in ahead:
             @pl.when((s == n - 1) & (r == when))
             def _():
                 for k in blocks:
-                    if k < NB:
-                        for d in range(2):
-                            onward(k, d).start()
+                    for d in range(2):
+                        onward(k, d).start()
         @pl.when((s == n - 1) & (r >= 1) & (r <= LAST - RB + 1))
         def _():
             pl.semaphore_signal(credit.at[0], inc=1, device_id={"dp": left}, device_id_type=pl.DeviceIdType.MESH)
@@ -175,7 +181,7 @@
         return 0
     lax.fori_loop(0, T // tt, fwd_down, 0)
 
-    def block(l, j, dg0, du0, b, q, pace):
+    def block(l, j, dg0, du0, b, q, pace, pace2):
         cols = pl.ds(pl.multiple_of(j * BW, BW), BW)
         q = ops(q, pace, b)
         def tokens(t, q):
@@ -201,7 +207,7 @@
                     S[pl.ds(pl.multiple_of(base + e * CH + 2 * H + cg * hr, 16), hr), :] = w[e * hr:(e + 1) * hr, cg * BW:(cg + 1) * BW]
         dgv = lambda: S[pl.ds(pl.multiple_of(dg0, 16), T), :]
         duv = lambda: S[pl.ds(pl.multiple_of(du0, 16), T), :]
-        q = ops(q, pace, b)
+        q = ops(q, pace2, b)
         w = mm(aT[...], jnp.concatenate([dgv(), duv()], axis=1)).astype(bf16)
         gate_up(w[:, :BW], 0)
         gate_up(w[:, BW:], 1)
@@ -211,13 +217,13 @@
     for c in loads[4:]:
         c.wait()
     def last_layer(j, q):
-        return block(1, j, GB + j * 2 * T, GB + j * 2 * T + T, j, q, jnp.where(j <= 2, n, cfg["pace"][0]))
+        return block(1, j, GB + j * 2 * T, GB + j * 2 * T + T, j, q, jnp.where(j <= 2, n, cfg["pace"][0]), jnp.where(j <= 2, n, cfg["pace"][1]))
     if comm:
-        pl.semaphore_wait(barrier, 2)
+        pl.semaphore_wait(barrier, n - 1)
     q = lax.fori_loop(0, NB, last_layer, 0)
 
     def d_input(t, q):
-        q = ops(q, cfg["pace"][1], NB)
+        q = ops(q, cfg["pace"][2], NB)
         rows = pl.ds(pl.multiple_of(t * tt, tt), tt)
         dg = jnp.concatenate([S[pl.ds(pl.multiple_of(GB + j * 2 * T + t * tt, 16), tt), :] for j in range(NB)], axis=1)
         du = jnp.concatenate([S[pl.ds(pl.multiple_of(GB + j * 2 * T + T + t * tt, 16), tt), :] for j in range(NB)], axis=1)
@@ -242,17 +248,38 @@
     lax.fori_loop(0, T // tt, renorm, 0)
 
     def first_layer(j, q):
-        return block(0, j, 2 * GB, 2 * GB + T, NB + j, q, cfg["pace"][2])
+        return block(0, j, 2 * GB, 2 * GB + T, NB + j, q, cfg["pace"][3], cfg["pace"][3])
     q = lax.fori_loop(0, NB, first_layer, q)
     if comm:
         lax.fori_loop(q, (LAST + 2) * n, op, 0)
+        copies = [
+            pltpu.make_async_remote_copy(
+                src_ref=ss, dst_ref=squares.at[me], send_sem=sq_send.at[i], recv_sem=sq_recv.at[me],
+                device_id={"dp": p}, device_id_type=pl.DeviceIdType.MESH)
+            for i, p in enumerate(peers)]
+        for c in copies:
+            c.start()
+        squares[me] = ss[...]
+        for k in range(min(6, NB), NB):
+            for d in range(2):
+                onward(k, d).start()
         for r in range(LAST - RB + 2, LAST + 1):
             for s in range(n - 1):
-                z = r - s
-                b = z // 2 if z < 2 * ramp else z - ramp
-                if z >= 0 and (z >= 2 * ramp or z % 2 == 0) and b < NBLK:
-                    for d in range(2):
-                        hop(r, s, d).wait_send()
+                for b in range(NBLK):
+                    if r - s == (2 * b if b < NB else 2 * b + gap if b <= ramp else b + ramp + gap):
+                        for d in range(2):
+                            hop(r, s, d).wait_send()
+        for i, p in enumerate(peers):
+            pltpu.make_async_remote_copy(
+                src_ref=ss, dst_ref=squares.at[p], send_sem=sq_send.at[i], recv_sem=sq_recv.at[p],
+                device_id={"dp": p}, device_id_type=pl.DeviceIdType.MESH).wait_recv()
+        total = squares[0]
+        for i in range(1, n):
+            total = total + squares[i]
+        total = jnp.sum(jnp.sum(total, axis=0, keepdims=True), axis=1, keepdims=True)
+        factor[...] = jnp.broadcast_to(jnp.minimum(1.0, 0.5 * lax.rsqrt(total / float(NBLK * BR * BW) + 1e-30)), factor.shape)
+        for c in copies:
+            c.wait_send()
         for d in range(2):
             for k in range(NB):
                 onward(k, d).wait_recv()
@@ -266,14 +293,14 @@
         for c in cps: c.wait()
 
 
-def k1(x, dy, wg, wu, wd, n, tt=512, tb=512, comm=True, cid=0, pace=(6, 7, 6)):
+def k1(x, dy, wg, wu, wd, n, tt=512, tb=512, comm=True, cid=0, pace=(5, 5, 6, 6), gap=0, quick=4):
     T, D = x.shape
     F = wg.shape[2]
     NB = F // BW
     NBLK = 2 * NB
     H = D // (2 * n); CH = 3 * H
     GB = NB * 3 * D
-    cfg = dict(n=n, T=T, D=D, F=F, tt=min(tt, T), tb=min(tb, T), comm=comm, pace=pace)
+    cfg = dict(n=n, T=T, D=D, F=F, tt=min(tt, T), tb=min(tb, T), comm=comm, pace=pace, gap=gap, quick=quick)
     any_ = pl.BlockSpec(memory_space=pl.ANY)
     flops = 18 * 2 * T * D * F
     return pl.pallas_call(
@@ -290,51 +317,11 @@
             pltpu.SemaphoreType.DMA((8,)), pltpu.SemaphoreType.DMA, pltpu.SemaphoreType.DMA((2, NBLK)),
             pltpu.SemaphoreType.DMA((2, RB * (n - 1))), pltpu.SemaphoreType.DMA((2, RB * (n - 1))), pltpu.SemaphoreType.REGULAR((2,)),
             pltpu.SemaphoreType.DMA((2, NB)), pltpu.SemaphoreType.DMA((2, NB)),
+            pltpu.VMEM((8, 128), f32), pltpu.VMEM((n, 8, 128), f32), pltpu.SemaphoreType.DMA((n - 1,)), pltpu.SemaphoreType.DMA((n,)),
         ],
         compiler_params=pltpu.CompilerParams(vmem_limit_bytes=67043328, collective_id=cid if comm else None, has_side_effects=True),
         cost_estimate=pl.CostEstimate(flops=flops, bytes_accessed=40 * 10**6, transcendentals=0),
         name="grads")(x, dy, wg, wu, wd)
-
-
-def factor_kernel(n, count, sq, out, slots, send_sem, recv_sem):
-    me = lax.axis_index("dp")
-    barrier = pltpu.get_barrier_semaphore()
-    peers = [lax.rem(me + p, n) for p in range(1, n)]
-    for q in peers:
-        pl.semaphore_signal(barrier, inc=1, device_id={"dp": q}, device_id_type=pl.DeviceIdType.MESH)
-    slots[me] = sq[...]
-    pl.semaphore_wait(barrier, n - 1)
-    copies = [
-        pltpu.make_async_remote_copy(
-            src_ref=sq, dst_ref=slots.at[me], send_sem=send_sem.at[i], recv_sem=recv_sem.at[me],
-            device_id={"dp": q}, device_id_type=pl.DeviceIdType.MESH)
-        for i, q in enumerate(peers)]
-    for c in copies:
-        c.start()
-    for i, q in enumerate(peers):
-        pltpu.make_async_remote_copy(
-            src_ref=sq, dst_ref=slots.at[q], send_sem=send_sem.at[i], recv_sem=recv_sem.at[q],
-            device_id={"dp": q}, device_id_type=pl.DeviceIdType.MESH).wait_recv()
-    total = slots[0]
-    for i in range(1, n):
-        total = total + slots[i]
-    total = jnp.sum(jnp.sum(total, axis=0, keepdims=True), axis=1, keepdims=True)
-    out[...] = jnp.broadcast_to(jnp.minimum(1.0, 0.5 * lax.rsqrt(total / count + 1e-30)), out.shape)
-    for c in copies:
-        c.wait_send()
-
-
-def clip_factor(squares, count, n):
-    vmem = pl.BlockSpec(memory_space=pltpu.VMEM)
-    return pl.pallas_call(
-        functools.partial(factor_kernel, n, float(count)),
-        out_shape=jax.ShapeDtypeStruct(squares.shape, f32),
-        in_specs=[vmem],
-        out_specs=vmem,
-        scratch_shapes=[pltpu.VMEM((n,) + squares.shape, f32), pltpu.SemaphoreType.DMA((n - 1,)), pltpu.SemaphoreType.DMA((n,))],
-        compiler_params=pltpu.CompilerParams(collective_id=1, has_side_effects=True, vmem_limit_bytes=2**20),
-        cost_estimate=pl.CostEstimate(flops=10**9, bytes_accessed=10**5, transcendentals=0),
-        name="factor")(squares)
 
 
 def adam_math(w, m, v, g):
@@ -359,30 +346,36 @@
     def rows(arrays, i, a):
         return arrays[a].at[layers[i], :, idx_ref[i]] if a % 3 == 2 else arrays[a].at[layers[i], idx_ref[i]]
 
-    loads = [[pltpu.make_async_copy(pays[i], gbuf.at[i], gsem.at[i])] + [pltpu.make_async_copy(rows(ins, i, a), place(i, a), isem.at[i, a]) for a in range(9)] for i in range(k)]
+    loads = [[pltpu.make_async_copy(rows(ins, i, a), place(i, a), isem.at[i, a]) for a in range(9)] for i in range(k)]
+    pay_loads = [pltpu.make_async_copy(pays[i], gbuf.at[i], gsem.at[i]) for i in range(k)]
     stores = [[pltpu.make_async_copy(place(i, a), rows(outs, i, a), osem.at[i, a]) for a in range(9)] for i in range(k)]
-    for piece in loads:
-        for c in piece:
-            c.start()
+    for i in range(k):
+        pay_loads[i].start()
+        for kind in range(3):
+            for a in range(kind, 9, 3):
+                loads[i][a].start()
     hr = wdown.shape[2]
     for i in range(k):
-        for c in loads[i]:
-            c.wait()
+        pay_loads[i].wait()
         def step(w, m, v, at, g):
             new = adam_math(w[at].astype(f32), m[at], v[at], g.astype(f32) * factor)
             for ref, value in zip((w, m, v), new, strict=True):
                 ref[at] = value
-        def block(j, _):
-            cols = pl.ds(pl.multiple_of(j * BW, BW), BW)
-            for kind in range(2):
-                step(wbuf.at[i, kind], fbuf.at[i, 0, kind], fbuf.at[i, 1, kind], (slice(None), cols), gbuf[i, j, kind])
-            for cg in range(wdown.shape[3] // BW):
-                at = (j, slice(None), slice(cg * BW, (cg + 1) * BW))
-                step(wdown.at[i], fdown.at[i, 0], fdown.at[i, 1], at, gbuf[i, j, 2, cg * hr : (cg + 1) * hr])
-            return 0
-        lax.fori_loop(0, gbuf.shape[1], block, 0)
-        for c in stores[i]:
-            c.start()
+        for kind in range(3):
+            for a in range(kind, 9, 3):
+                loads[i][a].wait()
+            def block(j, _):
+                if kind < 2:
+                    cols = pl.ds(pl.multiple_of(j * BW, BW), BW)
+                    step(wbuf.at[i, kind], fbuf.at[i, 0, kind], fbuf.at[i, 1, kind], (slice(None), cols), gbuf[i, j, kind])
+                else:
+                    for cg in range(wdown.shape[3] // BW):
+                        at = (j, slice(None), slice(cg * BW, (cg + 1) * BW))
+                        step(wdown.at[i], fdown.at[i, 0], fdown.at[i, 1], at, gbuf[i, j, 2, cg * hr : (cg + 1) * hr])
+                return 0
+            lax.fori_loop(0, gbuf.shape[1], block, 0)
+            for a in range(kind, 9, 3):
+                stores[i][a].start()
     for piece in stores:
         for c in piece:
             c.wait()
@@ -428,10 +421,9 @@
 
     def step(x, dy, *arrays):
         me = lax.axis_index("dp")
-        *sums, squares = k1(x[0], dy[0], *arrays[:3], n)
+        *sums, factor = k1(x[0], dy[0], *arrays[:3], n)
         _, _, F = arrays[0].shape
         ins = views(arrays, n)
-        count = sum(w.size for w in arrays[:3])
         last, first, came = ([o.reshape(F // BW, 3, o.shape[1] // 3, BW) for o in sums[i : i + 2]] for i in (0, 2, 4))
 
         def pieces(layer, pays, hops):
@@ -441,18 +433,15 @@
         outs, last = None, came
         for s in range(1, n):
             ahead = []
+            first = list(first)
             for d in range(2):
                 first[d] = lax.ppermute(first[d], "dp", to[d])
             if s < n - 1:
                 for d in range(2):
                     ahead.append(lax.ppermute(last[d], "dp", to[d]))
-            if s == 1:
-                factor = clip_factor(squares, count, n)
-            else:
-                outs = adam_call(factor, waiting, ins, outs)
-                waiting = []
-            waiting = waiting + pieces(0, first, s) + (pieces(1, ahead, s + 1) if ahead else [])
-            first, last = list(first), ahead
+            outs = adam_call(factor, waiting, ins, outs)
+            waiting = pieces(0, first, s) + (pieces(1, ahead, s + 1) if ahead else [])
+            last = ahead
         outs = adam_call(factor, waiting, ins, outs)
         return tuple(o.reshape(w.shape) for o, w in zip(outs, arrays))
 

time: 399 us -> 387 us (0.970)
  the two profiles are of different devices: /device:TPU:30 before, /device:TPU:22 now
where the time goes in v4:
time: 387 us
  Pallas kernels  302 us (78%)
  starting transfers between devices  41.3 us (11%)
  waiting for transfers between devices  36.7 us (9%)
  other arithmetic  4.38 us (1%)
    pallas_call x1, Pallas kernels, k1(): pl.pallas_call(functools.partial(kernel, cfg), out_shape=(jax.ShapeDtypeS...  219 us
    pallas_call x8, Pallas kernels, adam_call(): pl.pallas_call(functools.partial(adam_kernel, layers), grid_spec=pltpu.Pr...  82.4 us
    ppermute x14, waiting for transfers between devices, step(): first[d] = lax.ppermute(first[d], 'dp', to[d])  23.4 us
    ppermute x14, starting transfers between devices, step(): first[d] = lax.ppermute(first[d], 'dp', to[d])  21.4 us
    ppermute x12, starting transfers between devices, step(): ahead.append(lax.ppermute(last[d], 'dp', to[d]))  19.9 us
    ppermute x12, waiting for transfers between devices, step(): ahead.append(lax.ppermute(last[d], 'dp', to[d]))  13.3 us
  transfers between devices with their start and end apart: 26, of which 5 were waited for; matrix products, arithmetic and copies ran while one was open for 1% of the time, Pallas kernels for 20%

profile of v4, /device:TPU:22, one launch (start us, length us, event | category | flops | bytes accessed | tf_op | source)
XLA Modules:
  0.0 386.6 jit_solution(10152919019014333519)
XLA Ops:
  0.6 219.2 %grads.1 = (bf16[7,144,256]{2,1,0:T(8,128)(2,1)}, bf16[7,144,256]{2,1,0:T(8,128)(2,1)}, bf16[7,144,256]{2,1,0:T(8,128)(2,1)}, bf16[7,144,256]{2,1,0:T(8,128)(2,1...) custom-call(bf16[2048,768]{1,0:T(8,128)(2,1)} %bitcast.133, ...), custom_call_target="tpu_custom_call" | custom-call | flops 101468602368 | bytes 40000000 | tf_op jit(solution)/shard_map/grads/pallas_call | solution.py:306
  223.1 3.2 collective-permute-start.20
  226.4 9.6 %collective-permute-done.refs_0_ = bf16[7,3,48,256]{3,2,1,0:T(8,128)(2,1)S(1)} collective-permute-done((bf16[7,3,48,256]{3,2,1,0:T(8,128)(2,1)}, bf16[7,3,48,256]{3,2,1,0:T(8,128)(2,1)S(1)}, u32[]{:S(2)}, u32[]{:S(2)}) %collective-permute-start) | collective-permute-done | bytes 516128 | tf_op jit(solution)/shard_map/ppermute | solution.py:438
  236.0 3.2 collective-permute-start.8
  239.9 7.2 %collective-permute-done.14.refs_2_ = bf16[7,3,48,256]{3,2,1,0:T(8,128)(2,1)} collective-permute-done((bf16[7,3,48,256]{3,2,1,0:T(8,128)(2,1)}, bf16[7,3,48,256]{3,2,1,0:T(8,128)(2,1)}, u32[]{:S(2)}, u32[]{:S(2)}) %collective-permute-start.14) | collective-permute-done | bytes 516128 | tf_op jit(solution)/shard_map/ppermute | solution.py:441
  247.1 3.2 collective-permute-start.21
  250.3 7.7 %collective-permute-done.1.refs_0_ = bf16[7,3,48,256]{3,2,1,0:T(8,128)(2,1)S(1)} collective-permute-done((bf16[7,3,48,256]{3,2,1,0:T(8,128)(2,1)S(1)}, bf16[7,3,48,256]{3,2,1,0:T(8,128)(2,1)S(1)}, u32[]{:S(2)}, u32[]{:S(2)}) %collective-permute-start.1) | collective-permute-done | bytes 516128 | tf_op jit(solution)/shard_map/ppermute | solution.py:438
  258.1 3.3 collective-permute-start.9
  261.4 13.8 %adamw.8 = (bf16[2,16,48,1792]{3,2,1,0:T(8,128)(2,1)}, bf16[2,16,48,1792]{3,2,1,0:T(8,128)(2,1)}, bf16[2,7,16,16,768]{4,3,2,1,0:T(8,128)(2,1)}, f32[2,16,48,1792...) custom-call(s32[6]{0:T(128)} %stack.111.idx_ref, ...), custom_call_target="tpu_custom_call" | custom-call | flops 6000000000 | bytes 34062336 | tf_op jit(solution)/shard_map/adamw/pallas_call | solution.py:393
  275.3 3.2 collective-permute-start.22
  279.8 3.7 collective-permute-start.10
  285.4 6.0 %collective-permute-done.16.refs_2_ = bf16[7,3,48,256]{3,2,1,0:T(8,128)(2,1)} collective-permute-done((bf16[7,3,48,256]{3,2,1,0:T(8,128)(2,1)}, bf16[7,3,48,256]{3,2,1,0:T(8,128)(2,1)}, u32[]{:S(2)}, u32[]{:S(2)}) %collective-permute-start.16) | collective-permute-done | bytes 516128 | tf_op jit(solution)/shard_map/ppermute | solution.py:441
  291.5 3.2 collective-permute-start.23
  295.9 6.1 %collective-permute-done.10.refs_1_ = bf16[7,3,48,256]{3,2,1,0:T(8,128)(2,1)S(1)} collective-permute-done((bf16[7,3,48,256]{3,2,1,0:T(8,128)(2,1)}, bf16[7,3,48,256]{3,2,1,0:T(8,128)(2,1)S(1)}, u32[]{:S(2)}, u32[]{:S(2)}) %collective-permute-start.10) | collective-permute-done | bytes 516128 | tf_op jit(solution)/shard_map/ppermute | solution.py:438
  302.1 3.6 collective-permute-start.11
  305.7 10.3 %adamw.9 = (bf16[2,16,48,1792]{3,2,1,0:T(8,128)(2,1)}, bf16[2,16,48,1792]{3,2,1,0:T(8,128)(2,1)}, bf16[2,7,16,16,768]{4,3,2,1,0:T(8,128)(2,1)}, f32[2,16,48,1792...) custom-call(s32[4]{0:T(128)} %pad_add_fusion.6.idx_ref, ...), custom_call_target="tpu_custom_call", output_to_operand_aliasing={{0}: (15, {}), {1}: (16, {}), {2}: (17, {}), {3}: (18, {}),... | custom-call | flops 4000000000 | bytes 22708224 | tf_op jit(solution)/shard_map/adamw/pallas_call | solution.py:393
  316.1 3.3 collective-permute-start.24
  319.4 10.2 %adamw.10 = (bf16[2,16,48,1792]{3,2,1,0:T(8,128)(2,1)}, bf16[2,16,48,1792]{3,2,1,0:T(8,128)(2,1)}, bf16[2,7,16,16,768]{4,3,2,1,0:T(8,128)(2,1)}, f32[2,16,48,179...) custom-call(s32[4]{0:T(128)} %pad_add_fusion.5.idx_ref, ...), custom_call_target="tpu_custom_call", output_to_operand_aliasing={{0}: (15, {}), {1}: (16, {}), {2}: (17, {}), {3}: (18, {}),... | custom-call | flops 4000000000 | bytes 22708224 | tf_op jit(solution)/shard_map/adamw/pallas_call | solution.py:393
  331.8 10.2 %adamw.11 = (bf16[2,16,48,1792]{3,2,1,0:T(8,128)(2,1)}, bf16[2,16,48,1792]{3,2,1,0:T(8,128)(2,1)}, bf16[2,7,16,16,768]{4,3,2,1,0:T(8,128)(2,1)}, f32[2,16,48,179...) custom-call(s32[4]{0:T(128)} %pad_add_fusion.4.idx_ref, ...), custom_call_target="tpu_custom_call", output_to_operand_aliasing={{0}: (15, {}), {1}: (16, {}), {2}: (17, {}), {3}: (18, {}),... | custom-call | flops 4000000000 | bytes 22708224 | tf_op jit(solution)/shard_map/adamw/pallas_call | solution.py:393
  342.3 3.3 collective-permute-start.25
  345.6 10.2 %adamw.12 = (bf16[2,16,48,1792]{3,2,1,0:T(8,128)(2,1)}, bf16[2,16,48,1792]{3,2,1,0:T(8,128)(2,1)}, bf16[2,7,16,16,768]{4,3,2,1,0:T(8,128)(2,1)}, f32[2,16,48,179...) custom-call(s32[4]{0:T(128)} %pad_add_fusion.3.idx_ref, ...), custom_call_target="tpu_custom_call", output_to_operand_aliasing={{0}: (15, {}), {1}: (16, {}), {2}: (17, {}), {3}: (18, {}),... | custom-call | flops 4000000000 | bytes 22708224 | tf_op jit(solution)/shard_map/adamw/pallas_call | solution.py:393
  358.0 10.2 %adamw.13 = (bf16[2,16,48,1792]{3,2,1,0:T(8,128)(2,1)}, bf16[2,16,48,1792]{3,2,1,0:T(8,128)(2,1)}, bf16[2,7,16,16,768]{4,3,2,1,0:T(8,128)(2,1)}, f32[2,16,48,179...) custom-call(s32[4]{0:T(128)} %pad_add_fusion.2.idx_ref, ...), custom_call_target="tpu_custom_call", output_to_operand_aliasing={{0}: (15, {}), {1}: (16, {}), {2}: (17, {}), {3}: (18, {}),... | custom-call | flops 4000000000 | bytes 22708224 | tf_op jit(solution)/shard_map/adamw/pallas_call | solution.py:393
  368.3 10.5 %adamw.14 = (bf16[2,16,48,1792]{3,2,1,0:T(8,128)(2,1)}, bf16[2,16,48,1792]{3,2,1,0:T(8,128)(2,1)}, bf16[2,7,16,16,768]{4,3,2,1,0:T(8,128)(2,1)}, f32[2,16,48,179...) custom-call(s32[4]{0:T(128)} %pad_add_fusion.1.idx_ref, ...), custom_call_target="tpu_custom_call", output_to_operand_aliasing={{0}: (15, {}), {1}: (16, {}), {2}: (17, {}), {3}: (18, {}),... | custom-call | flops 4000000000 | bytes 22708224 | tf_op jit(solution)/shard_map/adamw/pallas_call | solution.py:393
  379.5 6.9 %adamw.15 = (bf16[2,16,48,1792]{3,2,1,0:T(8,128)(2,1)}, bf16[2,16,48,1792]{3,2,1,0:T(8,128)(2,1)}, bf16[2,7,16,16,768]{4,3,2,1,0:T(8,128)(2,1)}, f32[2,16,48,179...) custom-call(s32[2]{0:T(128)} %pad_add_fusion.idx_ref, ...), custom_call_target="tpu_custom_call", output_to_operand_aliasing={{0}: (13, {}), {1}: (14, {}), {2}: (15, {}), {3}: (16, {}),... | custom-call | flops 2000000000 | bytes 11354112 | tf_op jit(solution)/shard_map/adamw/pallas_call | solution.py:393
  (65 shorter events, 13.9 us)
Async XLA Ops:
  219.8 16.1 %collective-permute-start = (bf16[7,3,48,256]{3,2,1,0:T(8,128)(2,1)}, bf16[7,3,48,256]{3,2,1,0:T(8,128)(2,1)S(1)}, u32[]{:S(2)}, u32[]{:S(2)}) collective-permute-start(bf16[7,3,48,256]{3,2,1,0:T(8,128)(2,1)} %bitcast.125), channel_id=1, source_target_pairs={{0,1},{1,2},{2,3},{3,4},{4,5},{5,6},{6,7},{7,0},{8,9},{9,10},{10,1... | collective-permute-start | bytes 1548296 | tf_op jit(solution)/shard_map/ppermute | solution.py:438
  223.1 24.0 %collective-permute-start.14 = (bf16[7,3,48,256]{3,2,1,0:T(8,128)(2,1)}, bf16[7,3,48,256]{3,2,1,0:T(8,128)(2,1)}, u32[]{:S(2)}, u32[]{:S(2)}) collective-permute-start(bf16[7,3,48,256]{3,2,1,0:T(8,128)(2,1)} %bitcast.129), channel_id=1, source_target_pairs={{0,1},{1,2},{2,3},{3,4},{4,5},{5,6},{6,7},{7,0},{8,9},{9,10},{10,1... | collective-permute-start | bytes 1548296 | tf_op jit(solution)/shard_map/ppermute | solution.py:441
  223.1 24.0 %collective-permute-start.20 = (bf16[7,3,48,256]{3,2,1,0:T(8,128)(2,1)}, bf16[7,3,48,256]{3,2,1,0:T(8,128)(2,1)}, u32[]{:S(2)}, u32[]{:S(2)}) collective-permute-start(bf16[7,3,48,256]{3,2,1,0:T(8,128)(2,1)} %bitcast.131), channel_id=1, source_target_pairs={{0,7},{1,0},{2,1},{3,2},{4,3},{5,4},{6,5},{7,6},{8,15},{9,8},{10,9... | collective-permute-start | bytes 1548296 | tf_op jit(solution)/shard_map/ppermute | solution.py:441
  235.9 22.1 %collective-permute-start.1 = (bf16[7,3,48,256]{3,2,1,0:T(8,128)(2,1)S(1)}, bf16[7,3,48,256]{3,2,1,0:T(8,128)(2,1)S(1)}, u32[]{:S(2)}, u32[]{:S(2)}) collective-permute-start(bf16[7,3,48,256]{3,2,1,0:T(8,128)(2,1)S(1)} %collective-permute-done.refs_0_), channel_id=1, source_target_pairs={{0,1},{1,2},{2,3},{3,4},{4,5},{5,6},{6,7},{7,0},{8,9},{9,10},{10,1... | collective-permute-start | bytes 1548296 | tf_op jit(solution)/shard_map/ppermute | solution.py:438
  236.0 22.1 %collective-permute-start.8 = (bf16[7,3,48,256]{3,2,1,0:T(8,128)(2,1)S(1)}, bf16[7,3,48,256]{3,2,1,0:T(8,128)(2,1)S(1)}, u32[]{:S(2)}, u32[]{:S(2)}) collective-permute-start(bf16[7,3,48,256]{3,2,1,0:T(8,128)(2,1)S(1)} %collective-permute-done.7.refs_1_), channel_id=1, source_target_pairs={{0,7},{1,0},{2,1},{3,2},{4,3},{5,4},{6,5},{7,6},{8,15},{9,8},{10,9... | collective-permute-start | bytes 1548296 | tf_op jit(solution)/shard_map/ppermute | solution.py:438
  247.1 28.1 %collective-permute-start.15 = (bf16[7,3,48,256]{3,2,1,0:T(8,128)(2,1)}, bf16[7,3,48,256]{3,2,1,0:T(8,128)(2,1)}, u32[]{:S(2)}, u32[]{:S(2)}) collective-permute-start(bf16[7,3,48,256]{3,2,1,0:T(8,128)(2,1)} %collective-permute-done.14.refs_2_), channel_id=1, source_target_pairs={{0,1},{1,2},{2,3},{3,4},{4,5},{5,6},{6,7},{7,0},{8,9},{9,10},{10,1... | collective-permute-start | bytes 1548296 | tf_op jit(solution)/shard_map/ppermute | solution.py:441
  247.1 28.2 %collective-permute-start.21 = (bf16[7,3,48,256]{3,2,1,0:T(8,128)(2,1)}, bf16[7,3,48,256]{3,2,1,0:T(8,128)(2,1)}, u32[]{:S(2)}, u32[]{:S(2)}) collective-permute-start(bf16[7,3,48,256]{3,2,1,0:T(8,128)(2,1)} %collective-permute-done.20.refs_3_), channel_id=1, source_target_pairs={{0,7},{1,0},{2,1},{3,2},{4,3},{5,4},{6,5},{7,6},{8,15},{9,8},{10,9... | collective-permute-start | bytes 1548296 | tf_op jit(solution)/shard_map/ppermute | solution.py:441
  258.1 25.5 %collective-permute-start.2 = (bf16[7,3,48,256]{3,2,1,0:T(8,128)(2,1)S(1)}, bf16[7,3,48,256]{3,2,1,0:T(8,128)(2,1)}, u32[]{:S(2)}, u32[]{:S(2)}) collective-permute-start(bf16[7,3,48,256]{3,2,1,0:T(8,128)(2,1)S(1)} %collective-permute-done.1.refs_0_), channel_id=1, source_target_pairs={{0,1},{1,2},{2,3},{3,4},{4,5},{5,6},{6,7},{7,0},{8,9},{9,10},{10,1... | collective-permute-start | bytes 1548296 | tf_op jit(solution)/shard_map/ppermute | solution.py:438
  258.1 21.7 %collective-permute-start.9 = (bf16[7,3,48,256]{3,2,1,0:T(8,128)(2,1)S(1)}, bf16[7,3,48,256]{3,2,1,0:T(8,128)(2,1)}, u32[]{:S(2)}, u32[]{:S(2)}) collective-permute-start(bf16[7,3,48,256]{3,2,1,0:T(8,128)(2,1)S(1)} %collective-permute-done.8.refs_1_), channel_id=1, source_target_pairs={{0,7},{1,0},{2,1},{3,2},{4,3},{5,4},{6,5},{7,6},{8,15},{9,8},{10,9... | collective-permute-start | bytes 1548296 | tf_op jit(solution)/shard_map/ppermute | solution.py:438
  275.2 16.2 %collective-permute-start.16 = (bf16[7,3,48,256]{3,2,1,0:T(8,128)(2,1)}, bf16[7,3,48,256]{3,2,1,0:T(8,128)(2,1)}, u32[]{:S(2)}, u32[]{:S(2)}) collective-permute-start(bf16[7,3,48,256]{3,2,1,0:T(8,128)(2,1)} %collective-permute-done.15.refs_2_), channel_id=1, source_target_pairs={{0,1},{1,2},{2,3},{3,4},{4,5},{5,6},{6,7},{7,0},{8,9},{9,10},{10,1... | collective-permute-start | bytes 1548296 | tf_op jit(solution)/shard_map/ppermute | solution.py:441
  279.8 22.3 %collective-permute-start.10 = (bf16[7,3,48,256]{3,2,1,0:T(8,128)(2,1)}, bf16[7,3,48,256]{3,2,1,0:T(8,128)(2,1)S(1)}, u32[]{:S(2)}, u32[]{:S(2)}) collective-permute-start(bf16[7,3,48,256]{3,2,1,0:T(8,128)(2,1)} %collective-permute-done.9.refs_1_), channel_id=1, source_target_pairs={{0,7},{1,0},{2,1},{3,2},{4,3},{5,4},{6,5},{7,6},{8,15},{9,8},{10,9... | collective-permute-start | bytes 1548296 | tf_op jit(solution)/shard_map/ppermute | solution.py:438
  283.5 22.1 %collective-permute-start.3 = (bf16[7,3,48,256]{3,2,1,0:T(8,128)(2,1)}, bf16[7,3,48,256]{3,2,1,0:T(8,128)(2,1)S(1)}, u32[]{:S(2)}, u32[]{:S(2)}) collective-permute-start(bf16[7,3,48,256]{3,2,1,0:T(8,128)(2,1)} %collective-permute-done.2.refs_0_), channel_id=1, source_target_pairs={{0,1},{1,2},{2,3},{3,4},{4,5},{5,6},{6,7},{7,0},{8,9},{9,10},{10,1... | collective-permute-start | bytes 1548296 | tf_op jit(solution)/shard_map/ppermute | solution.py:438
  291.4 24.6 %collective-permute-start.17 = (bf16[7,3,48,256]{3,2,1,0:T(8,128)(2,1)}, bf16[7,3,48,256]{3,2,1,0:T(8,128)(2,1)}, u32[]{:S(2)}, u32[]{:S(2)}) collective-permute-start(bf16[7,3,48,256]{3,2,1,0:T(8,128)(2,1)} %collective-permute-done.16.refs_2_), channel_id=1, source_target_pairs={{0,1},{1,2},{2,3},{3,4},{4,5},{5,6},{6,7},{7,0},{8,9},{9,10},{10,1... | collective-permute-start | bytes 1548296 | tf_op jit(solution)/shard_map/ppermute | solution.py:441
  291.5 24.7 %collective-permute-start.23 = (bf16[7,3,48,256]{3,2,1,0:T(8,128)(2,1)}, bf16[7,3,48,256]{3,2,1,0:T(8,128)(2,1)}, u32[]{:S(2)}, u32[]{:S(2)}) collective-permute-start(bf16[7,3,48,256]{3,2,1,0:T(8,128)(2,1)} %collective-permute-done.22.refs_3_), channel_id=1, source_target_pairs={{0,7},{1,0},{2,1},{3,2},{4,3},{5,4},{6,5},{7,6},{8,15},{9,8},{10,9... | collective-permute-start | bytes 1548296 | tf_op jit(solution)/shard_map/ppermute | solution.py:441
  302.1 27.6 %collective-permute-start.11 = (bf16[7,3,48,256]{3,2,1,0:T(8,128)(2,1)S(1)}, bf16[7,3,48,256]{3,2,1,0:T(8,128)(2,1)S(1)}, u32[]{:S(2)}, u32[]{:S(2)}) collective-permute-start(bf16[7,3,48,256]{3,2,1,0:T(8,128)(2,1)S(1)} %collective-permute-done.10.refs_1_), channel_id=1, source_target_pairs={{0,7},{1,0},{2,1},{3,2},{4,3},{5,4},{6,5},{7,6},{8,15},{9,8},{10,9... | collective-permute-start | bytes 1548296 | tf_op jit(solution)/shard_map/ppermute | solution.py:438
  305.6 26.1 %collective-permute-start.4 = (bf16[7,3,48,256]{3,2,1,0:T(8,128)(2,1)S(1)}, bf16[7,3,48,256]{3,2,1,0:T(8,128)(2,1)}, u32[]{:S(2)}, u32[]{:S(2)}) collective-permute-start(bf16[7,3,48,256]{3,2,1,0:T(8,128)(2,1)S(1)} %collective-permute-done.3.refs_0_), channel_id=1, source_target_pairs={{0,1},{1,2},{2,3},{3,4},{4,5},{5,6},{6,7},{7,0},{8,9},{9,10},{10,1... | collective-permute-start | bytes 1548296 | tf_op jit(solution)/shard_map/ppermute | solution.py:438
  316.0 26.1 %collective-permute-start.18 = (bf16[7,3,48,256]{3,2,1,0:T(8,128)(2,1)}, bf16[7,3,48,256]{3,2,1,0:T(8,128)(2,1)}, u32[]{:S(2)}, u32[]{:S(2)}) collective-permute-start(bf16[7,3,48,256]{3,2,1,0:T(8,128)(2,1)} %collective-permute-done.17.refs_2_), channel_id=1, source_target_pairs={{0,1},{1,2},{2,3},{3,4},{4,5},{5,6},{6,7},{7,0},{8,9},{9,10},{10,1... | collective-permute-start | bytes 1548296 | tf_op jit(solution)/shard_map/ppermute | solution.py:441
  316.1 26.1 %collective-permute-start.24 = (bf16[7,3,48,256]{3,2,1,0:T(8,128)(2,1)}, bf16[7,3,48,256]{3,2,1,0:T(8,128)(2,1)}, u32[]{:S(2)}, u32[]{:S(2)}) collective-permute-start(bf16[7,3,48,256]{3,2,1,0:T(8,128)(2,1)} %collective-permute-done.23.refs_3_), channel_id=1, source_target_pairs={{0,7},{1,0},{2,1},{3,2},{4,3},{5,4},{6,5},{7,6},{8,15},{9,8},{10,9... | collective-permute-start | bytes 1548296 | tf_op jit(solution)/shard_map/ppermute | solution.py:441
  329.7 26.1 %collective-permute-start.12 = (bf16[7,3,48,256]{3,2,1,0:T(8,128)(2,1)S(1)}, bf16[7,3,48,256]{3,2,1,0:T(8,128)(2,1)S(1)}, u32[]{:S(2)}, u32[]{:S(2)}) collective-permute-start(bf16[7,3,48,256]{3,2,1,0:T(8,128)(2,1)S(1)} %collective-permute-done.11.refs_1_), channel_id=1, source_target_pairs={{0,7},{1,0},{2,1},{3,2},{4,3},{5,4},{6,5},{7,6},{8,15},{9,8},{10,9... | collective-permute-start | bytes 1548296 | tf_op jit(solution)/shard_map/ppermute | solution.py:438
  331.7 26.1 %collective-permute-start.5 = (bf16[7,3,48,256]{3,2,1,0:T(8,128)(2,1)}, bf16[7,3,48,256]{3,2,1,0:T(8,128)(2,1)S(1)}, u32[]{:S(2)}, u32[]{:S(2)}) collective-permute-start(bf16[7,3,48,256]{3,2,1,0:T(8,128)(2,1)} %collective-permute-done.4.refs_0_), channel_id=1, source_target_pairs={{0,1},{1,2},{2,3},{3,4},{4,5},{5,6},{6,7},{7,0},{8,9},{9,10},{10,1... | collective-permute-start | bytes 1548296 | tf_op jit(solution)/shard_map/ppermute | solution.py:438
  342.1 26.1 %collective-permute-start.19 = (bf16[7,3,48,256]{3,2,1,0:T(8,128)(2,1)}, bf16[7,3,48,256]{3,2,1,0:T(8,128)(2,1)}, u32[]{:S(2)}, u32[]{:S(2)}) collective-permute-start(bf16[7,3,48,256]{3,2,1,0:T(8,128)(2,1)} %collective-permute-done.18.refs_2_), channel_id=1, source_target_pairs={{0,1},{1,2},{2,3},{3,4},{4,5},{5,6},{6,7},{7,0},{8,9},{9,10},{10,1... | collective-permute-start | bytes 1548296 | tf_op jit(solution)/shard_map/ppermute | solution.py:441
  342.3 26.0 %collective-permute-start.25 = (bf16[7,3,48,256]{3,2,1,0:T(8,128)(2,1)}, bf16[7,3,48,256]{3,2,1,0:T(8,128)(2,1)}, u32[]{:S(2)}, u32[]{:S(2)}) collective-permute-start(bf16[7,3,48,256]{3,2,1,0:T(8,128)(2,1)} %collective-permute-done.24.refs_3_), channel_id=1, source_target_pairs={{0,7},{1,0},{2,1},{3,2},{4,3},{5,4},{6,5},{7,6},{8,15},{9,8},{10,9... | collective-permute-start | bytes 1548296 | tf_op jit(solution)/shard_map/ppermute | solution.py:441
  355.8 22.9 %collective-permute-start.13 = (bf16[7,3,48,256]{3,2,1,0:T(8,128)(2,1)S(1)}, bf16[7,3,48,256]{3,2,1,0:T(8,128)(2,1)S(1)}, u32[]{:S(2)}, u32[]{:S(2)}) collective-permute-start(bf16[7,3,48,256]{3,2,1,0:T(8,128)(2,1)S(1)} %collective-permute-done.12.refs_1_), channel_id=1, source_target_pairs={{0,7},{1,0},{2,1},{3,2},{4,3},{5,4},{6,5},{7,6},{8,15},{9,8},{10,9... | collective-permute-start | bytes 1548296 | tf_op jit(solution)/shard_map/ppermute | solution.py:438
  357.8 20.9 %collective-permute-start.6 = (bf16[7,3,48,256]{3,2,1,0:T(8,128)(2,1)S(1)}, bf16[7,3,48,256]{3,2,1,0:T(8,128)(2,1)}, u32[]{:S(2)}, u32[]{:S(2)}) collective-permute-start(bf16[7,3,48,256]{3,2,1,0:T(8,128)(2,1)S(1)} %collective-permute-done.5.refs_0_), channel_id=1, source_target_pairs={{0,1},{1,2},{2,3},{3,4},{4,5},{5,6},{6,7},{7,0},{8,9},{9,10},{10,1... | collective-permute-start | bytes 1548296 | tf_op jit(solution)/shard_map/ppermute | solution.py:438
  (12 other events, 187.4 us)

commit v5 on v4

--- a/solution.py
+++ b/solution.py
@@ -28,7 +28,7 @@
 
 
 def kernel(cfg, x_in, dy_in, wg_in, wu_in, wd_in, own00, own01, own10, own11, got0, got1, factor, S, xh, a, aT, dh, hid, wg, wu, wd, recv,
-           load_sem, x_sem, own_sem, send_sem, recv_sem, credit, got_send, got_recv, ss, squares, sq_send, sq_recv):
+           load_sem, block_sem, x_sem, own_sem, send_sem, recv_sem, credit, got_send, got_recv, ss, squares, sq_send, sq_recv):
     n, T, D, F, tt, tb, comm = cfg["n"], cfg["T"], cfg["D"], cfg["F"], cfg["tt"], cfg["tb"], cfg["comm"]
     NB = F // BW
     NBLK = 2 * NB
@@ -38,21 +38,23 @@
     GB = NB * BR
     hr = BW // (2 * n)
     ncg = D // BW
-    gap = cfg["gap"]
-    ramp = max(NBLK - cfg["quick"], NB)
+    ramp, gap = min(3, NB - 1), cfg["gap"]
     def start(b):
-        return jnp.where(b < NB, 2 * b, jnp.where(b <= ramp, 2 * b + gap, b + ramp + gap))
+        return jnp.where(b <= ramp, 2 * b, jnp.where(b < NB, b + ramp, b + ramp + gap))
     LAST = NBLK - 1 + ramp + gap + n - 2
     ahead = ((LAST - 2, range(0, min(1, NB))), (LAST - 1, range(1, min(3, NB))), (LAST, range(3, min(6, NB))))
     me = lax.axis_index("dp")
     right, left = lax.rem(me + 1, n), lax.rem(me + n - 1, n)
     peers = [lax.rem(me + i, n) for i in range(1, n)]
 
-    loads = [pltpu.make_async_copy(s, d, load_sem.at[i]) for i, (s, d) in enumerate((
-        (x_in, xh), (wg_in.at[0], wg.at[0]), (wu_in.at[0], wu.at[0]), (wd_in.at[0], wd.at[0]), (dy_in, dh),
-        (wg_in.at[1], wg.at[1]), (wu_in.at[1], wu.at[1]), (wd_in.at[1], wd.at[1])))]
-    for c in loads[:3]:
-        c.start()
+    x_load = pltpu.make_async_copy(x_in, xh, load_sem.at[0])
+    dy_load = pltpu.make_async_copy(dy_in, dh, load_sem.at[1])
+    down_loads = [pltpu.make_async_copy(wd_in.at[l], wd.at[l], load_sem.at[2 + l]) for l in range(2)]
+    last_loads = [pltpu.make_async_copy(s.at[1], d.at[1], load_sem.at[4 + i]) for i, (s, d) in enumerate(((wg_in, wg), (wu_in, wu)))]
+    def block_loads(j):
+        cols = pl.ds(pl.multiple_of(j * BW, BW), BW)
+        return [pltpu.make_async_copy(s.at[0, :, cols], d.at[0, :, cols], block_sem.at[i, j]) for i, (s, d) in enumerate(((wg_in, wg), (wu_in, wu)))]
+    x_load.start()
     if comm:
         barrier = pltpu.get_barrier_semaphore()
         for p in peers:
@@ -67,11 +69,9 @@
 
     def block_of(r, s):
         z = r - s
-        y = z - gap
-        b = jnp.where(z < 2 * NB, lax.div(z, 2), jnp.where(y < 2 * ramp, lax.div(y, 2), y - ramp))
-        early = (z >= 0) & (z < 2 * NB) & (lax.rem(z, 2) == 0)
-        late = (y >= 2 * NB) & ((y >= 2 * ramp) | (lax.rem(y, 2) == 0))
-        return b, (early | late) & (b < NBLK)
+        b = jnp.where(z <= 2 * ramp, lax.div(z, 2), jnp.where(z < NB + ramp, z - ramp, z - ramp - gap))
+        live = ((z >= 0) & (z <= 2 * ramp) & (lax.rem(z, 2) == 0)) | ((z > 2 * ramp) & (z < NB + ramp)) | (z >= NB + ramp + gap)
+        return b, live & (b < NBLK)
 
     def hop(r, s, d):
         b, _ = block_of(r, s)
@@ -151,23 +151,30 @@
         lax.fori_loop(q, end, op, 0)
         return end
 
-    loads[0].wait()
-    loads[3].start()
-    loads[1].wait()
-    loads[2].wait()
-    def fwd(t, _):
+    x_load.wait()
+    for j in range(NB):
+        for c in block_loads(j):
+            c.start()
+    down_loads[0].start()
+    def norm_x(t, _):
         rows = pl.ds(pl.multiple_of(t * tt, tt), tt)
-        xw = xh[rows, :].astype(f32)
-        at = (xw * rms_scale(xw)).astype(bf16)
-        for j in range(NB):
-            cols = slice(j * BW, (j + 1) * BW)
+        wide = xh[rows, :].astype(f32)
+        a[rows, :] = (wide * rms_scale(wide)).astype(bf16)
+        return 0
+    lax.fori_loop(0, T // tt, norm_x, 0)
+    def fwd(j, _):
+        for c in block_loads(j):
+            c.wait()
+        cols = pl.ds(pl.multiple_of(j * BW, BW), BW)
+        for t in range(T // tt):
+            at = a[t * tt:(t + 1) * tt, :]
             g = mm(at, wg[0, :, cols])
             u = mm(at, wu[0, :, cols])
             S[pl.ds(pl.multiple_of(GB + j * T + t * tt, 16), tt), :] = (g * sigmoid(g) * u).astype(bf16)
         return 0
-    lax.fori_loop(0, T // tt, fwd, 0)
-    loads[3].wait()
-    for c in loads[4:]:
+    lax.fori_loop(0, NB, fwd, 0)
+    down_loads[0].wait()
+    for c in last_loads + [dy_load, down_loads[1]]:
         c.start()
     def fwd_down(t, _):
         rows = pl.ds(pl.multiple_of(t * tt, tt), tt)
@@ -179,7 +186,7 @@
         a[rows, :] = a1
         aT[:, rows] = a1.T
         return 0
-    lax.fori_loop(0, T // tt, fwd_down, 0)
+    lax.fori_loop(0, T // tt, fwd_down, 0, unroll=cfg["unroll"])
 
     def block(l, j, dg0, du0, b, q, pace, pace2):
         cols = pl.ds(pl.multiple_of(j * BW, BW), BW)
@@ -214,42 +221,46 @@
         down(mm(hid[...], dh[...], TN).astype(bf16))
         return q
 
-    for c in loads[4:]:
+    for c in last_loads + [dy_load, down_loads[1]]:
         c.wait()
-    def last_layer(j, q):
-        return block(1, j, GB + j * 2 * T, GB + j * 2 * T + T, j, q, jnp.where(j <= 2, n, cfg["pace"][0]), jnp.where(j <= 2, n, cfg["pace"][1]))
     if comm:
         pl.semaphore_wait(barrier, n - 1)
-    q = lax.fori_loop(0, NB, last_layer, 0)
-
-    def d_input(t, q):
-        q = ops(q, cfg["pace"][2], NB)
-        rows = pl.ds(pl.multiple_of(t * tt, tt), tt)
-        dg = jnp.concatenate([S[pl.ds(pl.multiple_of(GB + j * 2 * T + t * tt, 16), tt), :] for j in range(NB)], axis=1)
-        du = jnp.concatenate([S[pl.ds(pl.multiple_of(GB + j * 2 * T + T + t * tt, 16), tt), :] for j in range(NB)], axis=1)
-        da = (mm(dg, wg[1], NT).astype(bf16).astype(f32) + mm(du, wu[1], NT).astype(bf16).astype(f32)).astype(bf16).astype(f32)
-        wide = xh[rows, :].astype(f32)
-        scale = rms_scale(wide)
-        dot = jnp.sum(da * wide, -1, keepdims=True)
-        dw = da * scale - wide * (scale * scale * scale * dot * (1.0 / D))
-        dh[rows, :] = (dh[rows, :].astype(f32) + dw.astype(bf16).astype(f32)).astype(bf16)
-        pltpu.make_async_copy(x_in.at[rows, :], xh.at[rows, :], x_sem).start()
+
+    def between(q):
+        def d_input(t, q):
+            q = ops(q, cfg["pace"][2], NB)
+            rows = pl.ds(pl.multiple_of(t * tt, tt), tt)
+            dg = jnp.concatenate([S[pl.ds(pl.multiple_of(GB + j * 2 * T + t * tt, 16), tt), :] for j in range(NB)], axis=1)
+            du = jnp.concatenate([S[pl.ds(pl.multiple_of(GB + j * 2 * T + T + t * tt, 16), tt), :] for j in range(NB)], axis=1)
+            da = (mm(dg, wg[1], NT).astype(bf16).astype(f32) + mm(du, wu[1], NT).astype(bf16).astype(f32)).astype(bf16).astype(f32)
+            wide = xh[rows, :].astype(f32)
+            scale = rms_scale(wide)
+            dot = jnp.sum(da * wide, -1, keepdims=True)
+            dw = da * scale - wide * (scale * scale * scale * dot * (1.0 / D))
+            dh[rows, :] = (dh[rows, :].astype(f32) + dw.astype(bf16).astype(f32)).astype(bf16)
+            pltpu.make_async_copy(x_in.at[rows, :], xh.at[rows, :], x_sem).start()
+            return q
+        q = lax.fori_loop(0, T // tt, d_input, q)
+        def renorm(t, q):
+            rows = pl.ds(pl.multiple_of(t * tt, tt), tt)
+            wide = xh[rows, :].astype(f32)
+            a0 = (wide * rms_scale(wide)).astype(bf16)
+            a[rows, :] = a0
+            aT[:, rows] = a0.T
+            return q
+        pltpu.make_async_copy(x_in, xh, x_sem).wait()
+        q = ops(q, 2, NB)
+        lax.fori_loop(0, T // tt, renorm, 0)
         return q
-    q = lax.fori_loop(0, T // tt, d_input, q)
-    def renorm(t, q):
-        rows = pl.ds(pl.multiple_of(t * tt, tt), tt)
-        wide = xh[rows, :].astype(f32)
-        a0 = (wide * rms_scale(wide)).astype(bf16)
-        a[rows, :] = a0
-        aT[:, rows] = a0.T
-        return q
-    pltpu.make_async_copy(x_in, xh, x_sem).wait()
-    q = ops(q, 2, NB)
-    lax.fori_loop(0, T // tt, renorm, 0)
-
-    def first_layer(j, q):
-        return block(0, j, 2 * GB, 2 * GB + T, NB + j, q, cfg["pace"][3], cfg["pace"][3])
-    q = lax.fori_loop(0, NB, first_layer, q)
+
+    def blocks(b, q):
+        q = lax.cond(b == NB, between, lambda q: q, q)
+        last = b < NB
+        dg0 = jnp.where(last, GB + b * 2 * T, 2 * GB)
+        pace = cfg["pace"]
+        return block(jnp.where(last, 1, 0), jnp.where(last, b, b - NB), dg0, dg0 + T, b, q,
+                     jnp.where(b <= 2, n, jnp.where(last, pace[0], pace[3])), jnp.where(b <= 2, n, jnp.where(last, pace[1], pace[3])))
+    q = lax.fori_loop(0, NBLK, blocks, 0)
     if comm:
         lax.fori_loop(q, (LAST + 2) * n, op, 0)
         copies = [
@@ -266,7 +277,7 @@
         for r in range(LAST - RB + 2, LAST + 1):
             for s in range(n - 1):
                 for b in range(NBLK):
-                    if r - s == (2 * b if b < NB else 2 * b + gap if b <= ramp else b + ramp + gap):
+                    if r - s == (2 * b if b <= ramp else b + ramp if b < NB else b + ramp + gap):
                         for d in range(2):
                             hop(r, s, d).wait_send()
         for i, p in enumerate(peers):
@@ -293,14 +304,14 @@
         for c in cps: c.wait()
 
 
-def k1(x, dy, wg, wu, wd, n, tt=512, tb=512, comm=True, cid=0, pace=(5, 5, 6, 6), gap=0, quick=4):
+def k1(x, dy, wg, wu, wd, n, tt=512, tb=512, comm=True, cid=0, pace=(4, 5, 4, 6), gap=2, unroll=True):
     T, D = x.shape
     F = wg.shape[2]
     NB = F // BW
     NBLK = 2 * NB
     H = D // (2 * n); CH = 3 * H
     GB = NB * 3 * D
-    cfg = dict(n=n, T=T, D=D, F=F, tt=min(tt, T), tb=min(tb, T), comm=comm, pace=pace, gap=gap, quick=quick)
+    cfg = dict(n=n, T=T, D=D, F=F, tt=min(tt, T), tb=min(tb, T), comm=comm, pace=pace, gap=gap, unroll=unroll)
     any_ = pl.BlockSpec(memory_space=pl.ANY)
     flops = 18 * 2 * T * D * F
     return pl.pallas_call(
@@ -314,7 +325,7 @@
             pltpu.VMEM((T, BW), bf16),
             pltpu.VMEM((2, D, F), bf16), pltpu.VMEM((2, D, F), bf16), pltpu.VMEM((2, F, D), bf16),
             pltpu.VMEM((2, RB * (n - 1), CH, BW), bf16),
-            pltpu.SemaphoreType.DMA((8,)), pltpu.SemaphoreType.DMA, pltpu.SemaphoreType.DMA((2, NBLK)),
+            pltpu.SemaphoreType.DMA((6,)), pltpu.SemaphoreType.DMA((2, NB)), pltpu.SemaphoreType.DMA, pltpu.SemaphoreType.DMA((2, NBLK)),
             pltpu.SemaphoreType.DMA((2, RB * (n - 1))), pltpu.SemaphoreType.DMA((2, RB * (n - 1))), pltpu.SemaphoreType.REGULAR((2,)),
             pltpu.SemaphoreType.DMA((2, NB)), pltpu.SemaphoreType.DMA((2, NB)),
             pltpu.VMEM((8, 128), f32), pltpu.VMEM((n, 8, 128), f32), pltpu.SemaphoreType.DMA((n - 1,)), pltpu.SemaphoreType.DMA((n,)),
@@ -439,7 +450,8 @@
             if s < n - 1:
                 for d in range(2):
                     ahead.append(lax.ppermute(last[d], "dp", to[d]))
-            outs = adam_call(factor, waiting, ins, outs)
+            for part in [waiting] if s < n - 1 else [waiting[:2], waiting[2:]]:
+                outs = adam_call(factor, part, ins, outs)
             waiting = pieces(0, first, s) + (pieces(1, ahead, s + 1) if ahead else [])
             last = ahead
         outs = adam_call(factor, waiting, ins, outs)

time: 387 us -> 386 us (level)
    pallas_call x1, Pallas kernels: 219 us -> 214 us  [k1(): pl.pallas_call(functools.partial(kernel, cfg), out_shape=(jax.ShapeDtypeS...]
    pallas_call x8 -> x9, Pallas kernels: 82.4 us -> 85.7 us  [adam_call(): pl.pallas_call(functools.partial(adam_kernel, layers), grid_spec=pltpu.Pr...]
  transfers between devices with their start and end apart: 26 -> 26, of which waited for: 5 -> 6; matrix products, arithmetic and copies ran while one was open for 1% -> 1% of each run, Pallas kernels for 20% -> 20%
where the time goes in v5:
time: 386 us
  Pallas kernels  300 us (78%)
  starting transfers between devices  41.5 us (11%)
  waiting for transfers between devices  36.4 us (9%)
  other arithmetic  4.36 us (1%)
    pallas_call x1, Pallas kernels, k1(): pl.pallas_call(functools.partial(kernel, cfg), out_shape=(jax.ShapeDtypeS...  214 us
    pallas_call x9, Pallas kernels, adam_call(): pl.pallas_call(functools.partial(adam_kernel, layers), grid_spec=pltpu.Pr...  85.7 us
    ppermute x14, waiting for transfers between devices, step(): first[d] = lax.ppermute(first[d], 'dp', to[d])  25.7 us
    ppermute x14, starting transfers between devices, step(): first[d] = lax.ppermute(first[d], 'dp', to[d])  21.3 us
    ppermute x12, starting transfers between devices, step(): ahead.append(lax.ppermute(last[d], 'dp', to[d]))  20.2 us
    ppermute x12, waiting for transfers between devices, step(): ahead.append(lax.ppermute(last[d], 'dp', to[d]))  10.7 us
  transfers between devices with their start and end apart: 26, of which 6 were waited for; matrix products, arithmetic and copies ran while one was open for 1% of the time, Pallas kernels for 20%

profile of v5, /device:TPU:22, one launch (start us, length us, event | category | flops | bytes accessed | tf_op | source)
XLA Modules:
  0.0 385.9 jit_solution(8321537439687949774)
XLA Ops:
  0.6 214.2 %grads.1 = (bf16[7,144,256]{2,1,0:T(8,128)(2,1)}, bf16[7,144,256]{2,1,0:T(8,128)(2,1)}, bf16[7,144,256]{2,1,0:T(8,128)(2,1)}, bf16[7,144,256]{2,1,0:T(8,128)(2,1...) custom-call(bf16[2048,768]{1,0:T(8,128)(2,1)} %bitcast.142, ...), custom_call_target="tpu_custom_call" | custom-call | flops 101468602368 | bytes 40000000 | tf_op jit(solution)/shard_map/grads/pallas_call | solution.py:317
  218.2 3.2 collective-permute-start.20
  221.4 9.6 %collective-permute-done.refs_0_ = bf16[7,3,48,256]{3,2,1,0:T(8,128)(2,1)S(1)} collective-permute-done((bf16[7,3,48,256]{3,2,1,0:T(8,128)(2,1)}, bf16[7,3,48,256]{3,2,1,0:T(8,128)(2,1)S(1)}, u32[]{:S(2)}, u32[]{:S(2)}) %collective-permute-start) | collective-permute-done | bytes 516128 | tf_op jit(solution)/shard_map/ppermute | solution.py:449
  231.0 3.2 collective-permute-start.8
  236.2 5.9 %collective-permute-done.14.refs_2_ = bf16[7,3,48,256]{3,2,1,0:T(8,128)(2,1)S(1)} collective-permute-done((bf16[7,3,48,256]{3,2,1,0:T(8,128)(2,1)}, bf16[7,3,48,256]{3,2,1,0:T(8,128)(2,1)S(1)}, u32[]{:S(2)}, u32[]{:S(2)}) %collective-permute-start.14) | collective-permute-done | bytes 516128 | tf_op jit(solution)/shard_map/ppermute | solution.py:452
  242.1 3.3 collective-permute-start.21
  245.4 7.7 %collective-permute-done.1.refs_0_ = bf16[7,3,48,256]{3,2,1,0:T(8,128)(2,1)S(1)} collective-permute-done((bf16[7,3,48,256]{3,2,1,0:T(8,128)(2,1)S(1)}, bf16[7,3,48,256]{3,2,1,0:T(8,128)(2,1)S(1)}, u32[]{:S(2)}, u32[]{:S(2)}) %collective-permute-start.1) | collective-permute-done | bytes 516128 | tf_op jit(solution)/shard_map/ppermute | solution.py:449
  259.5 4.8 %collective-permute-done.15.refs_2_ = bf16[7,3,48,256]{3,2,1,0:T(8,128)(2,1)} collective-permute-done((bf16[7,3,48,256]{3,2,1,0:T(8,128)(2,1)S(1)}, bf16[7,3,48,256]{3,2,1,0:T(8,128)(2,1)}, u32[]{:S(2)}, u32[]{:S(2)}) %collective-permute-start.15) | collective-permute-done | bytes 516128 | tf_op jit(solution)/shard_map/ppermute | solution.py:452
  264.3 3.2 collective-permute-start.22
  267.5 7.3 %collective-permute-done.9.refs_1_ = bf16[7,3,48,256]{3,2,1,0:T(8,128)(2,1)} collective-permute-done((bf16[7,3,48,256]{3,2,1,0:T(8,128)(2,1)S(1)}, bf16[7,3,48,256]{3,2,1,0:T(8,128)(2,1)}, u32[]{:S(2)}, u32[]{:S(2)}) %collective-permute-start.9) | collective-permute-done | bytes 516128 | tf_op jit(solution)/shard_map/ppermute | solution.py:449
  274.8 3.8 collective-permute-start.10
  278.6 13.8 %adamw.9 = (bf16[2,16,48,1792]{3,2,1,0:T(8,128)(2,1)}, bf16[2,16,48,1792]{3,2,1,0:T(8,128)(2,1)}, bf16[2,7,16,16,768]{4,3,2,1,0:T(8,128)(2,1)}, f32[2,16,48,1792...) custom-call(s32[6]{0:T(128)} %stack.112.idx_ref, ...), custom_call_target="tpu_custom_call" | custom-call | flops 6000000000 | bytes 34062336 | tf_op jit(solution)/shard_map/adamw/pallas_call | solution.py:404
  292.6 3.3 collective-permute-start.23
  297.0 3.7 collective-permute-start.11
  300.7 10.2 %adamw.10 = (bf16[2,16,48,1792]{3,2,1,0:T(8,128)(2,1)}, bf16[2,16,48,1792]{3,2,1,0:T(8,128)(2,1)}, bf16[2,7,16,16,768]{4,3,2,1,0:T(8,128)(2,1)}, f32[2,16,48,179...) custom-call(s32[4]{0:T(128)} %pad_add_fusion.6.idx_ref, ...), custom_call_target="tpu_custom_call", output_to_operand_aliasing={{0}: (15, {}), {1}: (16, {}), {2}: (17, {}), {3}: (18, {}),... | custom-call | flops 4000000000 | bytes 22708224 | tf_op jit(solution)/shard_map/adamw/pallas_call | solution.py:404
  311.0 10.3 %adamw.11 = (bf16[2,16,48,1792]{3,2,1,0:T(8,128)(2,1)}, bf16[2,16,48,1792]{3,2,1,0:T(8,128)(2,1)}, bf16[2,7,16,16,768]{4,3,2,1,0:T(8,128)(2,1)}, f32[2,16,48,179...) custom-call(s32[4]{0:T(128)} %pad_add_fusion.5.idx_ref, ...), custom_call_target="tpu_custom_call", output_to_operand_aliasing={{0}: (15, {}), {1}: (16, {}), {2}: (17, {}), {3}: (18, {}),... | custom-call | flops 4000000000 | bytes 22708224 | tf_op jit(solution)/shard_map/adamw/pallas_call | solution.py:404
  321.4 3.4 collective-permute-start.24
  326.8 10.2 %adamw.12 = (bf16[2,16,48,1792]{3,2,1,0:T(8,128)(2,1)}, bf16[2,16,48,1792]{3,2,1,0:T(8,128)(2,1)}, bf16[2,7,16,16,768]{4,3,2,1,0:T(8,128)(2,1)}, f32[2,16,48,179...) custom-call(s32[4]{0:T(128)} %pad_add_fusion.4.idx_ref, ...), custom_call_target="tpu_custom_call", output_to_operand_aliasing={{0}: (15, {}), {1}: (16, {}), {2}: (17, {}), {3}: (18, {}),... | custom-call | flops 4000000000 | bytes 22708224 | tf_op jit(solution)/shard_map/adamw/pallas_call | solution.py:404
  337.1 10.3 %adamw.13 = (bf16[2,16,48,1792]{3,2,1,0:T(8,128)(2,1)}, bf16[2,16,48,1792]{3,2,1,0:T(8,128)(2,1)}, bf16[2,7,16,16,768]{4,3,2,1,0:T(8,128)(2,1)}, f32[2,16,48,179...) custom-call(s32[4]{0:T(128)} %pad_add_fusion.3.idx_ref, ...), custom_call_target="tpu_custom_call", output_to_operand_aliasing={{0}: (15, {}), {1}: (16, {}), {2}: (17, {}), {3}: (18, {}),... | custom-call | flops 4000000000 | bytes 22708224 | tf_op jit(solution)/shard_map/adamw/pallas_call | solution.py:404
  347.6 3.3 collective-permute-start.25
  353.0 10.2 %adamw.14 = (bf16[2,16,48,1792]{3,2,1,0:T(8,128)(2,1)}, bf16[2,16,48,1792]{3,2,1,0:T(8,128)(2,1)}, bf16[2,7,16,16,768]{4,3,2,1,0:T(8,128)(2,1)}, f32[2,16,48,179...) custom-call(s32[4]{0:T(128)} %pad_add_fusion.2.idx_ref, ...), custom_call_target="tpu_custom_call", output_to_operand_aliasing={{0}: (15, {}), {1}: (16, {}), {2}: (17, {}), {3}: (18, {}),... | custom-call | flops 4000000000 | bytes 22708224 | tf_op jit(solution)/shard_map/adamw/pallas_call | solution.py:404
  363.2 6.9 %adamw.15 = (bf16[2,16,48,1792]{3,2,1,0:T(8,128)(2,1)}, bf16[2,16,48,1792]{3,2,1,0:T(8,128)(2,1)}, bf16[2,7,16,16,768]{4,3,2,1,0:T(8,128)(2,1)}, f32[2,16,48,179...) custom-call(s32[2]{0:T(128)} %pad_add_fusion.1.idx_ref, ...), custom_call_target="tpu_custom_call", output_to_operand_aliasing={{0}: (13, {}), {1}: (14, {}), {2}: (15, {}), {3}: (16, {}),... | custom-call | flops 2000000000 | bytes 11354112 | tf_op jit(solution)/shard_map/adamw/pallas_call | solution.py:404
  371.0 6.9 %adamw.16 = (bf16[2,16,48,1792]{3,2,1,0:T(8,128)(2,1)}, bf16[2,16,48,1792]{3,2,1,0:T(8,128)(2,1)}, bf16[2,7,16,16,768]{4,3,2,1,0:T(8,128)(2,1)}, f32[2,16,48,179...) custom-call(s32[2]{0:T(128)} %pad_add_fusion.idx_ref, ...), custom_call_target="tpu_custom_call", output_to_operand_aliasing={{0}: (13, {}), {1}: (14, {}), {2}: (15, {}), {3}: (16, {}),... | custom-call | flops 2000000000 | bytes 11354112 | tf_op jit(solution)/shard_map/adamw/pallas_call | solution.py:404
  378.8 6.9 %adamw.17 = (bf16[2,16,48,1792]{3,2,1,0:T(8,128)(2,1)}, bf16[2,16,48,1792]{3,2,1,0:T(8,128)(2,1)}, bf16[2,7,16,16,768]{4,3,2,1,0:T(8,128)(2,1)}, f32[2,16,48,179...) custom-call(s32[2]{0:T(128)} %pad_add_fusion.idx_ref, ...), custom_call_target="tpu_custom_call", output_to_operand_aliasing={{0}: (13, {}), {1}: (14, {}), {2}: (15, {}), {3}: (16, {}),... | custom-call | flops 2000000000 | bytes 11354112 | tf_op jit(solution)/shard_map/adamw/pallas_call | solution.py:404
  (68 shorter events, 19.1 us)
Async XLA Ops:
  218.2 23.9 %collective-permute-start.14 = (bf16[7,3,48,256]{3,2,1,0:T(8,128)(2,1)}, bf16[7,3,48,256]{3,2,1,0:T(8,128)(2,1)S(1)}, u32[]{:S(2)}, u32[]{:S(2)}) collective-permute-start(bf16[7,3,48,256]{3,2,1,0:T(8,128)(2,1)} %bitcast.138), channel_id=1, source_target_pairs={{0,1},{1,2},{2,3},{3,4},{4,5},{5,6},{6,7},{7,0},{8,9},{9,10},{10,1... | collective-permute-start | bytes 1548296 | tf_op jit(solution)/shard_map/ppermute | solution.py:452
  218.2 23.9 %collective-permute-start.20 = (bf16[7,3,48,256]{3,2,1,0:T(8,128)(2,1)}, bf16[7,3,48,256]{3,2,1,0:T(8,128)(2,1)}, u32[]{:S(2)}, u32[]{:S(2)}) collective-permute-start(bf16[7,3,48,256]{3,2,1,0:T(8,128)(2,1)} %bitcast.140), channel_id=1, source_target_pairs={{0,7},{1,0},{2,1},{3,2},{4,3},{5,4},{6,5},{7,6},{8,15},{9,8},{10,9... | collective-permute-start | bytes 1548296 | tf_op jit(solution)/shard_map/ppermute | solution.py:452
  231.0 22.1 %collective-permute-start.1 = (bf16[7,3,48,256]{3,2,1,0:T(8,128)(2,1)S(1)}, bf16[7,3,48,256]{3,2,1,0:T(8,128)(2,1)S(1)}, u32[]{:S(2)}, u32[]{:S(2)}) collective-permute-start(bf16[7,3,48,256]{3,2,1,0:T(8,128)(2,1)S(1)} %collective-permute-done.refs_0_), channel_id=1, source_target_pairs={{0,1},{1,2},{2,3},{3,4},{4,5},{5,6},{6,7},{7,0},{8,9},{9,10},{10,1... | collective-permute-start | bytes 1548296 | tf_op jit(solution)/shard_map/ppermute | solution.py:449
  231.0 22.1 %collective-permute-start.8 = (bf16[7,3,48,256]{3,2,1,0:T(8,128)(2,1)S(1)}, bf16[7,3,48,256]{3,2,1,0:T(8,128)(2,1)S(1)}, u32[]{:S(2)}, u32[]{:S(2)}) collective-permute-start(bf16[7,3,48,256]{3,2,1,0:T(8,128)(2,1)S(1)} %collective-permute-done.7.refs_1_), channel_id=1, source_target_pairs={{0,7},{1,0},{2,1},{3,2},{4,3},{5,4},{6,5},{7,6},{8,15},{9,8},{10,9... | collective-permute-start | bytes 1548296 | tf_op jit(solution)/shard_map/ppermute | solution.py:449
  242.1 22.2 %collective-permute-start.15 = (bf16[7,3,48,256]{3,2,1,0:T(8,128)(2,1)S(1)}, bf16[7,3,48,256]{3,2,1,0:T(8,128)(2,1)}, u32[]{:S(2)}, u32[]{:S(2)}) collective-permute-start(bf16[7,3,48,256]{3,2,1,0:T(8,128)(2,1)S(1)} %collective-permute-done.14.refs_2_), channel_id=1, source_target_pairs={{0,1},{1,2},{2,3},{3,4},{4,5},{5,6},{6,7},{7,0},{8,9},{9,10},{10,1... | collective-permute-start | bytes 1548296 | tf_op jit(solution)/shard_map/ppermute | solution.py:452
  242.1 22.2 %collective-permute-start.21 = (bf16[7,3,48,256]{3,2,1,0:T(8,128)(2,1)}, bf16[7,3,48,256]{3,2,1,0:T(8,128)(2,1)}, u32[]{:S(2)}, u32[]{:S(2)}) collective-permute-start(bf16[7,3,48,256]{3,2,1,0:T(8,128)(2,1)} %collective-permute-done.20.refs_3_), channel_id=1, source_target_pairs={{0,7},{1,0},{2,1},{3,2},{4,3},{5,4},{6,5},{7,6},{8,15},{9,8},{10,9... | collective-permute-start | bytes 1548296 | tf_op jit(solution)/shard_map/ppermute | solution.py:452
  253.1 25.5 %collective-permute-start.2 = (bf16[7,3,48,256]{3,2,1,0:T(8,128)(2,1)S(1)}, bf16[7,3,48,256]{3,2,1,0:T(8,128)(2,1)}, u32[]{:S(2)}, u32[]{:S(2)}) collective-permute-start(bf16[7,3,48,256]{3,2,1,0:T(8,128)(2,1)S(1)} %collective-permute-done.1.refs_0_), channel_id=1, source_target_pairs={{0,1},{1,2},{2,3},{3,4},{4,5},{5,6},{6,7},{7,0},{8,9},{9,10},{10,1... | collective-permute-start | bytes 1548296 | tf_op jit(solution)/shard_map/ppermute | solution.py:449
  253.1 21.6 %collective-permute-start.9 = (bf16[7,3,48,256]{3,2,1,0:T(8,128)(2,1)S(1)}, bf16[7,3,48,256]{3,2,1,0:T(8,128)(2,1)}, u32[]{:S(2)}, u32[]{:S(2)}) collective-permute-start(bf16[7,3,48,256]{3,2,1,0:T(8,128)(2,1)S(1)} %collective-permute-done.8.refs_1_), channel_id=1, source_target_pairs={{0,7},{1,0},{2,1},{3,2},{4,3},{5,4},{6,5},{7,6},{8,15},{9,8},{10,9... | collective-permute-start | bytes 1548296 | tf_op jit(solution)/shard_map/ppermute | solution.py:449
  264.3 28.1 %collective-permute-start.16 = (bf16[7,3,48,256]{3,2,1,0:T(8,128)(2,1)}, bf16[7,3,48,256]{3,2,1,0:T(8,128)(2,1)}, u32[]{:S(2)}, u32[]{:S(2)}) collective-permute-start(bf16[7,3,48,256]{3,2,1,0:T(8,128)(2,1)} %collective-permute-done.15.refs_2_), channel_id=1, source_target_pairs={{0,1},{1,2},{2,3},{3,4},{4,5},{5,6},{6,7},{7,0},{8,9},{9,10},{10,1... | collective-permute-start | bytes 1548296 | tf_op jit(solution)/shard_map/ppermute | solution.py:452
  264.3 28.2 %collective-permute-start.22 = (bf16[7,3,48,256]{3,2,1,0:T(8,128)(2,1)}, bf16[7,3,48,256]{3,2,1,0:T(8,128)(2,1)}, u32[]{:S(2)}, u32[]{:S(2)}) collective-permute-start(bf16[7,3,48,256]{3,2,1,0:T(8,128)(2,1)} %collective-permute-done.21.refs_3_), channel_id=1, source_target_pairs={{0,7},{1,0},{2,1},{3,2},{4,3},{5,4},{6,5},{7,6},{8,15},{9,8},{10,9... | collective-permute-start | bytes 1548296 | tf_op jit(solution)/shard_map/ppermute | solution.py:452
  274.8 22.2 %collective-permute-start.10 = (bf16[7,3,48,256]{3,2,1,0:T(8,128)(2,1)}, bf16[7,3,48,256]{3,2,1,0:T(8,128)(2,1)}, u32[]{:S(2)}, u32[]{:S(2)}) collective-permute-start(bf16[7,3,48,256]{3,2,1,0:T(8,128)(2,1)} %collective-permute-done.9.refs_1_), channel_id=1, source_target_pairs={{0,7},{1,0},{2,1},{3,2},{4,3},{5,4},{6,5},{7,6},{8,15},{9,8},{10,9... | collective-permute-start | bytes 1548296 | tf_op jit(solution)/shard_map/ppermute | solution.py:449
  278.6 22.1 %collective-permute-start.3 = (bf16[7,3,48,256]{3,2,1,0:T(8,128)(2,1)}, bf16[7,3,48,256]{3,2,1,0:T(8,128)(2,1)}, u32[]{:S(2)}, u32[]{:S(2)}) collective-permute-start(bf16[7,3,48,256]{3,2,1,0:T(8,128)(2,1)} %collective-permute-done.2.refs_0_), channel_id=1, source_target_pairs={{0,1},{1,2},{2,3},{3,4},{4,5},{5,6},{6,7},{7,0},{8,9},{9,10},{10,1... | collective-permute-start | bytes 1548296 | tf_op jit(solution)/shard_map/ppermute | solution.py:449
  292.4 28.9 %collective-permute-start.17 = (bf16[7,3,48,256]{3,2,1,0:T(8,128)(2,1)}, bf16[7,3,48,256]{3,2,1,0:T(8,128)(2,1)}, u32[]{:S(2)}, u32[]{:S(2)}) collective-permute-start(bf16[7,3,48,256]{3,2,1,0:T(8,128)(2,1)} %collective-permute-done.16.refs_2_), channel_id=1, source_target_pairs={{0,1},{1,2},{2,3},{3,4},{4,5},{5,6},{6,7},{7,0},{8,9},{9,10},{10,1... | collective-permute-start | bytes 1548296 | tf_op jit(solution)/shard_map/ppermute | solution.py:452
  292.6 28.9 %collective-permute-start.23 = (bf16[7,3,48,256]{3,2,1,0:T(8,128)(2,1)}, bf16[7,3,48,256]{3,2,1,0:T(8,128)(2,1)S(1)}, u32[]{:S(2)}, u32[]{:S(2)}) collective-permute-start(bf16[7,3,48,256]{3,2,1,0:T(8,128)(2,1)} %collective-permute-done.22.refs_3_), channel_id=1, source_target_pairs={{0,7},{1,0},{2,1},{3,2},{4,3},{5,4},{6,5},{7,6},{8,15},{9,8},{10,9... | collective-permute-start | bytes 1548296 | tf_op jit(solution)/shard_map/ppermute | solution.py:452
  297.0 27.8 %collective-permute-start.11 = (bf16[7,3,48,256]{3,2,1,0:T(8,128)(2,1)}, bf16[7,3,48,256]{3,2,1,0:T(8,128)(2,1)S(1)}, u32[]{:S(2)}, u32[]{:S(2)}) collective-permute-start(bf16[7,3,48,256]{3,2,1,0:T(8,128)(2,1)} %collective-permute-done.10.refs_1_), channel_id=1, source_target_pairs={{0,7},{1,0},{2,1},{3,2},{4,3},{5,4},{6,5},{7,6},{8,15},{9,8},{10,9... | collective-permute-start | bytes 1548296 | tf_op jit(solution)/shard_map/ppermute | solution.py:449
  300.7 26.0 %collective-permute-start.4 = (bf16[7,3,48,256]{3,2,1,0:T(8,128)(2,1)}, bf16[7,3,48,256]{3,2,1,0:T(8,128)(2,1)S(1)}, u32[]{:S(2)}, u32[]{:S(2)}) collective-permute-start(bf16[7,3,48,256]{3,2,1,0:T(8,128)(2,1)} %collective-permute-done.3.refs_0_), channel_id=1, source_target_pairs={{0,1},{1,2},{2,3},{3,4},{4,5},{5,6},{6,7},{7,0},{8,9},{9,10},{10,1... | collective-permute-start | bytes 1548296 | tf_op jit(solution)/shard_map/ppermute | solution.py:449
  321.3 26.1 %collective-permute-start.18 = (bf16[7,3,48,256]{3,2,1,0:T(8,128)(2,1)}, bf16[7,3,48,256]{3,2,1,0:T(8,128)(2,1)}, u32[]{:S(2)}, u32[]{:S(2)}) collective-permute-start(bf16[7,3,48,256]{3,2,1,0:T(8,128)(2,1)} %collective-permute-done.17.refs_2_), channel_id=1, source_target_pairs={{0,1},{1,2},{2,3},{3,4},{4,5},{5,6},{6,7},{7,0},{8,9},{9,10},{10,1... | collective-permute-start | bytes 1548296 | tf_op jit(solution)/shard_map/ppermute | solution.py:452
  321.4 26.2 %collective-permute-start.24 = (bf16[7,3,48,256]{3,2,1,0:T(8,128)(2,1)S(1)}, bf16[7,3,48,256]{3,2,1,0:T(8,128)(2,1)}, u32[]{:S(2)}, u32[]{:S(2)}) collective-permute-start(bf16[7,3,48,256]{3,2,1,0:T(8,128)(2,1)S(1)} %collective-permute-done.23.refs_3_), channel_id=1, source_target_pairs={{0,7},{1,0},{2,1},{3,2},{4,3},{5,4},{6,5},{7,6},{8,15},{9,8},{10,9... | collective-permute-start | bytes 1548296 | tf_op jit(solution)/shard_map/ppermute | solution.py:452
  324.8 26.1 %collective-permute-start.12 = (bf16[7,3,48,256]{3,2,1,0:T(8,128)(2,1)S(1)}, bf16[7,3,48,256]{3,2,1,0:T(8,128)(2,1)}, u32[]{:S(2)}, u32[]{:S(2)}) collective-permute-start(bf16[7,3,48,256]{3,2,1,0:T(8,128)(2,1)S(1)} %collective-permute-done.11.refs_1_), channel_id=1, source_target_pairs={{0,7},{1,0},{2,1},{3,2},{4,3},{5,4},{6,5},{7,6},{8,15},{9,8},{10,9... | collective-permute-start | bytes 1548296 | tf_op jit(solution)/shard_map/ppermute | solution.py:449
  326.7 26.1 %collective-permute-start.5 = (bf16[7,3,48,256]{3,2,1,0:T(8,128)(2,1)S(1)}, bf16[7,3,48,256]{3,2,1,0:T(8,128)(2,1)}, u32[]{:S(2)}, u32[]{:S(2)}) collective-permute-start(bf16[7,3,48,256]{3,2,1,0:T(8,128)(2,1)S(1)} %collective-permute-done.4.refs_0_), channel_id=1, source_target_pairs={{0,1},{1,2},{2,3},{3,4},{4,5},{5,6},{6,7},{7,0},{8,9},{9,10},{10,1... | collective-permute-start | bytes 1548296 | tf_op jit(solution)/shard_map/ppermute | solution.py:449
  347.4 22.7 %collective-permute-start.19 = (bf16[7,3,48,256]{3,2,1,0:T(8,128)(2,1)}, bf16[7,3,48,256]{3,2,1,0:T(8,128)(2,1)}, u32[]{:S(2)}, u32[]{:S(2)}) collective-permute-start(bf16[7,3,48,256]{3,2,1,0:T(8,128)(2,1)} %collective-permute-done.18.refs_2_), channel_id=1, source_target_pairs={{0,1},{1,2},{2,3},{3,4},{4,5},{5,6},{6,7},{7,0},{8,9},{9,10},{10,1... | collective-permute-start | bytes 1548296 | tf_op jit(solution)/shard_map/ppermute | solution.py:452
  347.6 22.5 %collective-permute-start.25 = (bf16[7,3,48,256]{3,2,1,0:T(8,128)(2,1)}, bf16[7,3,48,256]{3,2,1,0:T(8,128)(2,1)S(1)}, u32[]{:S(2)}, u32[]{:S(2)}) collective-permute-start(bf16[7,3,48,256]{3,2,1,0:T(8,128)(2,1)} %collective-permute-done.24.refs_3_), channel_id=1, source_target_pairs={{0,7},{1,0},{2,1},{3,2},{4,3},{5,4},{6,5},{7,6},{8,15},{9,8},{10,9... | collective-permute-start | bytes 1548296 | tf_op jit(solution)/shard_map/ppermute | solution.py:452
  350.9 26.9 %collective-permute-start.13 = (bf16[7,3,48,256]{3,2,1,0:T(8,128)(2,1)}, bf16[7,3,48,256]{3,2,1,0:T(8,128)(2,1)S(1)}, u32[]{:S(2)}, u32[]{:S(2)}) collective-permute-start(bf16[7,3,48,256]{3,2,1,0:T(8,128)(2,1)} %collective-permute-done.12.refs_1_), channel_id=1, source_target_pairs={{0,7},{1,0},{2,1},{3,2},{4,3},{5,4},{6,5},{7,6},{8,15},{9,8},{10,9... | collective-permute-start | bytes 1548296 | tf_op jit(solution)/shard_map/ppermute | solution.py:449
  352.8 25.0 %collective-permute-start.6 = (bf16[7,3,48,256]{3,2,1,0:T(8,128)(2,1)}, bf16[7,3,48,256]{3,2,1,0:T(8,128)(2,1)S(1)}, u32[]{:S(2)}, u32[]{:S(2)}) collective-permute-start(bf16[7,3,48,256]{3,2,1,0:T(8,128)(2,1)} %collective-permute-done.5.refs_0_), channel_id=1, source_target_pairs={{0,1},{1,2},{2,3},{3,4},{4,5},{5,6},{6,7},{7,0},{8,9},{9,10},{10,1... | collective-permute-start | bytes 1548296 | tf_op jit(solution)/shard_map/ppermute | solution.py:449
  (13 other events, 296.6 us)

commit v6 on v5

--- a/solution.py
+++ b/solution.py
@@ -342,11 +342,14 @@
     return (w - 0.02 * step).astype(bf16), m, v
 
 
-def adam_kernel(layers, idx_ref, fac_ref, *refs):
-    k = len(layers)
-    pays, ins, outs = refs[:k], refs[k : k + 9], refs[-17:-8]
-    gbuf, wbuf, wdown, fbuf, fdown, gsem, isem, osem = refs[-8:]
-    factor = fac_ref[0:1, 0:1]
+def adam_kernel(n, where, fac_hbm, *refs):
+    k = len(where)
+    pays, ins, outs = refs[:k], refs[k : k + 9], refs[-19:-10]
+    fac, gbuf, wbuf, wdown, fbuf, fdown, fsem, gsem, isem, osem = refs[-10:]
+    me = lax.axis_index("dp")
+    layers = [layer for layer, _, _ in where]
+    chunks = [2 * lax.rem(me + (n - hops if d == 0 else hops), n) + d for _, d, hops in where]
+    fac_load = pltpu.make_async_copy(fac_hbm, fac, fsem)
 
     def place(i, a):
         which, kind = a // 3, a % 3
@@ -355,7 +358,7 @@
         return fdown.at[i, which - 1] if kind == 2 else fbuf.at[i, which - 1, kind]
 
     def rows(arrays, i, a):
-        return arrays[a].at[layers[i], :, idx_ref[i]] if a % 3 == 2 else arrays[a].at[layers[i], idx_ref[i]]
+        return arrays[a].at[layers[i], :, chunks[i]] if a % 3 == 2 else arrays[a].at[layers[i], chunks[i]]
 
     loads = [[pltpu.make_async_copy(rows(ins, i, a), place(i, a), isem.at[i, a]) for a in range(9)] for i in range(k)]
     pay_loads = [pltpu.make_async_copy(pays[i], gbuf.at[i], gsem.at[i]) for i in range(k)]
@@ -365,7 +368,11 @@
         for kind in range(3):
             for a in range(kind, 9, 3):
                 loads[i][a].start()
+        if i == 0:
+            fac_load.start()
     hr = wdown.shape[2]
+    fac_load.wait()
+    factor = fac[0:1, 0:1]
     for i in range(k):
         pay_loads[i].wait()
         def step(w, m, v, at, g):
@@ -392,30 +399,27 @@
             c.wait()
 
 
-def adam_call(factor, pieces, ins, prev):
+def adam_call(n, factor, pieces, ins, prev):
     k = len(pieces)
-    layers = tuple(l for l, _, _ in pieces)
-    idx = jnp.stack([c for _, c, _ in pieces]).astype(jnp.int32)
-    pays = [g for _, _, g in pieces]
-    hbm = pl.BlockSpec(memory_space=pl.ANY)
+    pays = [g for _, g in pieces]
+    hbm = pl.BlockSpec(memory_space=pltpu.HBM)
     kept = [] if prev is None else list(prev)
     size = k * pays[0].size
     rows, down = ins[0].shape[2:], (ins[2].shape[1],) + ins[2].shape[3:]
     return pl.pallas_call(
-        functools.partial(adam_kernel, layers),
-        grid_spec=pltpu.PrefetchScalarGridSpec(
-            num_scalar_prefetch=1, grid=(1,),
-            in_specs=[pl.BlockSpec((8, 128), lambda i, idx: (0, 0))] + [hbm] * (k + 9 + len(kept)),
-            out_specs=[hbm] * 9,
-            scratch_shapes=[
-                pltpu.VMEM((k,) + pays[0].shape, bf16), pltpu.VMEM((k, 2) + rows, bf16), pltpu.VMEM((k,) + down, bf16),
-                pltpu.VMEM((k, 2, 2) + rows, f32), pltpu.VMEM((k, 2) + down, f32),
-                pltpu.SemaphoreType.DMA((k,)), pltpu.SemaphoreType.DMA((k, 9)), pltpu.SemaphoreType.DMA((k, 9))]),
+        functools.partial(adam_kernel, n, tuple(w for w, _ in pieces)),
+        in_specs=[hbm] * (1 + k + 9 + len(kept)),
+        out_specs=[hbm] * 9,
+        scratch_shapes=[
+            pltpu.VMEM(factor.shape, f32),
+            pltpu.VMEM((k,) + pays[0].shape, bf16), pltpu.VMEM((k, 2) + rows, bf16), pltpu.VMEM((k,) + down, bf16),
+            pltpu.VMEM((k, 2, 2) + rows, f32), pltpu.VMEM((k, 2) + down, f32),
+            pltpu.SemaphoreType.DMA, pltpu.SemaphoreType.DMA((k,)), pltpu.SemaphoreType.DMA((k, 9)), pltpu.SemaphoreType.DMA((k, 9))],
         out_shape=[jax.ShapeDtypeStruct(x.shape, x.dtype) for x in ins],
-        input_output_aliases={} if prev is None else {2 + k + 9 + i: i for i in range(9)},
+        input_output_aliases={} if prev is None else {1 + k + 9 + i: i for i in range(9)},
         compiler_params=pltpu.CompilerParams(vmem_limit_bytes=62 * 2**20),
         cost_estimate=pl.CostEstimate(flops=10**9 * k, bytes_accessed=22 * size, transcendentals=size),
-        name="adamw")(idx, factor, *pays, *ins, *kept)
+        name="adamw")(factor, *pays, *ins, *kept)
 
 
 def views(arrays, n):
@@ -431,14 +435,13 @@
     to = ([(i, (i + 1) % n) for i in range(n)], [(i, (i - 1) % n) for i in range(n)])
 
     def step(x, dy, *arrays):
-        me = lax.axis_index("dp")
         *sums, factor = k1(x[0], dy[0], *arrays[:3], n)
         _, _, F = arrays[0].shape
         ins = views(arrays, n)
         last, first, came = ([o.reshape(F // BW, 3, o.shape[1] // 3, BW) for o in sums[i : i + 2]] for i in (0, 2, 4))
 
         def pieces(layer, pays, hops):
-            return [(layer, 2 * lax.rem(me - hops + n, n), pays[0]), (layer, 2 * lax.rem(me + hops, n) + 1, pays[1])]
+            return [((layer, d, hops), pays[d]) for d in range(2)]
 
         waiting = pieces(1, last, 0) + pieces(0, first, 0) + pieces(1, came, 1)
         outs, last = None, came
@@ -451,10 +454,10 @@
                 for d in range(2):
                     ahead.append(lax.ppermute(last[d], "dp", to[d]))
             for part in [waiting] if s < n - 1 else [waiting[:2], waiting[2:]]:
-                outs = adam_call(factor, part, ins, outs)
+                outs = adam_call(n, factor, part, ins, outs)
             waiting = pieces(0, first, s) + (pieces(1, ahead, s + 1) if ahead else [])
             last = ahead
-        outs = adam_call(factor, waiting, ins, outs)
+        outs = adam_call(n, factor, waiting, ins, outs)
         return tuple(o.reshape(w.shape) for o, w in zip(outs, arrays))
 
     step = jax.shard_map(

time: 386 us -> 375 us (0.972)
  the two profiles are of different devices: /device:TPU:22 before, /device:TPU:21 now
where the time goes in v6:
time: 375 us; the launch traced here: 368 us
  Pallas kernels  290 us (77%)
  waiting for transfers between devices  42.7 us (11%)
  starting transfers between devices  33.5 us (9%)
    pallas_call x1, Pallas kernels, k1(): pl.pallas_call(functools.partial(kernel, cfg), out_shape=(jax.ShapeDtypeS...  213 us
    pallas_call x9, Pallas kernels, adam_call(): pl.pallas_call(functools.partial(adam_kernel, n, tuple((w for w, _ in pie...  76.5 us
    ppermute x12, waiting for transfers between devices, step(): ahead.append(lax.ppermute(last[d], 'dp', to[d]))  21.6 us
    ppermute x14, waiting for transfers between devices, step(): first[d] = lax.ppermute(first[d], 'dp', to[d])  21.2 us
    ppermute x14, starting transfers between devices, step(): first[d] = lax.ppermute(first[d], 'dp', to[d])  17 us
    ppermute x12, starting transfers between devices, step(): ahead.append(lax.ppermute(last[d], 'dp', to[d]))  16.6 us
  transfers between devices with their start and end apart: 26, of which 6 were waited for; matrix products, arithmetic and copies ran while one was open for 0% of the time, Pallas kernels for 19%

profile of v6, /device:TPU:21, one launch (start us, length us, event | category | flops | bytes accessed | tf_op | source)
XLA Modules:
  0.0 368.3 jit_solution(4083063100581521967)
XLA Ops:
  0.6 213.4 %grads.1 = (bf16[7,144,256]{2,1,0:T(8,128)(2,1)}, bf16[7,144,256]{2,1,0:T(8,128)(2,1)}, bf16[7,144,256]{2,1,0:T(8,128)(2,1)}, bf16[7,144,256]{2,1,0:T(8,128)(2,1...) custom-call(bf16[2048,768]{1,0:T(8,128)(2,1)} %bitcast.126, ...), custom_call_target="tpu_custom_call" | custom-call | flops 101468602368 | bytes 40000000 | tf_op jit(solution)/shard_map/grads/pallas_call | solution.py:317
  218.5 7.0 %collective-permute-done.7.refs_1_ = bf16[7,3,48,256]{3,2,1,0:T(8,128)(2,1)S(1)} collective-permute-done((bf16[7,3,48,256]{3,2,1,0:T(8,128)(2,1)}, bf16[7,3,48,256]{3,2,1,0:T(8,128)(2,1)S(1)}, u32[]{:S(2)}, u32[]{:S(2)}) %collective-permute-start.7) | collective-permute-done | bytes 516128 | tf_op jit(solution)/shard_map/ppermute | solution.py:452
  225.4 3.1 collective-permute-start.8
  228.6 10.8 %collective-permute-done.14.refs_2_ = bf16[7,3,48,256]{3,2,1,0:T(8,128)(2,1)S(1)} collective-permute-done((bf16[7,3,48,256]{3,2,1,0:T(8,128)(2,1)}, bf16[7,3,48,256]{3,2,1,0:T(8,128)(2,1)S(1)}, u32[]{:S(2)}, u32[]{:S(2)}) %collective-permute-start.14) | collective-permute-done | bytes 516128 | tf_op jit(solution)/shard_map/ppermute | solution.py:455
  239.3 2.7 collective-permute-start.21
  242.0 5.5 %collective-permute-done.8.refs_1_ = bf16[7,3,48,256]{3,2,1,0:T(8,128)(2,1)S(1)} collective-permute-done((bf16[7,3,48,256]{3,2,1,0:T(8,128)(2,1)S(1)}, bf16[7,3,48,256]{3,2,1,0:T(8,128)(2,1)S(1)}, u32[]{:S(2)}, u32[]{:S(2)}) %collective-permute-start.8) | collective-permute-done | bytes 516128 | tf_op jit(solution)/shard_map/ppermute | solution.py:452
  247.6 3.1 collective-permute-start.9
  250.7 10.8 %collective-permute-done.15.refs_2_ = bf16[7,3,48,256]{3,2,1,0:T(8,128)(2,1)S(1)} collective-permute-done((bf16[7,3,48,256]{3,2,1,0:T(8,128)(2,1)S(1)}, bf16[7,3,48,256]{3,2,1,0:T(8,128)(2,1)S(1)}, u32[]{:S(2)}, u32[]{:S(2)}) %collective-permute-start.15) | collective-permute-done | bytes 516128 | tf_op jit(solution)/shard_map/ppermute | solution.py:455
  261.5 2.7 collective-permute-start.22
  264.1 5.7 %collective-permute-done.9.refs_1_ = bf16[7,3,48,256]{3,2,1,0:T(8,128)(2,1)S(1)} collective-permute-done((bf16[7,3,48,256]{3,2,1,0:T(8,128)(2,1)S(1)}, bf16[7,3,48,256]{3,2,1,0:T(8,128)(2,1)S(1)}, u32[]{:S(2)}, u32[]{:S(2)}) %collective-permute-start.9) | collective-permute-done | bytes 516128 | tf_op jit(solution)/shard_map/ppermute | solution.py:452
  269.8 3.0 collective-permute-start.10
  273.0 13.1 %adamw.9 = (bf16[2,16,48,1792]{3,2,1,0:T(8,128)(2,1)}, bf16[2,16,48,1792]{3,2,1,0:T(8,128)(2,1)}, bf16[2,7,16,16,768]{4,3,2,1,0:T(8,128)(2,1)}, f32[2,16,48,1792...) custom-call(f32[8,128]{1,0:T(8,128)} %get-tuple-element.97.fac_hbm, ...), custom_call_target="tpu_custom_call" | custom-call | flops 6000000000 | bytes 34062336 | tf_op jit(solution)/shard_map/adamw/pallas_call | solution.py:409
  286.3 2.7 collective-permute-start.23
  288.9 3.0 collective-permute-done.10.refs_1_
  291.9 3.0 collective-permute-start.11
  294.9 9.3 %adamw.10 = (bf16[2,16,48,1792]{3,2,1,0:T(8,128)(2,1)}, bf16[2,16,48,1792]{3,2,1,0:T(8,128)(2,1)}, bf16[2,7,16,16,768]{4,3,2,1,0:T(8,128)(2,1)}, f32[2,16,48,179...) custom-call(f32[8,128]{1,0:T(8,128)} %get-tuple-element.97.fac_hbm, ...), custom_call_target="tpu_custom_call", output_to_operand_aliasing={{0}: (14, {}), {1}: (15, {}), {2}: (16, {}), {3}: (17, {}),... | custom-call | flops 4000000000 | bytes 22708224 | tf_op jit(solution)/shard_map/adamw/pallas_call | solution.py:409
  304.2 9.3 %adamw.11 = (bf16[2,16,48,1792]{3,2,1,0:T(8,128)(2,1)}, bf16[2,16,48,1792]{3,2,1,0:T(8,128)(2,1)}, bf16[2,7,16,16,768]{4,3,2,1,0:T(8,128)(2,1)}, f32[2,16,48,179...) custom-call(f32[8,128]{1,0:T(8,128)} %get-tuple-element.97.fac_hbm, ...), custom_call_target="tpu_custom_call", output_to_operand_aliasing={{0}: (14, {}), {1}: (15, {}), {2}: (16, {}), {3}: (17, {}),... | custom-call | flops 4000000000 | bytes 22708224 | tf_op jit(solution)/shard_map/adamw/pallas_call | solution.py:409
  313.7 2.8 collective-permute-start.24
  318.0 9.3 %adamw.12 = (bf16[2,16,48,1792]{3,2,1,0:T(8,128)(2,1)}, bf16[2,16,48,1792]{3,2,1,0:T(8,128)(2,1)}, bf16[2,7,16,16,768]{4,3,2,1,0:T(8,128)(2,1)}, f32[2,16,48,179...) custom-call(f32[8,128]{1,0:T(8,128)} %get-tuple-element.97.fac_hbm, ...), custom_call_target="tpu_custom_call", output_to_operand_aliasing={{0}: (14, {}), {1}: (15, {}), {2}: (16, {}), {3}: (17, {}),... | custom-call | flops 4000000000 | bytes 22708224 | tf_op jit(solution)/shard_map/adamw/pallas_call | solution.py:409
  327.3 9.3 %adamw.13 = (bf16[2,16,48,1792]{3,2,1,0:T(8,128)(2,1)}, bf16[2,16,48,1792]{3,2,1,0:T(8,128)(2,1)}, bf16[2,7,16,16,768]{4,3,2,1,0:T(8,128)(2,1)}, f32[2,16,48,179...) custom-call(f32[8,128]{1,0:T(8,128)} %get-tuple-element.97.fac_hbm, ...), custom_call_target="tpu_custom_call", output_to_operand_aliasing={{0}: (14, {}), {1}: (15, {}), {2}: (16, {}), {3}: (17, {}),... | custom-call | flops 4000000000 | bytes 22708224 | tf_op jit(solution)/shard_map/adamw/pallas_call | solution.py:409
  340.8 9.2 %adamw.14 = (bf16[2,16,48,1792]{3,2,1,0:T(8,128)(2,1)}, bf16[2,16,48,1792]{3,2,1,0:T(8,128)(2,1)}, bf16[2,7,16,16,768]{4,3,2,1,0:T(8,128)(2,1)}, f32[2,16,48,179...) custom-call(f32[8,128]{1,0:T(8,128)} %get-tuple-element.97.fac_hbm, ...), custom_call_target="tpu_custom_call", output_to_operand_aliasing={{0}: (14, {}), {1}: (15, {}), {2}: (16, {}), {3}: (17, {}),... | custom-call | flops 4000000000 | bytes 22708224 | tf_op jit(solution)/shard_map/adamw/pallas_call | solution.py:409
  350.1 5.7 %adamw.15 = (bf16[2,16,48,1792]{3,2,1,0:T(8,128)(2,1)}, bf16[2,16,48,1792]{3,2,1,0:T(8,128)(2,1)}, bf16[2,7,16,16,768]{4,3,2,1,0:T(8,128)(2,1)}, f32[2,16,48,179...) custom-call(f32[8,128]{1,0:T(8,128)} %get-tuple-element.97.fac_hbm, ...), custom_call_target="tpu_custom_call", output_to_operand_aliasing={{0}: (12, {}), {1}: (13, {}), {2}: (14, {}), {3}: (15, {}),... | custom-call | flops 2000000000 | bytes 11354112 | tf_op jit(solution)/shard_map/adamw/pallas_call | solution.py:409
  355.8 5.7 %adamw.16 = (bf16[2,16,48,1792]{3,2,1,0:T(8,128)(2,1)}, bf16[2,16,48,1792]{3,2,1,0:T(8,128)(2,1)}, bf16[2,7,16,16,768]{4,3,2,1,0:T(8,128)(2,1)}, f32[2,16,48,179...) custom-call(f32[8,128]{1,0:T(8,128)} %get-tuple-element.97.fac_hbm, ...), custom_call_target="tpu_custom_call", output_to_operand_aliasing={{0}: (12, {}), {1}: (13, {}), {2}: (14, {}), {3}: (15, {}),... | custom-call | flops 2000000000 | bytes 11354112 | tf_op jit(solution)/shard_map/adamw/pallas_call | solution.py:409
  362.5 5.6 %adamw.17 = (bf16[2,16,48,1792]{3,2,1,0:T(8,128)(2,1)}, bf16[2,16,48,1792]{3,2,1,0:T(8,128)(2,1)}, bf16[2,7,16,16,768]{4,3,2,1,0:T(8,128)(2,1)}, f32[2,16,48,179...) custom-call(f32[8,128]{1,0:T(8,128)} %get-tuple-element.97.fac_hbm, ...), custom_call_target="tpu_custom_call", output_to_operand_aliasing={{0}: (12, {}), {1}: (13, {}), {2}: (14, {}), {3}: (15, {}),... | custom-call | flops 2000000000 | bytes 11354112 | tf_op jit(solution)/shard_map/adamw/pallas_call | solution.py:409
  (66 shorter events, 11.5 us)
Async XLA Ops:
  215.8 23.5 %collective-permute-start.14 = (bf16[7,3,48,256]{3,2,1,0:T(8,128)(2,1)}, bf16[7,3,48,256]{3,2,1,0:T(8,128)(2,1)S(1)}, u32[]{:S(2)}, u32[]{:S(2)}) collective-permute-start(bf16[7,3,48,256]{3,2,1,0:T(8,128)(2,1)} %bitcast.122), channel_id=1, source_target_pairs={{0,1},{1,2},{2,3},{3,4},{4,5},{5,6},{6,7},{7,0},{8,9},{9,10},{10,1... | collective-permute-start | bytes 1548296 | tf_op jit(solution)/shard_map/ppermute | solution.py:455
  216.1 23.3 %collective-permute-start.20 = (bf16[7,3,48,256]{3,2,1,0:T(8,128)(2,1)}, bf16[7,3,48,256]{3,2,1,0:T(8,128)(2,1)S(1)}, u32[]{:S(2)}, u32[]{:S(2)}) collective-permute-start(bf16[7,3,48,256]{3,2,1,0:T(8,128)(2,1)} %bitcast.124), channel_id=1, source_target_pairs={{0,7},{1,0},{2,1},{3,2},{4,3},{5,4},{6,5},{7,6},{8,15},{9,8},{10,9... | collective-permute-start | bytes 1548296 | tf_op jit(solution)/shard_map/ppermute | solution.py:455
  225.4 22.1 %collective-permute-start.8 = (bf16[7,3,48,256]{3,2,1,0:T(8,128)(2,1)S(1)}, bf16[7,3,48,256]{3,2,1,0:T(8,128)(2,1)S(1)}, u32[]{:S(2)}, u32[]{:S(2)}) collective-permute-start(bf16[7,3,48,256]{3,2,1,0:T(8,128)(2,1)S(1)} %collective-permute-done.7.refs_1_), channel_id=1, source_target_pairs={{0,7},{1,0},{2,1},{3,2},{4,3},{5,4},{6,5},{7,6},{8,15},{9,8},{10,9... | collective-permute-start | bytes 1548296 | tf_op jit(solution)/shard_map/ppermute | solution.py:452
  228.5 22.1 %collective-permute-start.1 = (bf16[7,3,48,256]{3,2,1,0:T(8,128)(2,1)S(1)}, bf16[7,3,48,256]{3,2,1,0:T(8,128)(2,1)S(1)}, u32[]{:S(2)}, u32[]{:S(2)}) collective-permute-start(bf16[7,3,48,256]{3,2,1,0:T(8,128)(2,1)S(1)} %collective-permute-done.refs_0_), channel_id=1, source_target_pairs={{0,1},{1,2},{2,3},{3,4},{4,5},{5,6},{6,7},{7,0},{8,9},{9,10},{10,1... | collective-permute-start | bytes 1548296 | tf_op jit(solution)/shard_map/ppermute | solution.py:452
  239.3 22.1 %collective-permute-start.15 = (bf16[7,3,48,256]{3,2,1,0:T(8,128)(2,1)S(1)}, bf16[7,3,48,256]{3,2,1,0:T(8,128)(2,1)S(1)}, u32[]{:S(2)}, u32[]{:S(2)}) collective-permute-start(bf16[7,3,48,256]{3,2,1,0:T(8,128)(2,1)S(1)} %collective-permute-done.14.refs_2_), channel_id=1, source_target_pairs={{0,1},{1,2},{2,3},{3,4},{4,5},{5,6},{6,7},{7,0},{8,9},{9,10},{10,1... | collective-permute-start | bytes 1548296 | tf_op jit(solution)/shard_map/ppermute | solution.py:455
  239.3 22.1 %collective-permute-start.21 = (bf16[7,3,48,256]{3,2,1,0:T(8,128)(2,1)S(1)}, bf16[7,3,48,256]{3,2,1,0:T(8,128)(2,1)}, u32[]{:S(2)}, u32[]{:S(2)}) collective-permute-start(bf16[7,3,48,256]{3,2,1,0:T(8,128)(2,1)S(1)} %collective-permute-done.20.refs_3_), channel_id=1, source_target_pairs={{0,7},{1,0},{2,1},{3,2},{4,3},{5,4},{6,5},{7,6},{8,15},{9,8},{10,9... | collective-permute-start | bytes 1548296 | tf_op jit(solution)/shard_map/ppermute | solution.py:455
  247.6 22.2 %collective-permute-start.9 = (bf16[7,3,48,256]{3,2,1,0:T(8,128)(2,1)S(1)}, bf16[7,3,48,256]{3,2,1,0:T(8,128)(2,1)S(1)}, u32[]{:S(2)}, u32[]{:S(2)}) collective-permute-start(bf16[7,3,48,256]{3,2,1,0:T(8,128)(2,1)S(1)} %collective-permute-done.8.refs_1_), channel_id=1, source_target_pairs={{0,7},{1,0},{2,1},{3,2},{4,3},{5,4},{6,5},{7,6},{8,15},{9,8},{10,9... | collective-permute-start | bytes 1548296 | tf_op jit(solution)/shard_map/ppermute | solution.py:452
  250.7 22.1 %collective-permute-start.2 = (bf16[7,3,48,256]{3,2,1,0:T(8,128)(2,1)S(1)}, bf16[7,3,48,256]{3,2,1,0:T(8,128)(2,1)}, u32[]{:S(2)}, u32[]{:S(2)}) collective-permute-start(bf16[7,3,48,256]{3,2,1,0:T(8,128)(2,1)S(1)} %collective-permute-done.1.refs_0_), channel_id=1, source_target_pairs={{0,1},{1,2},{2,3},{3,4},{4,5},{5,6},{6,7},{7,0},{8,9},{9,10},{10,1... | collective-permute-start | bytes 1548296 | tf_op jit(solution)/shard_map/ppermute | solution.py:452
  261.4 24.7 %collective-permute-start.16 = (bf16[7,3,48,256]{3,2,1,0:T(8,128)(2,1)S(1)}, bf16[7,3,48,256]{3,2,1,0:T(8,128)(2,1)}, u32[]{:S(2)}, u32[]{:S(2)}) collective-permute-start(bf16[7,3,48,256]{3,2,1,0:T(8,128)(2,1)S(1)} %collective-permute-done.15.refs_2_), channel_id=1, source_target_pairs={{0,1},{1,2},{2,3},{3,4},{4,5},{5,6},{6,7},{7,0},{8,9},{9,10},{10,1... | collective-permute-start | bytes 1548296 | tf_op jit(solution)/shard_map/ppermute | solution.py:455
  261.5 24.8 %collective-permute-start.22 = (bf16[7,3,48,256]{3,2,1,0:T(8,128)(2,1)}, bf16[7,3,48,256]{3,2,1,0:T(8,128)(2,1)}, u32[]{:S(2)}, u32[]{:S(2)}) collective-permute-start(bf16[7,3,48,256]{3,2,1,0:T(8,128)(2,1)} %collective-permute-done.21.refs_3_), channel_id=1, source_target_pairs={{0,7},{1,0},{2,1},{3,2},{4,3},{5,4},{6,5},{7,6},{8,15},{9,8},{10,9... | collective-permute-start | bytes 1548296 | tf_op jit(solution)/shard_map/ppermute | solution.py:455
  269.8 22.1 %collective-permute-start.10 = (bf16[7,3,48,256]{3,2,1,0:T(8,128)(2,1)S(1)}, bf16[7,3,48,256]{3,2,1,0:T(8,128)(2,1)S(1)}, u32[]{:S(2)}, u32[]{:S(2)}) collective-permute-start(bf16[7,3,48,256]{3,2,1,0:T(8,128)(2,1)S(1)} %collective-permute-done.9.refs_1_), channel_id=1, source_target_pairs={{0,7},{1,0},{2,1},{3,2},{4,3},{5,4},{6,5},{7,6},{8,15},{9,8},{10,9... | collective-permute-start | bytes 1548296 | tf_op jit(solution)/shard_map/ppermute | solution.py:452
  272.8 22.1 %collective-permute-start.3 = (bf16[7,3,48,256]{3,2,1,0:T(8,128)(2,1)}, bf16[7,3,48,256]{3,2,1,0:T(8,128)(2,1)}, u32[]{:S(2)}, u32[]{:S(2)}) collective-permute-start(bf16[7,3,48,256]{3,2,1,0:T(8,128)(2,1)} %collective-permute-done.2.refs_0_), channel_id=1, source_target_pairs={{0,1},{1,2},{2,3},{3,4},{4,5},{5,6},{6,7},{7,0},{8,9},{9,10},{10,1... | collective-permute-start | bytes 1548296 | tf_op jit(solution)/shard_map/ppermute | solution.py:452
  286.1 27.4 %collective-permute-start.17 = (bf16[7,3,48,256]{3,2,1,0:T(8,128)(2,1)}, bf16[7,3,48,256]{3,2,1,0:T(8,128)(2,1)}, u32[]{:S(2)}, u32[]{:S(2)}) collective-permute-start(bf16[7,3,48,256]{3,2,1,0:T(8,128)(2,1)} %collective-permute-done.16.refs_2_), channel_id=1, source_target_pairs={{0,1},{1,2},{2,3},{3,4},{4,5},{5,6},{6,7},{7,0},{8,9},{9,10},{10,1... | collective-permute-start | bytes 1548296 | tf_op jit(solution)/shard_map/ppermute | solution.py:455
  286.3 27.4 %collective-permute-start.23 = (bf16[7,3,48,256]{3,2,1,0:T(8,128)(2,1)}, bf16[7,3,48,256]{3,2,1,0:T(8,128)(2,1)}, u32[]{:S(2)}, u32[]{:S(2)}) collective-permute-start(bf16[7,3,48,256]{3,2,1,0:T(8,128)(2,1)} %collective-permute-done.22.refs_3_), channel_id=1, source_target_pairs={{0,7},{1,0},{2,1},{3,2},{4,3},{5,4},{6,5},{7,6},{8,15},{9,8},{10,9... | collective-permute-start | bytes 1548296 | tf_op jit(solution)/shard_map/ppermute | solution.py:455
  291.9 24.6 %collective-permute-start.11 = (bf16[7,3,48,256]{3,2,1,0:T(8,128)(2,1)S(1)}, bf16[7,3,48,256]{3,2,1,0:T(8,128)(2,1)S(1)}, u32[]{:S(2)}, u32[]{:S(2)}) collective-permute-start(bf16[7,3,48,256]{3,2,1,0:T(8,128)(2,1)S(1)} %collective-permute-done.10.refs_1_), channel_id=1, source_target_pairs={{0,7},{1,0},{2,1},{3,2},{4,3},{5,4},{6,5},{7,6},{8,15},{9,8},{10,9... | collective-permute-start | bytes 1548296 | tf_op jit(solution)/shard_map/ppermute | solution.py:452
  294.9 22.9 %collective-permute-start.4 = (bf16[7,3,48,256]{3,2,1,0:T(8,128)(2,1)}, bf16[7,3,48,256]{3,2,1,0:T(8,128)(2,1)S(1)}, u32[]{:S(2)}, u32[]{:S(2)}) collective-permute-start(bf16[7,3,48,256]{3,2,1,0:T(8,128)(2,1)} %collective-permute-done.3.refs_0_), channel_id=1, source_target_pairs={{0,1},{1,2},{2,3},{3,4},{4,5},{5,6},{6,7},{7,0},{8,9},{9,10},{10,1... | collective-permute-start | bytes 1548296 | tf_op jit(solution)/shard_map/ppermute | solution.py:452
  313.5 23.1 %collective-permute-start.18 = (bf16[7,3,48,256]{3,2,1,0:T(8,128)(2,1)}, bf16[7,3,48,256]{3,2,1,0:T(8,128)(2,1)}, u32[]{:S(2)}, u32[]{:S(2)}) collective-permute-start(bf16[7,3,48,256]{3,2,1,0:T(8,128)(2,1)} %collective-permute-done.17.refs_2_), channel_id=1, source_target_pairs={{0,1},{1,2},{2,3},{3,4},{4,5},{5,6},{6,7},{7,0},{8,9},{9,10},{10,1... | collective-permute-start | bytes 1548296 | tf_op jit(solution)/shard_map/ppermute | solution.py:455
  313.7 23.2 %collective-permute-start.24 = (bf16[7,3,48,256]{3,2,1,0:T(8,128)(2,1)}, bf16[7,3,48,256]{3,2,1,0:T(8,128)(2,1)}, u32[]{:S(2)}, u32[]{:S(2)}) collective-permute-start(bf16[7,3,48,256]{3,2,1,0:T(8,128)(2,1)} %collective-permute-done.23.refs_3_), channel_id=1, source_target_pairs={{0,7},{1,0},{2,1},{3,2},{4,3},{5,4},{6,5},{7,6},{8,15},{9,8},{10,9... | collective-permute-start | bytes 1548296 | tf_op jit(solution)/shard_map/ppermute | solution.py:455
  316.5 22.9 %collective-permute-start.12 = (bf16[7,3,48,256]{3,2,1,0:T(8,128)(2,1)S(1)}, bf16[7,3,48,256]{3,2,1,0:T(8,128)(2,1)S(1)}, u32[]{:S(2)}, u32[]{:S(2)}) collective-permute-start(bf16[7,3,48,256]{3,2,1,0:T(8,128)(2,1)S(1)} %collective-permute-done.11.refs_1_), channel_id=1, source_target_pairs={{0,7},{1,0},{2,1},{3,2},{4,3},{5,4},{6,5},{7,6},{8,15},{9,8},{10,9... | collective-permute-start | bytes 1548296 | tf_op jit(solution)/shard_map/ppermute | solution.py:452
  317.8 22.8 %collective-permute-start.5 = (bf16[7,3,48,256]{3,2,1,0:T(8,128)(2,1)S(1)}, bf16[7,3,48,256]{3,2,1,0:T(8,128)(2,1)}, u32[]{:S(2)}, u32[]{:S(2)}) collective-permute-start(bf16[7,3,48,256]{3,2,1,0:T(8,128)(2,1)S(1)} %collective-permute-done.4.refs_0_), channel_id=1, source_target_pairs={{0,1},{1,2},{2,3},{3,4},{4,5},{5,6},{6,7},{7,0},{8,9},{9,10},{10,1... | collective-permute-start | bytes 1548296 | tf_op jit(solution)/shard_map/ppermute | solution.py:452
  336.6 19.2 %collective-permute-start.19 = (bf16[7,3,48,256]{3,2,1,0:T(8,128)(2,1)}, bf16[7,3,48,256]{3,2,1,0:T(8,128)(2,1)}, u32[]{:S(2)}, u32[]{:S(2)}) collective-permute-start(bf16[7,3,48,256]{3,2,1,0:T(8,128)(2,1)} %collective-permute-done.18.refs_2_), channel_id=1, source_target_pairs={{0,1},{1,2},{2,3},{3,4},{4,5},{5,6},{6,7},{7,0},{8,9},{9,10},{10,1... | collective-permute-start | bytes 1548296 | tf_op jit(solution)/shard_map/ppermute | solution.py:455
  336.9 18.9 %collective-permute-start.25 = (bf16[7,3,48,256]{3,2,1,0:T(8,128)(2,1)}, bf16[7,3,48,256]{3,2,1,0:T(8,128)(2,1)}, u32[]{:S(2)}, u32[]{:S(2)}) collective-permute-start(bf16[7,3,48,256]{3,2,1,0:T(8,128)(2,1)} %collective-permute-done.24.refs_3_), channel_id=1, source_target_pairs={{0,7},{1,0},{2,1},{3,2},{4,3},{5,4},{6,5},{7,6},{8,15},{9,8},{10,9... | collective-permute-start | bytes 1548296 | tf_op jit(solution)/shard_map/ppermute | solution.py:455
  339.4 22.1 %collective-permute-start.13 = (bf16[7,3,48,256]{3,2,1,0:T(8,128)(2,1)S(1)}, bf16[7,3,48,256]{3,2,1,0:T(8,128)(2,1)S(1)}, u32[]{:S(2)}, u32[]{:S(2)}) collective-permute-start(bf16[7,3,48,256]{3,2,1,0:T(8,128)(2,1)S(1)} %collective-permute-done.12.refs_1_), channel_id=1, source_target_pairs={{0,7},{1,0},{2,1},{3,2},{4,3},{5,4},{6,5},{7,6},{8,15},{9,8},{10,9... | collective-permute-start | bytes 1548296 | tf_op jit(solution)/shard_map/ppermute | solution.py:452
  340.6 20.9 %collective-permute-start.6 = (bf16[7,3,48,256]{3,2,1,0:T(8,128)(2,1)}, bf16[7,3,48,256]{3,2,1,0:T(8,128)(2,1)S(1)}, u32[]{:S(2)}, u32[]{:S(2)}) collective-permute-start(bf16[7,3,48,256]{3,2,1,0:T(8,128)(2,1)} %collective-permute-done.5.refs_0_), channel_id=1, source_target_pairs={{0,1},{1,2},{2,3},{3,4},{4,5},{5,6},{6,7},{7,0},{8,9},{9,10},{10,1... | collective-permute-start | bytes 1548296 | tf_op jit(solution)/shard_map/ppermute | solution.py:452
  (16 other events, 313.4 us)
